TPU v7x, 32 devices: a whole 2x2x4 slice. The times are simulated.
32 devices in a mesh: fsdp: 8 (over z, x), tensor: 4 (over y, core).
Axes of the slice: x: 2, y: 2, z: 4, core: 2. Of those that a mesh axis runs over, the one named last changes fastest.
Arguments:
- tokens: bfloat16 [32, 512, 768], P('fsdp', 'tensor'), may hold values from -6 to 6
- lengths: int32 [32], P('fsdp'), may hold values from 128 to 512, as said below
- cotangent: bfloat16 [32, 512, 768], P('fsdp', 'tensor'), may hold values from -6 to 6
- w_query: bfloat16 [768, 768], P('fsdp', 'tensor'), may hold values from -0.21875 to 0.21875
- w_key: bfloat16 [768, 768], P('fsdp', 'tensor'), may hold values from -0.3125 to 0.3125
- w_value: bfloat16 [768, 768], P('fsdp', 'tensor'), may hold values from -0.21875 to 0.21875
- w_output: bfloat16 [768, 768], P('tensor', 'fsdp'), may hold values from -1 to 1
- w_inner: bfloat16 [768, 3072], P('fsdp', 'tensor'), may hold values from -0.21875 to 0.21875
- w_outer: bfloat16 [3072, 768], P('tensor', 'fsdp'), may hold values from -0.15625 to 0.15625
- b_query: float32 [768], P(('fsdp', 'tensor')), may hold values from -3 to 3
- b_value: float32 [768], P(('fsdp', 'tensor')), may hold values from -1.2 to 1.2
- b_output: float32 [768], P(('fsdp', 'tensor')), may hold values from -1.8 to 1.8
- b_inner: float32 [3072], P(('fsdp', 'tensor')), may hold values from -3 to 3
- b_outer: float32 [768], P(('fsdp', 'tensor')), may hold values from -1.8 to 1.8
- gain_first: float32 [768], P(('fsdp', 'tensor')), may hold values from 0.1 to 1.9
- shift_first: float32 [768], P(('fsdp', 'tensor')), may hold values from -1.8 to 1.8
- gain_second: float32 [768], P(('fsdp', 'tensor')), may hold values from 0.1 to 1.9
- shift_second: float32 [768], P(('fsdp', 'tensor')), may hold values from -1.8 to 1.8
Outputs:
- output: bfloat16 [32, 512, 768], P('fsdp', 'tensor')
- input_grad: float32 [32, 512, 768], P('fsdp', 'tensor')
- grad_w_query: float32 [768, 768], P('fsdp', 'tensor')
- grad_w_key: float32 [768, 768], P('fsdp', 'tensor')
- grad_w_value: float32 [768, 768], P('fsdp', 'tensor')
- grad_w_output: float32 [768, 768], P('tensor', 'fsdp')
- grad_w_inner: float32 [768, 3072], P('fsdp', 'tensor')
- grad_w_outer: float32 [3072, 768], P('tensor', 'fsdp')
- grad_b_query: float32 [768], P(('fsdp', 'tensor'))
- grad_b_value: float32 [768], P(('fsdp', 'tensor'))
- grad_b_output: float32 [768], P(('fsdp', 'tensor'))
- grad_b_inner: float32 [3072], P(('fsdp', 'tensor'))
- grad_b_outer: float32 [768], P(('fsdp', 'tensor'))
- grad_gain_first: float32 [768], P(('fsdp', 'tensor'))
- grad_shift_first: float32 [768], P(('fsdp', 'tensor'))
- grad_gain_second: float32 [768], P(('fsdp', 'tensor'))
- grad_shift_second: float32 [768], P(('fsdp', 'tensor'))
Inputs may be any that keep to these rules, and one draw needn't show every extreme that they name: Row s holds a sequence in its first lengths[s] slots; in every draw one row is full and one holds exactly 128 slots.
All inputs are finite; a program needn't handle non-finite values.
Results may differ from a plain program's by a relative error of at most 0.025.
Values may be sent and summed in bfloat16 or wider, within the bound.
A program may use at most 192 MiB of HBM per device.

v0:
```python
from functools import partial

import jax
import jax.numpy as jnp
from jax import lax
from jax.sharding import PartitionSpec as P

HEAD = 64


epsilon = 1e-05
root_half = 0.7071067811865476
inverse_root_two_pi = 0.3989422804014327


def gelu_value(inner):
    return 0.5 * inner * (1.0 + jax.scipy.special.erf(inner * root_half))


def gelu_slope(inner):
    return 0.5 * (
        1.0 + jax.scipy.special.erf(inner * root_half)
    ) + inner * inverse_root_two_pi * jnp.exp(-0.5 * inner * inner)


def normalize(rows):
    mean = jnp.mean(rows, axis=1, keepdims=True)
    centered = rows - mean
    variance = jnp.mean(centered * centered, axis=1, keepdims=True)
    factor = lax.rsqrt(variance + epsilon)
    return (centered * factor, factor)


def normalize_back(grad_normed, normed, factor):
    return factor * (
        grad_normed
        - jnp.mean(grad_normed, axis=1, keepdims=True)
        - normed * jnp.mean(grad_normed * normed, axis=1, keepdims=True)
    )


def column_sum(rows):
    return jnp.sum(rows.astype(jnp.float32), axis=0)


def dot_rows(left, right):
    return lax.dot_general(
        left, right, (((0,), (0,)), ((), ())), preferred_element_type=jnp.float32
    )


def dot_back(left, right):
    return lax.dot_general(
        left, right, (((1,), (1,)), ((), ())), preferred_element_type=jnp.float32
    )


def place(values, offset, total_length):
    return lax.dynamic_update_slice(jnp.zeros((total_length,), jnp.float32), values, (offset,))


def block_scores(keys, key_valid, query_block):
    raw = jnp.einsum(
        "qhd,khd->hqk", query_block, keys, preferred_element_type=jnp.float32
    ) * HEAD ** (-0.5)
    return jnp.where(key_valid[None, None, :], raw, -1000000000.0)


def attend_forward(keys, values, key_valid, query_block):
    masked = block_scores(keys, key_valid, query_block)
    top = jnp.max(masked, axis=2, keepdims=True)
    expo = jnp.exp(masked - top)
    total = jnp.sum(expo, axis=2, keepdims=True)
    probs = (expo / total).astype(jnp.bfloat16)
    context = jnp.einsum("hqk,khd->qhd", probs, values, preferred_element_type=jnp.float32)
    return (context, top, total)


def attend_backward(keys, values, key_valid, carry, item):
    key_grad, value_grad = carry
    query_block, context_grad_block, top, total = item
    masked = block_scores(keys, key_valid, query_block)
    probs = jnp.exp(masked - top) / total
    probs_low = probs.astype(jnp.bfloat16)
    prob_grad = jnp.einsum(
        "qhd,khd->hqk", context_grad_block, values, preferred_element_type=jnp.float32
    )
    delta = jnp.sum(prob_grad * probs, axis=2, keepdims=True)
    score_grad = (probs * (prob_grad - delta)).astype(jnp.bfloat16)
    factor = HEAD ** (-0.5)
    query_grad = (
        jnp.einsum("hqk,khd->qhd", score_grad, keys, preferred_element_type=jnp.float32) * factor
    )
    key_grad = (
        key_grad
        + jnp.einsum("hqk,qhd->khd", score_grad, query_block, preferred_element_type=jnp.float32)
        * factor
    )
    value_grad = value_grad + jnp.einsum(
        "hqk,qhd->khd", probs_low, context_grad_block, preferred_element_type=jnp.float32
    )
    return ((key_grad, value_grad), query_grad)


def gather_weights(w_query, w_key, w_value, w_output, w_inner, w_outer):
    return (
        lax.all_gather(w_query, "fsdp", axis=0, tiled=True),
        lax.all_gather(w_key, "fsdp", axis=0, tiled=True),
        lax.all_gather(w_value, "fsdp", axis=0, tiled=True),
        lax.all_gather(w_output, "fsdp", axis=1, tiled=True),
        lax.all_gather(w_inner, "fsdp", axis=0, tiled=True),
        lax.all_gather(w_outer, "fsdp", axis=1, tiled=True),
    )


def split_joint(joint_sum, output_sum, inner_sum, outer_sum, head_width):
    return (
        joint_sum[:, :head_width],
        joint_sum[:, head_width : 2 * head_width],
        joint_sum[:, 2 * head_width :],
        output_sum,
        inner_sum,
        outer_sum,
    )


def add_tuples(left, right):
    return tuple((first_item + second_item for first_item, second_item in zip(left, right)))


def local(
    tokens,
    lengths,
    cotangent,
    w_query,
    w_key,
    w_value,
    w_output,
    w_inner,
    w_outer,
    b_query,
    b_value,
    b_output,
    b_inner,
    b_outer,
    gain_first,
    shift_first,
    gain_second,
    shift_second,
):
    tensor_size = lax.axis_size("tensor")
    tensor_rank = lax.axis_index("tensor")
    micro_count = tokens.shape[0]
    part_rows = tokens.shape[1]
    width = tokens.shape[2]
    seq_rows = part_rows * tensor_size
    head_width = w_query.shape[1]
    inner_width = w_inner.shape[1]
    local_heads = head_width // HEAD
    block_rows = min(512, seq_rows)
    block_count = seq_rows // block_rows
    vector_full = (
        lax.all_gather(b_query, ("fsdp", "tensor"), axis=0, tiled=True),
        lax.all_gather(b_value, ("fsdp", "tensor"), axis=0, tiled=True),
        lax.all_gather(b_output, ("fsdp", "tensor"), axis=0, tiled=True),
        lax.all_gather(b_inner, ("fsdp", "tensor"), axis=0, tiled=True),
        lax.all_gather(b_outer, ("fsdp", "tensor"), axis=0, tiled=True),
        lax.all_gather(gain_first, ("fsdp", "tensor"), axis=0, tiled=True),
        lax.all_gather(shift_first, ("fsdp", "tensor"), axis=0, tiled=True),
        lax.all_gather(gain_second, ("fsdp", "tensor"), axis=0, tiled=True),
        lax.all_gather(shift_second, ("fsdp", "tensor"), axis=0, tiled=True),
    )
    query_bias = lax.dynamic_slice_in_dim(vector_full[0], tensor_rank * head_width, head_width)
    value_bias = lax.dynamic_slice_in_dim(vector_full[1], tensor_rank * head_width, head_width)
    inner_bias = lax.dynamic_slice_in_dim(vector_full[3], tensor_rank * inner_width, inner_width)
    joint_bias = jnp.concatenate([query_bias, jnp.zeros((head_width,), jnp.float32), value_bias])
    grad_query_bias = jnp.zeros((head_width,), jnp.float32)
    grad_value_bias = jnp.zeros((head_width,), jnp.float32)
    grad_inner_bias = jnp.zeros((inner_width,), jnp.float32)
    grad_output_bias = jnp.zeros((width,), jnp.float32)
    grad_outer_bias = jnp.zeros((width,), jnp.float32)
    grad_gain_one = jnp.zeros((width,), jnp.float32)
    grad_shift_one = jnp.zeros((width,), jnp.float32)
    grad_gain_two = jnp.zeros((width,), jnp.float32)
    grad_shift_two = jnp.zeros((width,), jnp.float32)
    local_totals = None
    shard_totals = None
    outputs = []
    input_grads = []
    slot_index = jnp.arange(seq_rows, dtype=jnp.int32)
    part_index = tensor_rank * part_rows + jnp.arange(part_rows, dtype=jnp.int32)
    for micro_index in range(micro_count):
        forward_weights = gather_weights(w_query, w_key, w_value, w_output, w_inner, w_outer)
        joint_w = jnp.concatenate(
            [forward_weights[0], forward_weights[1], forward_weights[2]], axis=1
        )
        output_w = forward_weights[3]
        inner_w = forward_weights[4]
        outer_w = forward_weights[5]
        length = lengths[micro_index]
        key_valid = slot_index < length
        row_valid = (part_index < length).astype(jnp.float32)[:, None]
        own_rows = tokens[micro_index]
        whole = lax.all_gather(own_rows, "tensor", axis=0, tiled=True)
        joint = (jnp.dot(whole, joint_w, preferred_element_type=jnp.float32) + joint_bias).astype(
            jnp.bfloat16
        )
        query = joint[:, :head_width].reshape(block_count, block_rows, local_heads, HEAD)
        keys = joint[:, head_width : 2 * head_width].reshape(seq_rows, local_heads, HEAD)
        values = joint[:, 2 * head_width :].reshape(seq_rows, local_heads, HEAD)
        context_blocks, tops, totals = lax.map(
            partial(attend_forward, keys, values, key_valid), query
        )
        context_low = context_blocks.reshape(seq_rows, head_width).astype(jnp.bfloat16)
        attended = (
            lax.psum_scatter(
                jnp.dot(context_low, output_w, preferred_element_type=jnp.float32).astype(
                    jnp.bfloat16
                ),
                "tensor",
                scatter_dimension=0,
                tiled=True,
            ).astype(jnp.float32)
            + vector_full[2]
        )
        normed_first, factor_first = normalize(own_rows.astype(jnp.float32) + attended)
        first = normed_first * vector_full[5] + vector_full[6]
        first_whole = lax.all_gather(first.astype(jnp.bfloat16), "tensor", axis=0, tiled=True)
        inner = jnp.dot(first_whole, inner_w, preferred_element_type=jnp.float32) + inner_bias
        active = gelu_value(inner).astype(jnp.bfloat16)
        mixed = (
            lax.psum_scatter(
                jnp.dot(active, outer_w, preferred_element_type=jnp.float32).astype(jnp.bfloat16),
                "tensor",
                scatter_dimension=0,
                tiled=True,
            ).astype(jnp.float32)
            + vector_full[4]
        )
        normed_second, factor_second = normalize(first + mixed)
        outputs.append(
            ((normed_second * vector_full[7] + vector_full[8]) * row_valid).astype(jnp.bfloat16)
        )
        backward_weights = gather_weights(w_query, w_key, w_value, w_output, w_inner, w_outer)
        joint_w = jnp.concatenate(
            [backward_weights[0], backward_weights[1], backward_weights[2]], axis=1
        )
        output_w = backward_weights[3]
        inner_w = backward_weights[4]
        outer_w = backward_weights[5]
        out_grad = cotangent[micro_index].astype(jnp.float32) * row_valid
        grad_gain_two = grad_gain_two + column_sum(out_grad * normed_second)
        grad_shift_two = grad_shift_two + column_sum(out_grad)
        sum_grad = normalize_back(out_grad * vector_full[7], normed_second, factor_second)
        mixed_grad = sum_grad.astype(jnp.bfloat16)
        grad_outer_bias = grad_outer_bias + column_sum(mixed_grad)
        mixed_whole = lax.all_gather(mixed_grad, "tensor", axis=0, tiled=True)
        outer_sum = dot_rows(active, mixed_whole)
        inner_grad = (dot_back(mixed_whole, outer_w) * gelu_slope(inner)).astype(jnp.bfloat16)
        grad_inner_bias = grad_inner_bias + column_sum(inner_grad)
        inner_sum = dot_rows(first_whole, inner_grad)
        first_grad = sum_grad + lax.psum_scatter(
            dot_back(inner_grad, inner_w).astype(jnp.bfloat16),
            "tensor",
            scatter_dimension=0,
            tiled=True,
        ).astype(jnp.float32)
        grad_gain_one = grad_gain_one + column_sum(first_grad * normed_first)
        grad_shift_one = grad_shift_one + column_sum(first_grad)
        residual_grad = normalize_back(first_grad * vector_full[5], normed_first, factor_first)
        attended_grad = residual_grad.astype(jnp.bfloat16)
        grad_output_bias = grad_output_bias + column_sum(attended_grad)
        attended_whole = lax.all_gather(attended_grad, "tensor", axis=0, tiled=True)
        output_sum = dot_rows(context_low, attended_whole)
        context_grad = (
            dot_back(attended_whole, output_w)
            .astype(jnp.bfloat16)
            .reshape(block_count, block_rows, local_heads, HEAD)
        )
        empty = jnp.zeros((seq_rows, local_heads, HEAD), jnp.float32)
        carried, query_grad = lax.scan(
            partial(attend_backward, keys, values, key_valid),
            (empty, empty),
            (query, context_grad, tops, totals),
        )
        joint_grad = jnp.concatenate(
            [
                query_grad.reshape(seq_rows, head_width),
                carried[0].reshape(seq_rows, head_width),
                carried[1].reshape(seq_rows, head_width),
            ],
            axis=1,
        ).astype(jnp.bfloat16)
        grad_query_bias = grad_query_bias + column_sum(joint_grad[:, :head_width])
        grad_value_bias = grad_value_bias + column_sum(joint_grad[:, 2 * head_width :])
        joint_sum = dot_rows(whole, joint_grad)
        input_grads.append(
            residual_grad
            + lax.psum_scatter(
                dot_back(joint_grad, joint_w).astype(jnp.bfloat16),
                "tensor",
                scatter_dimension=0,
                tiled=True,
            ).astype(jnp.float32)
        )
        batch_sums = (joint_sum, output_sum, inner_sum, outer_sum)
        local_totals = batch_sums if local_totals is None else add_tuples(local_totals, batch_sums)
    pieces = split_joint(
        local_totals[0], local_totals[1], local_totals[2], local_totals[3], head_width
    )
    shard_totals = (
        lax.psum_scatter(pieces[0], "fsdp", scatter_dimension=0, tiled=True),
        lax.psum_scatter(pieces[1], "fsdp", scatter_dimension=0, tiled=True),
        lax.psum_scatter(pieces[2], "fsdp", scatter_dimension=0, tiled=True),
        lax.psum_scatter(pieces[3], "fsdp", scatter_dimension=1, tiled=True),
        lax.psum_scatter(pieces[4], "fsdp", scatter_dimension=0, tiled=True),
        lax.psum_scatter(pieces[5], "fsdp", scatter_dimension=1, tiled=True),
    )
    vector_grads = (
        lax.psum_scatter(
            place(grad_query_bias, tensor_rank * head_width, width),
            ("fsdp", "tensor"),
            scatter_dimension=0,
            tiled=True,
        ),
        lax.psum_scatter(
            place(grad_value_bias, tensor_rank * head_width, width),
            ("fsdp", "tensor"),
            scatter_dimension=0,
            tiled=True,
        ),
        lax.psum_scatter(grad_output_bias, ("fsdp", "tensor"), scatter_dimension=0, tiled=True),
        lax.psum_scatter(
            place(grad_inner_bias, tensor_rank * inner_width, inner_width * tensor_size),
            ("fsdp", "tensor"),
            scatter_dimension=0,
            tiled=True,
        ),
        lax.psum_scatter(grad_outer_bias, ("fsdp", "tensor"), scatter_dimension=0, tiled=True),
        lax.psum_scatter(grad_gain_one, ("fsdp", "tensor"), scatter_dimension=0, tiled=True),
        lax.psum_scatter(grad_shift_one, ("fsdp", "tensor"), scatter_dimension=0, tiled=True),
        lax.psum_scatter(grad_gain_two, ("fsdp", "tensor"), scatter_dimension=0, tiled=True),
        lax.psum_scatter(grad_shift_two, ("fsdp", "tensor"), scatter_dimension=0, tiled=True),
    )
    return (
        jnp.stack(outputs),
        jnp.stack(input_grads),
        shard_totals[0],
        shard_totals[1],
        shard_totals[2],
        shard_totals[3],
        shard_totals[4],
        shard_totals[5],
        vector_grads[0],
        vector_grads[1],
        vector_grads[2],
        vector_grads[3],
        vector_grads[4],
        vector_grads[5],
        vector_grads[6],
        vector_grads[7],
        vector_grads[8],
    )


def solution(mesh):
    placed = (
        P("fsdp", "tensor", None),
        P("fsdp"),
        P("fsdp", "tensor", None),
        P("fsdp", "tensor"),
        P("fsdp", "tensor"),
        P("fsdp", "tensor"),
        P("tensor", "fsdp"),
        P("fsdp", "tensor"),
        P("tensor", "fsdp"),
        P(("fsdp", "tensor")),
        P(("fsdp", "tensor")),
        P(("fsdp", "tensor")),
        P(("fsdp", "tensor")),
        P(("fsdp", "tensor")),
        P(("fsdp", "tensor")),
        P(("fsdp", "tensor")),
        P(("fsdp", "tensor")),
        P(("fsdp", "tensor")),
    )
    return jax.shard_map(
        local,
        mesh=mesh,
        in_specs=placed,
        out_specs=(
            P("fsdp", "tensor", None),
            P("fsdp", "tensor", None),
            P("fsdp", "tensor"),
            P("fsdp", "tensor"),
            P("fsdp", "tensor"),
            P("tensor", "fsdp"),
            P("fsdp", "tensor"),
            P("tensor", "fsdp"),
            P(("fsdp", "tensor")),
            P(("fsdp", "tensor")),
            P(("fsdp", "tensor")),
            P(("fsdp", "tensor")),
            P(("fsdp", "tensor")),
            P(("fsdp", "tensor")),
            P(("fsdp", "tensor")),
            P(("fsdp", "tensor")),
            P(("fsdp", "tensor")),
        ),
        check_vma=False,
    )
```

profile of v0, /device:TPU:0, one launch (start us, length us, event | category | flops | bytes accessed | tf_op | source)
XLA Modules:
  0.0 1132.8 jit_solution(9939941270343481000)
XLA Ops:
  17.3 42.9 %all-reduce.19 = (f32[768]{0:T(1024)S(1)}, f32[768]{0:T(1024)S(1)}, f32[768]{0:T(1024)S(1)}, f32[768]{0:T(1024)S(1)}, f32[768]{0:T(1024)S(1)}, /*index=5*/f32[3072]{0:T(1024)}, f32[768]{0:T(1024)}, f32[768]{0:T(1024)S(1)}) all-reduce(f32[768]{0:T(1024)S(1)} %dynamic-update-slice.4, ...), channel_id=1, replica_groups=mesh['fsdp'=8,'tensor'=4] {'fsdp','tensor'}, use_global_device_ids=true, to_apply=%add.4 | all-reduce | flops 8448 | bytes 67584
  61.2 31.2 %all_gather.68 = bf16[192,768]{0,1:T(8,128)(2,1)S(1)} all-gather(bf16[192,96]{0,1:T(8,128)(2,1)S(1)} %copy.55), channel_id=1, replica_groups=mesh['fsdp'=8,'tensor'=4] {'fsdp'}, dimensions={1}, use_global_device_ids=true | all-gather | bytes 331776 | tf_op jit(solution)/shard_map/all_gather | solution.py:110
  92.4 31.2 %all_gather.62 = bf16[768,192]{1,0:T(8,128)(2,1)S(1)} all-gather(bf16[96,192]{1,0:T(8,128)(2,1)} %param.21), channel_id=1, replica_groups=mesh['fsdp'=8,'tensor'=4] {'fsdp'}, dimensions={0}, use_global_device_ids=true | all-gather | bytes 331776 | tf_op jit(solution)/shard_map/all_gather | solution.py:107
  123.7 31.2 %all_gather.63 = bf16[768,192]{1,0:T(8,128)(2,1)S(1)} all-gather(bf16[96,192]{1,0:T(8,128)(2,1)} %param.22), channel_id=1, replica_groups=mesh['fsdp'=8,'tensor'=4] {'fsdp'}, dimensions={0}, use_global_device_ids=true | all-gather | bytes 331776 | tf_op jit(solution)/shard_map/all_gather | solution.py:108
  154.8 31.0 %all_gather.64 = bf16[768,192]{1,0:T(8,128)(2,1)S(1)} all-gather(bf16[96,192]{1,0:T(8,128)(2,1)S(1)} %copy-done.146), channel_id=1, replica_groups=mesh['fsdp'=8,'tensor'=4] {'fsdp'}, dimensions={0}, use_global_device_ids=true | all-gather | bytes 331776 | tf_op jit(solution)/shard_map/all_gather | solution.py:109
  185.8 9.5 all-gather
  222.7 8.9 all-gather.1
  263.0 18.9 %reduce-scatter.35.cloned.1.call-done = bf16[128,768]{1,0:T(8,128)(2,1)} async-done(((bf16[512,768]{1,0:T(8,128)(2,1)}), bf16[128,768]{1,0:T(8,128)(2,1)}) %reduce-scatter.35.cloned.1.call-update) | async-done | bytes 196624 | tf_op jit(solution)/shard_map/reduce_scatter | solution.py:216
  281.9 25.9 %reduce-scatter.43.cloned.1.call-done = bf16[128,768]{1,0:T(8,128)(2,1)} async-done(((bf16[512,768]{1,0:T(8,128)(2,1)}), bf16[128,768]{1,0:T(8,128)(2,1)}) %reduce-scatter.43.cloned.1.call-update) | async-done | bytes 196624 | tf_op jit(solution)/shard_map/reduce_scatter | solution.py:216
  323.3 21.9 %all-gather.9.cloned.1.call-done = bf16[768,768]{0,1:T(8,128)(2,1)} async-done(((bf16[768,96]{0,1:T(8,128)(2,1)}), bf16[768,768]{0,1:T(8,128)(2,1)}) %all-gather.9.cloned.1.call-update) | async-done | bytes 1179664 | tf_op jit(solution)/shard_map/all_gather | solution.py:112
  363.2 11.0 all_gather.157
  379.7 20.7 %reduce-scatter.33.cloned.1.call-done = bf16[128,768]{1,0:T(8,128)(2,1)} async-done(((bf16[512,768]{1,0:T(8,128)(2,1)}), bf16[128,768]{1,0:T(8,128)(2,1)}) %reduce-scatter.33.cloned.1.call-update) | async-done | bytes 196624 | tf_op jit(solution)/shard_map/reduce_scatter | solution.py:232
  426.3 26.6 %reduce-scatter.41.cloned.1.call-done = bf16[128,768]{1,0:T(8,128)(2,1)} async-done(((bf16[512,768]{1,0:T(8,128)(2,1)}), bf16[128,768]{1,0:T(8,128)(2,1)}) %reduce-scatter.41.cloned.1.call-update) | async-done | bytes 196624 | tf_op jit(solution)/shard_map/reduce_scatter | solution.py:232
  493.4 10.4 all_gather.162
  553.4 26.4 %reduce-scatter.47.cloned.1.call-done = bf16[128,768]{1,0:T(8,128)(2,1)} async-done(((bf16[512,768]{1,0:T(8,128)(2,1)}), bf16[128,768]{1,0:T(8,128)(2,1)}) %reduce-scatter.47.cloned.1.call-update) | async-done | bytes 196624 | tf_op jit(solution)/shard_map/reduce_scatter | solution.py:262
  593.5 8.9 all_gather.163
  689.1 40.6 %all-reduce.18 = (f32[768]{0:T(1024)S(1)}, f32[768]{0:T(1024)S(1)}, f32[768]{0:T(1024)S(1)}, f32[768]{0:T(1024)S(1)}, f32[3072]{0:T(1024)S(1)}, /*index=5*/f32[7...) all-reduce(f32[768]{0:T(1024)S(1)} %dynamic-update-slice.8, ...), channel_id=1, replica_groups=mesh['fsdp'=8,'tensor'=4] {'fsdp','tensor'}, use_global_device_ids=true, to_apply=%add.8 | all-reduce | flops 9984 | bytes 79872
  740.2 17.1 %reduce-scatter.57.cloned.1.call-done = bf16[128,768]{1,0:T(8,128)(2,1)} async-done(((bf16[512,768]{1,0:T(8,128)(2,1)}), bf16[128,768]{1,0:T(8,128)(2,1)}) %reduce-scatter.57.cloned.1.call-update) | async-done | bytes 196624 | tf_op jit(solution)/shard_map/reduce_scatter | solution.py:299
  758.3 24.6 %reduce-scatter.49.cloned.1.call-done = bf16[128,768]{1,0:T(8,128)(2,1)} async-done(((bf16[512,768]{1,0:T(8,128)(2,1)}), bf16[128,768]{1,0:T(8,128)(2,1)}) %reduce-scatter.49.cloned.1.call-update) | async-done | bytes 196624 | tf_op jit(solution)/shard_map/reduce_scatter | solution.py:299
  785.2 64.5 %reduce-scatter.71.cloned.1.call-done = f32[96,192]{1,0:T(8,128)} async-done(((f32[768,192]{1,0:T(8,128)}), f32[96,192]{1,0:T(8,128)}) %reduce-scatter.71.cloned.1.call-update) | async-done | bytes 73744
  849.6 65.4 %reduce-scatter.69.cloned.1.call-done = f32[96,192]{1,0:T(8,128)} async-done(((f32[768,192]{1,0:T(8,128)}), f32[96,192]{1,0:T(8,128)}) %reduce-scatter.69.cloned.1.call-update) | async-done | bytes 73744
  915.0 65.9 %reduce-scatter.67.cloned.1.call-done = f32[96,192]{1,0:T(8,128)} async-done(((f32[768,192]{1,0:T(8,128)}), f32[96,192]{1,0:T(8,128)}) %reduce-scatter.67.cloned.1.call-update) | async-done | bytes 73744
  980.9 72.0 %reduce-scatter.63.cloned.1.call-done = f32[96,768]{1,0:T(8,128)} async-done(((f32[768,768]{1,0:T(8,128)}), f32[96,768]{1,0:T(8,128)}) %reduce-scatter.63.cloned.1.call-update) | async-done | bytes 294928 | tf_op jit(solution)/shard_map/reduce_scatter | solution.py:316
  1052.9 72.1 %reduce-scatter.65.cloned.1.call-done = f32[768,96]{0,1:T(8,128)} async-done(((f32[768,768]{0,1:T(8,128)}), f32[768,96]{0,1:T(8,128)}) %reduce-scatter.65.cloned.1.call-update) | async-done | bytes 294928 | tf_op jit(solution)/shard_map/reduce_scatter | solution.py:317
  (746 shorter events, 335.0 us)
Async XLA Ops:
  8.0 253.8 %reduce-scatter.31.cloned.1.call-start = ((), (), s32[]{:S(2)}) async-start(), calls=%async_computation.22 | async-start | bytes 983040 | tf_op jit(solution)/shard_map/reduce_scatter | solution.py:216
  204.4 58.6 %reduce-scatter.39.cloned.1.call-start = ((), (), s32[]{:S(2)}) async-start(), calls=%async_computation.28 | async-start | bytes 983040 | tf_op jit(solution)/shard_map/reduce_scatter | solution.py:216
  222.6 59.3 %reduce-scatter.35.cloned.1.call-start = ((), (), s32[]{:S(2)}) async-start(), calls=%async_computation.26 | async-start | bytes 983040 | tf_op jit(solution)/shard_map/reduce_scatter | solution.py:216
  242.2 65.6 %reduce-scatter.43.cloned.1.call-start = ((), (), s32[]{:S(2)}) async-start(), calls=%async_computation.30 | async-start | bytes 983040 | tf_op jit(solution)/shard_map/reduce_scatter | solution.py:216
  259.2 60.5 %all-gather.7.cloned.1.call-start = ((), (), s32[]{:S(2)}) async-start(), calls=%async_computation.23 | async-start | bytes 1327104 | tf_op jit(solution)/shard_map/all_gather | solution.py:111
  259.8 85.3 %all-gather.9.cloned.1.call-start = ((), (), s32[]{:S(2)}) async-start(), calls=%async_computation.24 | async-start | bytes 1327104 | tf_op jit(solution)/shard_map/all_gather | solution.py:112
  260.4 119.3 %reduce-scatter.37.cloned.1.call-start = ((), (), s32[]{:S(2)}) async-start(), calls=%async_computation.27 | async-start | bytes 983040 | tf_op jit(solution)/shard_map/reduce_scatter | solution.py:232
  348.1 52.4 %reduce-scatter.33.cloned.1.call-start = ((), (), s32[]{:S(2)}) async-start(), calls=%async_computation.25 | async-start | bytes 983040 | tf_op jit(solution)/shard_map/reduce_scatter | solution.py:232
  363.2 63.1 %reduce-scatter.45.cloned.1.call-start = ((), (), s32[]{:S(2)}) async-start(), calls=%async_computation.31 | async-start | bytes 983040 | tf_op jit(solution)/shard_map/reduce_scatter | solution.py:232
  379.6 73.3 %reduce-scatter.41.cloned.1.call-start = ((), (), s32[]{:S(2)}) async-start(), calls=%async_computation.29 | async-start | bytes 983040 | tf_op jit(solution)/shard_map/reduce_scatter | solution.py:232
  414.9 110.7 %reduce-scatter.51.cloned.1.call-start = ((), (), s32[]{:S(2)}) async-start(), calls=%async_computation.34 | async-start | bytes 983040 | tf_op jit(solution)/shard_map/reduce_scatter | solution.py:262
  475.9 51.6 %reduce-scatter.59.cloned.1.call-start = ((), (), s32[]{:S(2)}) async-start(), calls=%async_computation.38 | async-start | bytes 983040 | tf_op jit(solution)/shard_map/reduce_scatter | solution.py:262
  493.4 60.0 %reduce-scatter.55.cloned.1.call-start = ((), (), s32[]{:S(2)}) async-start(), calls=%async_computation.36 | async-start | bytes 983040 | tf_op jit(solution)/shard_map/reduce_scatter | solution.py:262
  510.2 69.6 %reduce-scatter.47.cloned.1.call-start = ((), (), s32[]{:S(2)}) async-start(), calls=%async_computation.32 | async-start | bytes 983040 | tf_op jit(solution)/shard_map/reduce_scatter | solution.py:262
  525.5 211.0 %reduce-scatter.73.cloned.1.call-start = ((), (), s32[]{:S(2)}) async-start(), calls=%async_computation.45 | async-start | bytes 884736
  616.4 121.8 %reduce-scatter.61.cloned.1.call-start = ((), (), s32[]{:S(2)}) async-start(), calls=%async_computation.39 | async-start | bytes 983040 | tf_op jit(solution)/shard_map/reduce_scatter | solution.py:299
  632.1 107.1 %reduce-scatter.53.cloned.1.call-start = ((), (), s32[]{:S(2)}) async-start(), calls=%async_computation.35 | async-start | bytes 983040 | tf_op jit(solution)/shard_map/reduce_scatter | solution.py:299
  641.1 116.2 %reduce-scatter.57.cloned.1.call-start = ((), (), s32[]{:S(2)}) async-start(), calls=%async_computation.37 | async-start | bytes 983040 | tf_op jit(solution)/shard_map/reduce_scatter | solution.py:299
  651.9 131.0 %reduce-scatter.49.cloned.1.call-start = ((), (), s32[]{:S(2)}) async-start(), calls=%async_computation.33 | async-start | bytes 983040 | tf_op jit(solution)/shard_map/reduce_scatter | solution.py:299
  661.1 188.5 %reduce-scatter.71.cloned.1.call-start = ((), (), s32[]{:S(2)}) async-start(), calls=%async_computation.44 | async-start | bytes 884736
  667.4 247.7 %reduce-scatter.69.cloned.1.call-start = ((), (), s32[]{:S(2)}) async-start(), calls=%async_computation.43 | async-start | bytes 884736
  668.6 312.3 %reduce-scatter.67.cloned.1.call-start = ((), (), s32[]{:S(2)}) async-start(), calls=%async_computation.42 | async-start | bytes 884736
  669.9 383.0 %reduce-scatter.63.cloned.1.call-start = ((), (), s32[]{:S(2)}) async-start(), calls=%async_computation.40 | async-start | bytes 2654208 | tf_op jit(solution)/shard_map/reduce_scatter | solution.py:316
  677.1 447.8 %reduce-scatter.65.cloned.1.call-start = ((), (), s32[]{:S(2)}) async-start(), calls=%async_computation.41 | async-start | bytes 2654208 | tf_op jit(solution)/shard_map/reduce_scatter | solution.py:317
  (237 other events, 2437.8 us)
Sparse Core Ops, SparseCore 0:
  204.5 22.4 reduce-scatter.30
  229.7 25.6 reduce-scatter.38
  258.6 23.2 reduce-scatter.34
  284.5 23.3 reduce-scatter.42
  348.2 23.9 reduce-scatter.36
  375.3 25.1 reduce-scatter.32
  403.0 23.2 reduce-scatter.44
  429.6 23.2 reduce-scatter.40
  476.0 25.0 reduce-scatter.50
  504.2 23.2 reduce-scatter.58
  530.1 23.2 reduce-scatter.54
  556.5 23.2 reduce-scatter.46
Sparse Core Ops, SparseCore 1:
  261.9 41.1 all-gather.6
  305.1 40.0 all-gather.8
  616.5 62.9 reduce-scatter.72
  682.8 22.3 reduce-scatter.60
  707.7 23.7 reduce-scatter.52
  734.2 23.0 reduce-scatter.56
  759.7 23.2 reduce-scatter.48
  787.0 62.6 reduce-scatter.70
  853.4 61.6 reduce-scatter.68
  919.3 61.6 reduce-scatter.66
  984.8 68.0 reduce-scatter.62
  1057.0 67.9 reduce-scatter.64
where the time goes:
time: 1140 us; the launch traced here: 1130 us
  waiting for transfers between devices  539 us (47%)
  blocking collectives  350 us (31%)
  matrix products  124 us (11%)
  other arithmetic  57.4 us (5%)
  local copies, waits for them, and re-layouts  40.8 us (4%)
  between operations  19.1 us (2%)
    unnamed x28, waiting for transfers between devices  197 us
    unnamed x2, blocking collectives  83.5 us
    reduce_scatter x1, waiting for transfers between devices, local(): lax.psum_scatter(pieces[5], 'fsdp', scatter_dimension=1, tiled=True)  72.1 us
    reduce_scatter x1, waiting for transfers between devices, local(): lax.psum_scatter(pieces[4], 'fsdp', scatter_dimension=0, tiled=True)  72 us
    reduce_scatter x4, waiting for transfers between devices, local(): lax.psum_scatter(jnp.dot(active, outer_w, preferred_element_type=jnp.floa...  53.4 us
    reduce_scatter x4, waiting for transfers between devices, local(): lax.psum_scatter(jnp.dot(context_low, output_w, preferred_element_type=jn...  44.8 us
    reduce_scatter x4, waiting for transfers between devices, local(): lax.psum_scatter(dot_back(joint_grad, joint_w).astype(jnp.bfloat16), 'ten...  41.8 us
    unnamed x510, local copies, waits for them, and re-layouts  37.6 us
  transfers between devices with their start and end apart: 24, of which 16 were waited for; matrix products, arithmetic and copies ran while one was open for 14% of the time, Pallas kernels for 0%

commit v1 on v0

--- a/solution.py
+++ b/solution.py
@@ -3,7 +3,11 @@
 import jax
 import jax.numpy as jnp
 from jax import lax
+from jax.experimental import pallas as pl
+from jax.experimental.pallas import tpu as pltpu
 from jax.sharding import PartitionSpec as P
+
+FSDP, TENSOR = "fsdp", "tensor"
 
 HEAD = 64
 
@@ -104,12 +108,12 @@
 
 def gather_weights(w_query, w_key, w_value, w_output, w_inner, w_outer):
     return (
-        lax.all_gather(w_query, "fsdp", axis=0, tiled=True),
-        lax.all_gather(w_key, "fsdp", axis=0, tiled=True),
-        lax.all_gather(w_value, "fsdp", axis=0, tiled=True),
-        lax.all_gather(w_output, "fsdp", axis=1, tiled=True),
-        lax.all_gather(w_inner, "fsdp", axis=0, tiled=True),
-        lax.all_gather(w_outer, "fsdp", axis=1, tiled=True),
+        lax.all_gather(w_query, FSDP, axis=0, tiled=True),
+        lax.all_gather(w_key, FSDP, axis=0, tiled=True),
+        lax.all_gather(w_value, FSDP, axis=0, tiled=True),
+        lax.all_gather(w_output, FSDP, axis=1, tiled=True),
+        lax.all_gather(w_inner, FSDP, axis=0, tiled=True),
+        lax.all_gather(w_outer, FSDP, axis=1, tiled=True),
     )
 
 
@@ -128,7 +132,7 @@
     return tuple((first_item + second_item for first_item, second_item in zip(left, right)))
 
 
-def local(
+def local_generic(
     tokens,
     lengths,
     cotangent,
@@ -148,8 +152,8 @@
     gain_second,
     shift_second,
 ):
-    tensor_size = lax.axis_size("tensor")
-    tensor_rank = lax.axis_index("tensor")
+    tensor_size = lax.axis_size(TENSOR)
+    tensor_rank = lax.axis_index(TENSOR)
     micro_count = tokens.shape[0]
     part_rows = tokens.shape[1]
     width = tokens.shape[2]
@@ -160,15 +164,15 @@
     block_rows = min(512, seq_rows)
     block_count = seq_rows // block_rows
     vector_full = (
-        lax.all_gather(b_query, ("fsdp", "tensor"), axis=0, tiled=True),
-        lax.all_gather(b_value, ("fsdp", "tensor"), axis=0, tiled=True),
-        lax.all_gather(b_output, ("fsdp", "tensor"), axis=0, tiled=True),
-        lax.all_gather(b_inner, ("fsdp", "tensor"), axis=0, tiled=True),
-        lax.all_gather(b_outer, ("fsdp", "tensor"), axis=0, tiled=True),
-        lax.all_gather(gain_first, ("fsdp", "tensor"), axis=0, tiled=True),
-        lax.all_gather(shift_first, ("fsdp", "tensor"), axis=0, tiled=True),
-        lax.all_gather(gain_second, ("fsdp", "tensor"), axis=0, tiled=True),
-        lax.all_gather(shift_second, ("fsdp", "tensor"), axis=0, tiled=True),
+        lax.all_gather(b_query, (FSDP, TENSOR), axis=0, tiled=True),
+        lax.all_gather(b_value, (FSDP, TENSOR), axis=0, tiled=True),
+        lax.all_gather(b_output, (FSDP, TENSOR), axis=0, tiled=True),
+        lax.all_gather(b_inner, (FSDP, TENSOR), axis=0, tiled=True),
+        lax.all_gather(b_outer, (FSDP, TENSOR), axis=0, tiled=True),
+        lax.all_gather(gain_first, (FSDP, TENSOR), axis=0, tiled=True),
+        lax.all_gather(shift_first, (FSDP, TENSOR), axis=0, tiled=True),
+        lax.all_gather(gain_second, (FSDP, TENSOR), axis=0, tiled=True),
+        lax.all_gather(shift_second, (FSDP, TENSOR), axis=0, tiled=True),
     )
     query_bias = lax.dynamic_slice_in_dim(vector_full[0], tensor_rank * head_width, head_width)
     value_bias = lax.dynamic_slice_in_dim(vector_full[1], tensor_rank * head_width, head_width)
@@ -201,7 +205,7 @@
         key_valid = slot_index < length
         row_valid = (part_index < length).astype(jnp.float32)[:, None]
         own_rows = tokens[micro_index]
-        whole = lax.all_gather(own_rows, "tensor", axis=0, tiled=True)
+        whole = lax.all_gather(own_rows, TENSOR, axis=0, tiled=True)
         joint = (jnp.dot(whole, joint_w, preferred_element_type=jnp.float32) + joint_bias).astype(
             jnp.bfloat16
         )
@@ -217,7 +221,7 @@
                 jnp.dot(context_low, output_w, preferred_element_type=jnp.float32).astype(
                     jnp.bfloat16
                 ),
-                "tensor",
+                TENSOR,
                 scatter_dimension=0,
                 tiled=True,
             ).astype(jnp.float32)
@@ -225,13 +229,13 @@
         )
         normed_first, factor_first = normalize(own_rows.astype(jnp.float32) + attended)
         first = normed_first * vector_full[5] + vector_full[6]
-        first_whole = lax.all_gather(first.astype(jnp.bfloat16), "tensor", axis=0, tiled=True)
+        first_whole = lax.all_gather(first.astype(jnp.bfloat16), TENSOR, axis=0, tiled=True)
         inner = jnp.dot(first_whole, inner_w, preferred_element_type=jnp.float32) + inner_bias
         active = gelu_value(inner).astype(jnp.bfloat16)
         mixed = (
             lax.psum_scatter(
                 jnp.dot(active, outer_w, preferred_element_type=jnp.float32).astype(jnp.bfloat16),
-                "tensor",
+                TENSOR,
                 scatter_dimension=0,
                 tiled=True,
             ).astype(jnp.float32)
@@ -254,14 +258,14 @@
         sum_grad = normalize_back(out_grad * vector_full[7], normed_second, factor_second)
         mixed_grad = sum_grad.astype(jnp.bfloat16)
         grad_outer_bias = grad_outer_bias + column_sum(mixed_grad)
-        mixed_whole = lax.all_gather(mixed_grad, "tensor", axis=0, tiled=True)
+        mixed_whole = lax.all_gather(mixed_grad, TENSOR, axis=0, tiled=True)
         outer_sum = dot_rows(active, mixed_whole)
         inner_grad = (dot_back(mixed_whole, outer_w) * gelu_slope(inner)).astype(jnp.bfloat16)
         grad_inner_bias = grad_inner_bias + column_sum(inner_grad)
         inner_sum = dot_rows(first_whole, inner_grad)
         first_grad = sum_grad + lax.psum_scatter(
             dot_back(inner_grad, inner_w).astype(jnp.bfloat16),
-            "tensor",
+            TENSOR,
             scatter_dimension=0,
             tiled=True,
         ).astype(jnp.float32)
@@ -270,7 +274,7 @@
         residual_grad = normalize_back(first_grad * vector_full[5], normed_first, factor_first)
         attended_grad = residual_grad.astype(jnp.bfloat16)
         grad_output_bias = grad_output_bias + column_sum(attended_grad)
-        attended_whole = lax.all_gather(attended_grad, "tensor", axis=0, tiled=True)
+        attended_whole = lax.all_gather(attended_grad, TENSOR, axis=0, tiled=True)
         output_sum = dot_rows(context_low, attended_whole)
         context_grad = (
             dot_back(attended_whole, output_w)
@@ -298,7 +302,7 @@
             residual_grad
             + lax.psum_scatter(
                 dot_back(joint_grad, joint_w).astype(jnp.bfloat16),
-                "tensor",
+                TENSOR,
                 scatter_dimension=0,
                 tiled=True,
             ).astype(jnp.float32)
@@ -309,38 +313,38 @@
         local_totals[0], local_totals[1], local_totals[2], local_totals[3], head_width
     )
     shard_totals = (
-        lax.psum_scatter(pieces[0], "fsdp", scatter_dimension=0, tiled=True),
-        lax.psum_scatter(pieces[1], "fsdp", scatter_dimension=0, tiled=True),
-        lax.psum_scatter(pieces[2], "fsdp", scatter_dimension=0, tiled=True),
-        lax.psum_scatter(pieces[3], "fsdp", scatter_dimension=1, tiled=True),
-        lax.psum_scatter(pieces[4], "fsdp", scatter_dimension=0, tiled=True),
-        lax.psum_scatter(pieces[5], "fsdp", scatter_dimension=1, tiled=True),
+        lax.psum_scatter(pieces[0], FSDP, scatter_dimension=0, tiled=True),
+        lax.psum_scatter(pieces[1], FSDP, scatter_dimension=0, tiled=True),
+        lax.psum_scatter(pieces[2], FSDP, scatter_dimension=0, tiled=True),
+        lax.psum_scatter(pieces[3], FSDP, scatter_dimension=1, tiled=True),
+        lax.psum_scatter(pieces[4], FSDP, scatter_dimension=0, tiled=True),
+        lax.psum_scatter(pieces[5], FSDP, scatter_dimension=1, tiled=True),
     )
     vector_grads = (
         lax.psum_scatter(
             place(grad_query_bias, tensor_rank * head_width, width),
-            ("fsdp", "tensor"),
+            (FSDP, TENSOR),
             scatter_dimension=0,
             tiled=True,
         ),
         lax.psum_scatter(
             place(grad_value_bias, tensor_rank * head_width, width),
-            ("fsdp", "tensor"),
+            (FSDP, TENSOR),
             scatter_dimension=0,
             tiled=True,
         ),
-        lax.psum_scatter(grad_output_bias, ("fsdp", "tensor"), scatter_dimension=0, tiled=True),
+        lax.psum_scatter(grad_output_bias, (FSDP, TENSOR), scatter_dimension=0, tiled=True),
         lax.psum_scatter(
             place(grad_inner_bias, tensor_rank * inner_width, inner_width * tensor_size),
-            ("fsdp", "tensor"),
+            (FSDP, TENSOR),
             scatter_dimension=0,
             tiled=True,
         ),
-        lax.psum_scatter(grad_outer_bias, ("fsdp", "tensor"), scatter_dimension=0, tiled=True),
-        lax.psum_scatter(grad_gain_one, ("fsdp", "tensor"), scatter_dimension=0, tiled=True),
-        lax.psum_scatter(grad_shift_one, ("fsdp", "tensor"), scatter_dimension=0, tiled=True),
-        lax.psum_scatter(grad_gain_two, ("fsdp", "tensor"), scatter_dimension=0, tiled=True),
-        lax.psum_scatter(grad_shift_two, ("fsdp", "tensor"), scatter_dimension=0, tiled=True),
+        lax.psum_scatter(grad_outer_bias, (FSDP, TENSOR), scatter_dimension=0, tiled=True),
+        lax.psum_scatter(grad_gain_one, (FSDP, TENSOR), scatter_dimension=0, tiled=True),
+        lax.psum_scatter(grad_shift_one, (FSDP, TENSOR), scatter_dimension=0, tiled=True),
+        lax.psum_scatter(grad_gain_two, (FSDP, TENSOR), scatter_dimension=0, tiled=True),
+        lax.psum_scatter(grad_shift_two, (FSDP, TENSOR), scatter_dimension=0, tiled=True),
     )
     return (
         jnp.stack(outputs),
@@ -363,49 +367,843 @@
     )
 
 
+MESH = pl.DeviceIdType.MESH
+WIDTH = 768
+HIDDEN = 3072
+HALF = WIDTH // 2
+KINDS = 3
+VECTOR_ROWS = 16
+ROW_OUTPUT, ROW_OUTER, ROW_GAIN1, ROW_SHIFT1, ROW_GAIN2, ROW_SHIFT2, ROW_INNER = 4, 5, 6, 7, 8, 9, 10
+BF16 = jnp.bfloat16
+F32 = jnp.float32
+
+
+def fits(sizes):
+    fsdp = sizes[FSDP]
+    return sizes[TENSOR] == 4 and fsdp % 2 == 0 and WIDTH % (16 * fsdp) == 0
+
+
+class Place:
+    def __init__(self, nz):
+        self.f = lax.axis_index(FSDP)
+        self.t = lax.axis_index(TENSOR)
+        self.nz = nz
+        self.z = self.f // 2
+        self.x = self.f % 2
+        self.y = self.t // 2
+        self.c = self.t % 2
+        self.core = (self.f, self.t + 1 - 2 * self.c)
+        self.along_y = (self.f, self.t + 2 - 4 * self.y)
+        self.along_x = (self.f + 1 - 2 * self.x, self.t)
+
+    def z_at(self, step):
+        return (self.z + step) % self.nz
+
+    def z_back(self, step):
+        return (self.z + self.nz - step) % self.nz
+
+    def along_z(self, step):
+        return (self.z_at(step) * 2 + self.x, self.t)
+
+    def in_group(self, step):
+        return (self.f, (self.t + step) % 4)
+
+
+class Net:
+    def __init__(self, send_sems, recv_sems):
+        self.send_sems = send_sems
+        self.recv_sems = recv_sems
+        self.count = 0
+
+    def plan(self, source, target, device):
+        copy = pltpu.make_async_remote_copy(
+            src_ref=source,
+            dst_ref=target,
+            send_sem=self.send_sems.at[self.count],
+            recv_sem=self.recv_sems.at[self.count],
+            device_id=device,
+            device_id_type=MESH,
+        )
+        self.count += 1
+        return copy
+
+    def keep(self, ref, device):
+        return self.plan(ref, ref, device)
+
+
+def start_all(copies):
+    for copy in copies:
+        copy.start()
+
+
+def sent_all(copies):
+    for copy in copies:
+        copy.wait_send()
+
+
+def greet(place):
+    barrier = pltpu.get_barrier_semaphore()
+    peers = [place.in_group(1), place.in_group(2), place.in_group(3), place.along_x]
+    peers += [place.along_z(step) for step in range(1, place.nz)]
+    for peer in peers:
+        pl.semaphore_signal(barrier, inc=1, device_id=peer, device_id_type=MESH)
+    pl.semaphore_wait(barrier, len(peers))
+
+
+def wait_all(copies):
+    for copy in copies:
+        copy.wait_recv()
+
+
+def vector_peers(place):
+    peers = []
+    stride = 1
+    while stride < place.nz:
+        z = place.z
+        other = z + stride - 2 * stride * ((z // stride) % 2)
+        peers.append((other * 2 + place.x, place.t))
+        stride *= 2
+    peers.insert(1, place.core)
+    return peers + [place.along_x, place.along_y]
+
+
+class Exchange:
+    def __init__(self, net, place, total, slots):
+        self.total, self.slots = total, slots
+        self.copies = [net.plan(total, slots.at[i], peer) for i, peer in enumerate(vector_peers(place))]
+
+    def start(self, index):
+        self.copies[index].start()
+
+    def finish(self, index):
+        self.copies[index].wait()
+        self.total[...] += self.slots[index]
+
+    def rest(self, index):
+        for later in range(index, len(self.copies)):
+            self.start(later)
+            self.finish(later)
+
+
+def dot(left, right):
+    return lax.dot_general(left, right, (((1,), (0,)), ((), ())), preferred_element_type=F32)
+
+
+class Layer:
+    def __init__(self, refs, length):
+        (
+            self.w, self.rows, self.back, self.rows_turned, self.joint, self.probs, self.context, self.acc,
+            self.normed, self.factor, self.first_low, self.first_turned, self.active, self.slope, self.grad_low,
+            self.grad_turned, self.out, self.vec, self.sums,
+        ) = refs
+        self.length = length
+        self.seq = self.rows.shape[0]
+        self.block = 128
+
+    def weight(self, kind, t):
+        return self.w[kind, t // 2, t % 2].reshape(WIDTH, WIDTH)
+
+    def output_weight(self, t):
+        return self.w[0, t // 2, t % 2, :, :, :, 512:768].reshape(WIDTH, 256)
+
+    def store_grad(self, kind, t, value):
+        nz = self.w.shape[3]
+        self.w[kind, t // 2, t % 2] = value.astype(BF16).reshape(nz, 2, WIDTH // (2 * nz), WIDTH)
+
+    def row(self, index):
+        return self.vec[pl.ds(index, 1), :]
+
+    def blocks(self, body):
+        def step(i, carry):
+            body(pl.ds(pl.multiple_of(i * self.block, self.block), self.block), i)
+            return carry
+
+        lax.fori_loop(0, self.seq // self.block, step, 0)
+
+    def row_valid(self, i):
+        index = lax.broadcasted_iota(jnp.int32, (self.block, 1), 0) + i * self.block
+        return (index < self.length).astype(F32)
+
+    def lanes(self, low, high, width):
+        lane = lax.broadcasted_iota(jnp.int32, (1, width), 1)
+        return (lane >= low) & (lane < high)
+
+    def pick(self, value, low, high):
+        return jnp.where(self.lanes(low, high, value.shape[1]), value, jnp.zeros_like(value))
+
+    def head_query(self, t, h):
+        return self.joint[t, :, 0:128] if h < 2 else self.joint[t, :, 384:512]
+
+    def head_key(self, t, h):
+        return self.joint[t, :, 128:256] if h < 2 else self.joint[t, :, 640:768]
+
+    def head_side(self, value, h):
+        return self.pick(value, 0, 64) if h == 0 else self.pick(value, 64, 128)
+
+    def head_value(self, t, h):
+        return self.pick(self.joint[t, :, 256:512], h * 64, h * 64 + 64)
+
+    def project(self, t):
+        self.joint[t] = (dot(self.rows[...], self.weight(0, t)) + self.row(t)).astype(BF16)
+
+    def attend(self, t):
+        key_valid = lax.broadcasted_iota(jnp.int32, (1, self.seq), 1) < self.length
+        context = None
+        for h in range(3):
+            raw = dot_back(self.head_query(t, h), self.head_side(self.head_key(t, h), h))
+            masked = jnp.where(key_valid, raw * HEAD ** -0.5, -1e9)
+            expo = jnp.exp(masked - jnp.max(masked, axis=1, keepdims=True))
+            probs = (expo * (1.0 / jnp.sum(expo, axis=1, keepdims=True))).astype(BF16)
+            self.probs[t * 3 + h] = probs
+            part = dot(probs, self.head_value(t, h))
+            context = part if context is None else context + part
+        low = context.astype(BF16)
+        self.context[t] = low
+        self.acc[...] += dot_back(low, self.output_weight(t))
+
+    def start(self):
+        def body(rows, i):
+            self.acc[rows] = self.rows[rows].astype(F32) + self.row(ROW_OUTPUT)
+
+        self.blocks(body)
+
+    def norm_first(self):
+        def body(rows, i):
+            normed, factor = normalize(self.acc[rows])
+            self.normed[rows] = normed
+            self.factor[rows] = jnp.broadcast_to(factor, (self.block, 128))
+            first = normed * self.row(ROW_GAIN1) + self.row(ROW_SHIFT1)
+            self.first_low[rows] = first.astype(BF16)
+            self.acc[rows] = first + self.row(ROW_OUTER)
+
+        self.blocks(body)
+
+    def feed_inner(self, t):
+        inner = dot(self.first_low[...], self.weight(1, t)) + self.row(ROW_INNER + t)
+        gate = 1.0 + lax.erf(inner * root_half)
+        self.active[t] = (0.5 * inner * gate).astype(BF16)
+        self.slope[t] = (0.5 * gate + inner * inverse_root_two_pi * jnp.exp(-0.5 * inner * inner)).astype(BF16)
+
+    def feed_outer(self, t):
+        self.acc[...] += dot_back(self.active[t], self.weight(2, t))
+
+    def clear_sums(self):
+        self.sums[...] = jnp.zeros_like(self.sums)
+
+    def add_sum(self, index, value):
+        self.sums[pl.ds(index, 1), :] += jnp.sum(value, axis=0, keepdims=True)
+
+    def norm_second(self):
+        def body(rows, i):
+            normed, factor = normalize(self.acc[rows])
+            valid = self.row_valid(i)
+            gain = self.row(ROW_GAIN2)
+            self.out[rows] = ((normed * gain + self.row(ROW_SHIFT2)) * valid).astype(BF16)
+            out_grad = self.back[rows].astype(F32) * valid
+            self.add_sum(ROW_GAIN2, out_grad * normed)
+            self.add_sum(ROW_SHIFT2, out_grad)
+            sum_grad = normalize_back(out_grad * gain, normed, factor)
+            self.acc[rows] = sum_grad
+            low = sum_grad.astype(BF16)
+            self.grad_low[rows] = low
+            self.add_sum(ROW_OUTER, low.astype(F32))
+
+        self.blocks(body)
+        self.grad_turned[...] = self.grad_low[...].T
+
+    def outer_back(self, t):
+        grad = (dot(self.grad_low[...], self.weight(2, t)) * self.slope[t].astype(F32)).astype(BF16)
+        self.slope[t] = grad
+        self.add_sum(ROW_INNER + t, grad.astype(F32))
+        self.store_grad(2, t, dot(self.grad_turned[...], self.active[t]))
+
+    def inner_back(self, t):
+        grad = self.slope[t]
+        self.acc[...] += dot_back(grad, self.weight(1, t))
+        self.store_grad(1, t, dot(self.first_turned[...], grad))
+
+    def norm_first_back(self):
+        def body(rows, i):
+            grad = self.acc[rows]
+            normed = self.normed[rows]
+            self.add_sum(ROW_GAIN1, grad * normed)
+            self.add_sum(ROW_SHIFT1, grad)
+            residual = normalize_back(grad * self.row(ROW_GAIN1), normed, self.factor[rows][:, 0:1])
+            self.acc[rows] = residual
+            low = residual.astype(BF16)
+            self.grad_low[rows] = low
+            self.add_sum(ROW_OUTPUT, low.astype(F32))
+
+        self.blocks(body)
+        self.grad_turned[...] = self.grad_low[...].T
+
+    def attend_back(self, t):
+        context_grad = self.pick(dot(self.grad_low[...], self.output_weight(t)), 0, 192).astype(BF16)
+        query_grads, key_grads, value_grad = [], [], None
+        for h in range(3):
+            probs = self.probs[t * 3 + h]
+            prob_grad = dot_back(context_grad, self.head_value(t, h))
+            wide = probs.astype(F32)
+            delta = jnp.sum(wide * prob_grad, axis=1, keepdims=True)
+            score_grad = (wide * (prob_grad - delta)).astype(BF16)
+            query_grads.append(dot(score_grad, self.head_side(self.head_key(t, h), h)) * HEAD ** -0.5)
+            key_grads.append(dot_rows(score_grad, self.head_side(self.head_query(t, h), h)) * HEAD ** -0.5)
+            part = dot_rows(probs, self.pick(context_grad, h * 64, h * 64 + 64))
+            value_grad = part if value_grad is None else value_grad + part
+        self.joint[t, :, 0:128] = (query_grads[0] + query_grads[1]).astype(BF16)
+        self.joint[t, :, 128:256] = (key_grads[0] + key_grads[1]).astype(BF16)
+        self.joint[t, :, 256:384] = value_grad[:, 0:128].astype(BF16)
+        self.joint[t, :, 384:512] = (value_grad[:, 128:256] + query_grads[2]).astype(BF16)
+        self.joint[t, :, 512:640] = jnp.zeros((self.seq, 128), BF16)
+        self.joint[t, :, 640:768] = key_grads[2].astype(BF16)
+
+    def joint_back(self, t):
+        joint = self.joint[t]
+        self.sums[pl.ds(t, 1), :] = jnp.sum(joint.astype(F32), axis=0, keepdims=True)
+        self.acc[...] += dot_back(joint, self.weight(0, t))
+        nz = self.w.shape[3]
+        shape = (nz, 2, WIDTH // (2 * nz), -1)
+        main = dot(self.rows_turned[...], joint[:, 0:512])
+        side = dot(self.rows_turned[...], joint[:, 512:768]) + dot(self.grad_turned[...], self.context[t])
+        self.w[0, t // 2, t % 2, :, :, :, 0:512] = main.astype(BF16).reshape(shape[:3] + (512,))
+        self.w[0, t // 2, t % 2, :, :, :, 512:768] = side.astype(BF16).reshape(shape[:3] + (256,))
+
+    def finish(self):
+        def body(rows, i):
+            self.back[rows] = self.acc[rows].astype(BF16)
+
+        self.blocks(body)
+
+
+def each(count, body):
+    def step(i, carry):
+        body(i)
+        return carry
+
+    lax.fori_loop(0, count, step, 0)
+
+
+BUFFER_COUNT = 19
+
+
+def buffer_shapes(nz, seq):
+    part = WIDTH // (2 * nz)
+    low, wide = (seq, WIDTH), (WIDTH, seq)
+    shapes = [
+        ((KINDS, 2, 2, nz, 2, part, WIDTH), BF16),
+        (low, BF16),
+        (low, BF16),
+        (wide, BF16),
+        ((4, seq, WIDTH), BF16),
+        ((12, seq, seq), BF16),
+        ((4, seq, 256), BF16),
+        (low, F32),
+        (low, F32),
+        ((seq, 128), F32),
+        (low, BF16),
+        (wide, BF16),
+        ((4, seq, WIDTH), BF16),
+        ((4, seq, WIDTH), BF16),
+        (low, BF16),
+        (wide, BF16),
+        (low, BF16),
+        ((VECTOR_ROWS, WIDTH), F32),
+        ((VECTOR_ROWS, WIDTH), F32),
+    ]
+    return [pltpu.VMEM(*shape) for shape in shapes]
+
+
+def landing_shapes(nz):
+    part = WIDTH // (2 * nz)
+    shapes = [
+        (KINDS, 2, nz, 2, part, WIDTH),
+        (KINDS, nz, 2, part, HALF),
+        (KINDS, nz, part, HALF),
+        (KINDS, nz - 1, part, HALF),
+        (KINDS, 2, nz, part, HALF),
+        (KINDS, nz - 1, 2, part, HALF),
+        (KINDS, 3, part, HALF),
+    ]
+    return [pltpu.VMEM(shape, BF16) for shape in shapes]
+
+
+class Gather:
+    def __init__(self, net, place, own, w, k):
+        p = place
+        a, b = pl.ds(0, HALF), pl.ds(HALF, HALF)
+        own_a, own_b = own.at[k, :, a], own.at[k, :, b]
+        mine_a, mine_b = (w.at[k, p.y, p.c, p.z, p.x, :, cols] for cols in (a, b))
+        steps = range(1, p.nz)
+        self.az = [net.plan(own_a, mine_a, p.along_z(step)) for step in steps]
+        self.by = [net.plan(own_b, mine_b, p.along_y)]
+        self.ax = [net.plan(own_a, mine_a, p.along_x)]
+        self.ax += [net.keep(w.at[k, p.y, p.c, p.z_back(step), p.x, :, a], p.along_x) for step in steps]
+        self.ay = [net.keep(w.at[k, p.y, p.c, :, x, :, a], p.along_y) for x in (p.x, 1 - p.x)]
+        self.ac = [net.keep(w.at[k, y, p.c, :, :, :, a], p.core) for y in (p.y, 1 - p.y)]
+        self.bz = [net.keep(w.at[k, :, p.c, p.z, p.x, :, b], p.along_z(step)) for step in steps]
+        self.bx = [net.keep(w.at[k, :, p.c, p.z_back(step), p.x, :, b], p.along_x) for step in range(p.nz)]
+        self.bc = [net.keep(w.at[k, :, p.c, :, x, :, b], p.core) for x in (p.x, 1 - p.x)]
+
+    def b_y_to_z(self):
+        wait_all(self.by)
+        start_all(self.bz)
+        self.bx[0].start()
+
+    def a_z_to_x(self):
+        for arrived, onward in zip(self.az, self.ax[1:]):
+            arrived.wait_recv()
+            onward.start()
+        self.ay[0].start()
+
+    def a_x_to_y(self):
+        wait_all(self.ax)
+        self.ay[1].start()
+        self.ac[0].start()
+
+    def b_z_to_x(self):
+        for arrived, onward in zip(self.bz, self.bx[1:]):
+            arrived.wait_recv()
+            onward.start()
+        self.bc[0].start()
+
+    def a_y_to_core(self):
+        wait_all(self.ay)
+        self.ac[1].start()
+
+    def b_x_to_core(self):
+        wait_all(self.bx)
+        self.bc[1].start()
+
+    def done(self):
+        wait_all(self.ac)
+        wait_all(self.bc)
+
+    def sent(self):
+        for copies in (self.az, self.ax, self.ay, self.ac, self.by, self.bz, self.bx, self.bc):
+            sent_all(copies)
+
+
+class Reduce:
+    def __init__(self, net, place, w, landings, result, k):
+        p = self.place = place
+        self.core, self.ya, self.xa, self.za, self.xb, self.zb, self.yb = (ref.at[k] for ref in landings)
+        self.w, self.result = w.at[k], result.at[k]
+        self.a, self.b = pl.ds(0, HALF), pl.ds(HALF, HALF)
+        self.ys = ys = (1 - p.y, p.y)
+        self.xs = xs = (1 - p.x, p.x)
+        self.zs = zs = [p.z_at((step + 1) % p.nz) for step in range(p.nz)]
+        self.c = [net.plan(self.w.at[y, 1 - p.c], self.core.at[y], p.core) for y in ys]
+        self.ay = [net.plan(self.core.at[ys[0], :, x, :, self.a], self.ya.at[:, x], p.along_y) for x in xs]
+        self.bx = [
+            [net.plan(self.core.at[y, z, xs[0], :, self.b], self.xb.at[y, z], p.along_x) for z in zs] for y in ys
+        ]
+        self.bz = [
+            [net.plan(self.xb.at[y, zs[i]], self.zb.at[i, y], p.along_z(i + 1)) for i in range(p.nz - 1)] for y in ys
+        ]
+        self.by = [net.plan(self.yb.at[ys[0]], self.yb.at[2], p.along_y)]
+        self.ax = [net.plan(self.ya.at[z, xs[0]], self.xa.at[z], p.along_x) for z in zs]
+        self.az = [net.plan(self.xa.at[zs[i]], self.za.at[i], p.along_z(i + 1)) for i in range(p.nz - 1)]
+
+    def add(self, target, source):
+        target[...] = (target[...].astype(F32) + source[...].astype(F32)).astype(BF16)
+
+    def core_half(self, half):
+        y = self.ys[half]
+        self.c[half].wait_recv()
+
+        def body(z):
+            self.add(self.core.at[y, z], self.w.at[y, self.place.c, z])
+
+        each(self.place.nz, body)
+        if half == 0:
+            start_all(self.ay)
+        start_all(self.bx[half])
+
+    def a_y(self, index):
+        self.ay[index].wait_recv()
+        x = self.xs[index]
+
+        def body(z):
+            self.add(self.ya.at[z, x], self.core.at[self.ys[1], z, x, :, self.a])
+
+        each(self.place.nz, body)
+        if index == 0:
+            start_all(self.ax)
+
+    def b_x(self, half):
+        y = self.ys[half]
+        for i, z in enumerate(self.zs):
+            self.bx[half][i].wait_recv()
+            self.add(self.xb.at[y, z], self.core.at[y, z, self.xs[1], :, self.b])
+            if i < self.place.nz - 1:
+                self.bz[half][i].start()
+
+    def a_x(self):
+        for i, z in enumerate(self.zs):
+            self.ax[i].wait_recv()
+            self.add(self.xa.at[z], self.ya.at[z, self.xs[1]])
+            if i < self.place.nz - 1:
+                self.az[i].start()
+
+    def b_z(self):
+        for half, y in enumerate(self.ys):
+            wait_all(self.bz[half])
+            total = self.xb[y, self.place.z].astype(F32)
+            for i in range(self.place.nz - 1):
+                total += self.zb[i, y].astype(F32)
+            self.yb[y] = total.astype(BF16)
+            if half == 0:
+                start_all(self.by)
+
+    def a_z(self):
+        wait_all(self.az)
+        total = self.xa[self.place.z].astype(F32)
+        for i in range(self.place.nz - 1):
+            total += self.za[i].astype(F32)
+        self.result[:, self.a] = total
+
+    def b_y(self):
+        wait_all(self.by)
+        self.result[:, self.b] = self.yb[self.ys[1]].astype(F32) + self.yb[2].astype(F32)
+
+    def sent(self):
+        for copies in (self.c, self.ay, *self.bx, *self.bz, self.by, self.ax, self.az):
+            sent_all(copies)
+
+
+def ticks(i, table):
+    for when, actions in table.items():
+        @pl.when(i == when)
+        def _(actions=actions):
+            for action, *given in actions:
+                action(*given)
+
+
+def layer_kernel(nz, *refs):
+    own, tokens, cotangent, lengths, vec_in, result, outs, backs, totals = refs[:9]
+    rest = list(refs[9:])
+    buffers, rest = rest[:BUFFER_COUNT], rest[BUFFER_COUNT:]
+    landings, (slots, back_slots, send_sems, recv_sems, local_sems) = rest[:7], rest[7:]
+    place = Place(nz)
+    net = Net(send_sems, recv_sems)
+    t = place.t
+    quarter = tokens.shape[1]
+    layer = Layer(buffers, lengths[t])
+    joint, inner, outer = [Gather(net, place, own, layer.w, k) for k in range(KINDS)]
+    to_joint, to_inner, to_outer = [Reduce(net, place, layer.w, landings, result, k) for k in range(KINDS)]
+
+    def quarter_of(ref, index):
+        return ref.at[pl.ds(pl.multiple_of(index * quarter, quarter), quarter)]
+
+    def swap_in(source, target):
+        return [
+            net.plan(source.at[(t + step) % 4], quarter_of(target, t), place.in_group(step)) for step in (2, 1, 3)
+        ]
+
+    def swap_out(source, target):
+        return [
+            net.plan(quarter_of(source, (t + step) % 4), target.at[t], place.in_group(step)) for step in (2, 1, 3)
+        ]
+
+    token_in = swap_in(tokens, layer.rows)
+    back_in = swap_in(cotangent, layer.back)
+    out_out = swap_out(layer.out, outs)
+    back_out = swap_out(layer.back, backs)
+    vec = Exchange(net, place, layer.vec, slots)
+    sums = Exchange(net, place, totals, back_slots)
+    pairs = [
+        (tokens.at[t], quarter_of(layer.rows, t)),
+        (cotangent.at[t], quarter_of(layer.back, t)),
+        *[(own.at[k], layer.w.at[k, place.y, place.c, place.z, place.x]) for k in range(KINDS)],
+        (quarter_of(layer.out, t), outs.at[t]),
+        (quarter_of(layer.back, t), backs.at[t]),
+    ]
+    local = [pltpu.make_async_copy(*pair, local_sems.at[i]) for i, pair in enumerate(pairs)]
+
+    def order(i):
+        return (1 - place.y + i) % 2 * 2 + (1 - place.c + i // 2) % 2
+
+    layer.vec[...] = vec_in[...]
+    greet(place)
+    vec.start(0)
+    start_all(joint.by + inner.by + outer.by)
+    start_all(joint.az)
+    joint.ax[0].start()
+    start_all(token_in)
+    start_all(local[:5])
+    vec.finish(0)
+    vec.start(1)
+    vec.finish(1)
+    vec.start(2)
+    for copy in local[:5]:
+        copy.wait()
+    joint.b_y_to_z()
+    joint.a_z_to_x()
+    vec.finish(2)
+    vec.start(3)
+    start_all(inner.az)
+    inner.ax[0].start()
+    inner.b_y_to_z()
+    vec.finish(3)
+    vec.rest(4)
+    joint.a_x_to_y()
+    joint.b_z_to_x()
+    start_all(outer.az)
+    outer.ax[0].start()
+    outer.b_y_to_z()
+    inner.a_z_to_x()
+    joint.a_y_to_core()
+    joint.b_x_to_core()
+    wait_all(token_in)
+    layer.start()
+    layer.rows_turned[...] = layer.rows[...].T
+    layer.clear_sums()
+    joint.done()
+    each(4, layer.project)
+    inner.a_x_to_y()
+
+    def attend(i):
+        layer.attend(i)
+        ticks(i, {
+            0: [(inner.b_z_to_x,)],
+            1: [(outer.a_z_to_x,)],
+            2: [(inner.a_y_to_core,), (inner.b_x_to_core,)],
+            3: [(outer.a_x_to_y,), (start_all, back_in)],
+        })
+
+    each(4, attend)
+    layer.norm_first()
+    layer.first_turned[...] = layer.first_low[...].T
+    inner.done()
+    outer.b_z_to_x()
+    each(4, layer.feed_inner)
+    outer.a_y_to_core()
+    outer.b_x_to_core()
+    outer.done()
+    each(4, layer.feed_outer)
+    wait_all(back_in)
+    layer.norm_second()
+    start_all(out_out)
+    local[5].start()
+    outer.sent()
+
+    def outer_back(i):
+        layer.outer_back(order(i))
+        ticks(i, {
+            0: [(to_outer.c[0].start,)],
+            1: [(to_outer.c[1].start,)],
+            2: [(to_outer.core_half, 0)],
+            3: [(to_outer.core_half, 1)],
+        })
+
+    each(4, outer_back)
+    inner.sent()
+
+    def inner_back(i):
+        layer.inner_back(order(i))
+        ticks(i, {
+            0: [(to_inner.c[0].start,)],
+            1: [(to_inner.c[1].start,)],
+            2: [(to_outer.a_y, 0), (to_inner.core_half, 0)],
+            3: [(to_inner.core_half, 1)],
+        })
+
+    each(4, inner_back)
+    to_outer.b_x(0)
+    layer.norm_first_back()
+    to_outer.a_y(1)
+    joint.sent()
+
+    def attend_back(i):
+        layer.attend_back(order(i))
+        ticks(i, {
+            0: [(to_outer.b_x, 1), (to_outer.a_x,)],
+            1: [(to_inner.b_x, 1), (to_inner.a_y, 1), (to_inner.a_x,)],
+            2: [(to_outer.b_y,), (to_inner.b_z,), (to_inner.a_z,)],
+            3: [(to_inner.b_y,)],
+        })
+        layer.joint_back(order(i))
+        ticks(i, {
+            0: [(to_joint.c[0].start,), (to_inner.a_y, 0), (to_inner.b_x, 0)],
+            1: [(to_joint.c[1].start,), (to_outer.b_z,), (to_outer.a_z,)],
+            2: [(to_joint.core_half, 0)],
+            3: [(to_joint.core_half, 1)],
+        })
+
+    each(4, attend_back)
+    wait_all(back_in[:0])
+    layer.finish()
+    start_all(back_out)
+    local[6].start()
+    totals[...] = layer.sums[...]
+    sums.start(0)
+    to_joint.a_y(0)
+    to_joint.b_x(0)
+    sums.finish(0)
+    sums.start(1)
+    to_joint.a_y(1)
+    to_joint.b_x(1)
+    sums.finish(1)
+    sums.start(2)
+    to_joint.a_x()
+    sums.finish(2)
+    sums.start(3)
+    to_joint.b_z()
+    to_joint.a_z()
+    sums.finish(3)
+    sums.rest(4)
+    to_joint.b_y()
+    for copy in local[5:]:
+        copy.wait()
+    wait_all(out_out + back_out)
+    for stage in (to_outer, to_inner, to_joint):
+        stage.sent()
+    sent_all(token_in + back_in + out_out + back_out)
+
+
+VMEM_SPEC = pl.BlockSpec(memory_space=pltpu.VMEM)
+ANY_SPEC = pl.BlockSpec(memory_space=pl.ANY)
+LIMIT = 67043328
+
+
+def whole_layer(own, tokens, cotangent, lengths, vectors):
+    nz = lax.axis_size(FSDP) // 2
+    part = WIDTH // (2 * nz)
+    seq = tokens.shape[1] * 4
+    steps = 3 + (nz - 1).bit_length()
+    count = 176
+    return pl.pallas_call(
+        partial(layer_kernel, nz),
+        out_shape=(
+            jax.ShapeDtypeStruct((KINDS, part, WIDTH), F32),
+            jax.ShapeDtypeStruct(tokens.shape, BF16),
+            jax.ShapeDtypeStruct(tokens.shape, BF16),
+            jax.ShapeDtypeStruct((VECTOR_ROWS, WIDTH), F32),
+        ),
+        in_specs=[ANY_SPEC, ANY_SPEC, ANY_SPEC, pl.BlockSpec(memory_space=pltpu.SMEM), VMEM_SPEC],
+        out_specs=(VMEM_SPEC, ANY_SPEC, ANY_SPEC, VMEM_SPEC),
+        scratch_shapes=buffer_shapes(nz, seq) + landing_shapes(nz) + [
+            pltpu.VMEM((steps, VECTOR_ROWS, WIDTH), F32),
+            pltpu.VMEM((steps, VECTOR_ROWS, WIDTH), F32),
+            pltpu.SemaphoreType.DMA((count,)),
+            pltpu.SemaphoreType.DMA((count,)),
+            pltpu.SemaphoreType.DMA((8,)),
+        ],
+        compiler_params=pltpu.CompilerParams(collective_id=0, has_side_effects=True, vmem_limit_bytes=LIMIT),
+        name="whole_layer",
+    )(own, tokens, cotangent, lengths, vectors)
+
+
+def pack_joint(q, k, v, o):
+    return jnp.concatenate(
+        [q[:, :128], k[:, :128], v[:, :128], v[:, 128:], q[:, 128:], o[:, :128], o[:, 128:], k[:, 128:]], axis=1
+    )
+
+
+def unpack_joint(joint):
+    q = jnp.concatenate([joint[:, 0:128], joint[:, 448:512]], axis=1)
+    k = jnp.concatenate([joint[:, 128:256], joint[:, 704:768]], axis=1)
+    return q, k, joint[:, 256:448], joint[:, 512:704]
+
+
+def local_fast(
+    tokens, lengths, cotangent, w_query, w_key, w_value, w_output, w_inner, w_outer,
+    b_query, b_value, b_output, b_inner, b_outer, gain_first, shift_first, gain_second, shift_second,
+):
+    tensor_rank = lax.axis_index(TENSOR)
+    rank = lax.axis_index(FSDP) * 4 + tensor_rank
+    own = jnp.stack([pack_joint(w_query, w_key, w_value, w_output.T), w_inner, w_outer.T])
+    size = b_query.shape[0]
+    zeros = jnp.zeros((VECTOR_ROWS, WIDTH), F32)
+    short = jnp.stack([b_output, b_outer, gain_first, shift_first, gain_second, shift_second])
+    placed = lax.dynamic_update_slice(zeros, short, (ROW_OUTPUT, rank * size))
+    start = rank * b_inner.shape[0]
+    placed = lax.dynamic_update_slice(placed, b_inner[None], (ROW_INNER + start // WIDTH, start % WIDTH))
+    start = rank * size
+    head_row, within = start // 192, start % 192
+    spot = jnp.arange(WIDTH)
+    query_spot = jnp.where(spot < 128, spot, jnp.where((spot >= 448) & (spot < 512), spot - 320, -1))
+    value_spot = jnp.where((spot >= 256) & (spot < 448), spot - 256, -1)
+
+    def spread(values, spots):
+        match = (spots[None, :] == within + jnp.arange(size)[:, None]).astype(F32)
+        return jnp.sum(match * values[:, None], axis=0)
+
+    joint_row = spread(b_query, query_spot) + spread(b_value, value_spot)
+    placed = lax.dynamic_update_slice(placed, joint_row[None], (head_row, 0))
+    sums, outs, backs, totals = whole_layer(own, tokens, cotangent, lengths, placed)
+    w_q, w_k, w_v, w_o = unpack_joint(sums[0])
+    short_own = lax.dynamic_slice(totals, (ROW_OUTPUT, rank * size), short.shape)
+    start = rank * b_inner.shape[0]
+    inner_own = lax.dynamic_slice(totals, (ROW_INNER + start // WIDTH, start % WIDTH), (1, b_inner.shape[0]))[0]
+    joint_own = lax.dynamic_index_in_dim(totals, head_row, keepdims=False)
+    bias_q = jnp.concatenate([joint_own[0:128], joint_own[448:512]])
+    query_own = lax.dynamic_slice(bias_q, (within,), (size,))
+    value_own = lax.dynamic_slice(joint_own, (256 + within,), (size,))
+    return (
+        outs,
+        backs.astype(F32),
+        w_q,
+        w_k,
+        w_v,
+        w_o.T,
+        sums[1],
+        sums[2].T,
+        query_own,
+        value_own,
+        short_own[0],
+        inner_own,
+        short_own[1],
+        short_own[2],
+        short_own[3],
+        short_own[4],
+        short_own[5],
+    )
+
+
 def solution(mesh):
     placed = (
-        P("fsdp", "tensor", None),
-        P("fsdp"),
-        P("fsdp", "tensor", None),
-        P("fsdp", "tensor"),
-        P("fsdp", "tensor"),
-        P("fsdp", "tensor"),
-        P("tensor", "fsdp"),
-        P("fsdp", "tensor"),
-        P("tensor", "fsdp"),
-        P(("fsdp", "tensor")),
-        P(("fsdp", "tensor")),
-        P(("fsdp", "tensor")),
-        P(("fsdp", "tensor")),
-        P(("fsdp", "tensor")),
-        P(("fsdp", "tensor")),
-        P(("fsdp", "tensor")),
-        P(("fsdp", "tensor")),
-        P(("fsdp", "tensor")),
+        P(FSDP, TENSOR, None),
+        P(FSDP),
+        P(FSDP, TENSOR, None),
+        P(FSDP, TENSOR),
+        P(FSDP, TENSOR),
+        P(FSDP, TENSOR),
+        P(TENSOR, FSDP),
+        P(FSDP, TENSOR),
+        P(TENSOR, FSDP),
+        P((FSDP, TENSOR)),
+        P((FSDP, TENSOR)),
+        P((FSDP, TENSOR)),
+        P((FSDP, TENSOR)),
+        P((FSDP, TENSOR)),
+        P((FSDP, TENSOR)),
+        P((FSDP, TENSOR)),
+        P((FSDP, TENSOR)),
+        P((FSDP, TENSOR)),
     )
     return jax.shard_map(
-        local,
+        local_fast if fits(mesh.shape) else local_generic,
         mesh=mesh,
         in_specs=placed,
         out_specs=(
-            P("fsdp", "tensor", None),
-            P("fsdp", "tensor", None),
-            P("fsdp", "tensor"),
-            P("fsdp", "tensor"),
-            P("fsdp", "tensor"),
-            P("tensor", "fsdp"),
-            P("fsdp", "tensor"),
-            P("tensor", "fsdp"),
-            P(("fsdp", "tensor")),
-            P(("fsdp", "tensor")),
-            P(("fsdp", "tensor")),
-            P(("fsdp", "tensor")),
-            P(("fsdp", "tensor")),
-            P(("fsdp", "tensor")),
-            P(("fsdp", "tensor")),
-            P(("fsdp", "tensor")),
-            P(("fsdp", "tensor")),
+            P(FSDP, TENSOR, None),
+            P(FSDP, TENSOR, None),
+            P(FSDP, TENSOR),
+            P(FSDP, TENSOR),
+            P(FSDP, TENSOR),
+            P(TENSOR, FSDP),
+            P(FSDP, TENSOR),
+            P(TENSOR, FSDP),
+            P((FSDP, TENSOR)),
+            P((FSDP, TENSOR)),
+            P((FSDP, TENSOR)),
+            P((FSDP, TENSOR)),
+            P((FSDP, TENSOR)),
+            P((FSDP, TENSOR)),
+            P((FSDP, TENSOR)),
+            P((FSDP, TENSOR)),
+            P((FSDP, TENSOR)),
         ),
         check_vma=False,
     )

time: 1140 us -> 221 us (0.19)
  waiting for transfers between devices: 539 us -> 0 us
  blocking collectives: 350 us -> 0 us
  Pallas kernels: 0 us -> 192 us
  matrix products: 124 us -> 0 us
  other arithmetic: 57.4 us -> 5.14 us
  local copies, waits for them, and re-layouts: 40.8 us -> 21.8 us
  between operations: 19.1 us -> 0.82 us
    reduce_scatter x18 -> x0, waiting for transfers between devices: 320 us -> none  [the longest x1 72.1 us: local(): lax.psum_scatter(pieces[5], 'fsdp', scatter_dimension=1, tiled=True)]
    all_gather x20 -> x0, blocking collectives: 267 us -> none  [the longest x4 36.1 us: local(): lax.all_gather(first.astype(jnp.bfloat16), 'tensor', axis=0, tiled=True)]
    unnamed x28 -> x0, waiting for transfers between devices: 197 us -> none
    pallas_call x0 -> x1, Pallas kernels: none -> 192 us  [whole_layer(): pl.pallas_call(partial(layer_kernel, nz), out_shape=(jax.ShapeDtypeStruct...]
    dot_general x68 -> x0, matrix products: 111 us -> none  [the longest x16 28.5 us: dot_back(): lax.dot_general(left, right, (((1,), (1,)), ((), ())), preferred_element_...]
    unnamed x2 -> x0, blocking collectives: 83.5 us -> none
    unnamed x510 -> x7, local copies, waits for them, and re-layouts: 37.6 us -> 2.51 us
    reduce_sum x25 -> x1, other arithmetic: 28.5 us -> 0.77 us  [spread(): return jnp.sum(match * values[:, None], axis=0)]
  transfers between devices with their start and end apart: 24 -> 0, of which waited for: 16 -> 0; matrix products, arithmetic and copies ran while one was open for 14% -> 0% of each run, Pallas kernels for 0% -> 0%
where the time goes in v1:
time: 221 us; the launch traced here: 220 us
  Pallas kernels  192 us (87%)
  local copies, waits for them, and re-layouts  21.8 us (10%)
  other arithmetic  5.14 us (2%)
    pallas_call x1, Pallas kernels, whole_layer(): pl.pallas_call(partial(layer_kernel, nz), out_shape=(jax.ShapeDtypeStruct...  192 us

profile of v1, /device:TPU:0, one launch (start us, length us, event | category | flops | bytes accessed | tf_op | source)
XLA Modules:
  0.0 219.9 jit_solution(2666548998442432640)
XLA Ops:
  0.8 0.8 stack.43
  1.5 0.8 select_reduce_fusion
  2.3 0.7 slice.77
  3.1 0.7 slice.75
  3.8 0.7 slice.78
  4.5 0.7 slice.76
  5.3 0.9 copy.37
  6.2 0.9 concatenate.13
  7.7 2.6 %dynamic_update_slice.9 = f32[16,768]{1,0:T(8,128)} dynamic-update-slice(f32[16,768]{1,0:T(8,128)} %broadcast_in_dim.9, f32[6,24]{1,0:T(8,128)S(1)} %stack.43, s32[]{:T(128)} %constant.71.clone.1, s32[]{:T(128)S(6)} %select_n.71) | dynamic-update-slice | bytes 1156 | tf_op jit(solution)/shard_map/dynamic_update_slice | solution.py:1119
  10.3 1.3 dynamic_update_slice.10
  11.6 1.4 dynamic_update_slice.11.refs_4_
  13.0 1.8 pad_maximum_fusion.refs_0_
  14.8 192.2 %whole_layer.1 = (f32[3,96,768]{2,1,0:T(8,128)}, bf16[4,128,768]{2,1,0:T(8,128)(2,1)}, bf16[4,128,768]{2,1,0:T(8,128)(2,1)}, f32[16,768]{1,0:T(8,128)}) custom-call(bf16[3,96,768]{2,1,0:T(8,128)(2,1)} %pad_maximum_fusion.refs_0_, bf16[4,128,768]{2,1,0:T(8,128)(2,1)} %refs_1_.1, bf16[4,128,768]{2,1,0:T(8,128)(2,1)} %refs_2_.1, s32[4]{0:T(128)} %refs_3_.1, ...), custom_call_target="tpu_custom_call" | custom-call | tf_op jit(solution)/shard_map/whole_layer/pallas_call | solution.py:1075
  207.0 1.3 dynamic-slice_bitcast_fusion.2
  208.3 1.3 dynamic-slice_bitcast_fusion.3
  209.5 0.7 dynamic-slice_bitcast_fusion
  210.3 0.7 dynamic-slice_bitcast_fusion.1
  211.5 0.8 constant_dynamic-slice_fusion
  212.9 2.1 slice_bitcast_fusion
  215.1 0.7 slice_bitcast_fusion.3
  215.7 0.7 copy.38
  216.5 0.6 pad_maximum_fusion.2
  217.8 1.3 convert_element_type.2
  219.0 0.9 copy.43
  (15 shorter events, 2.5 us)
Async XLA Ops:
  212.9 4.9 %copy-start.1 = (bf16[4,128,768]{2,1,0:T(8,128)(2,1)S(1)}, bf16[4,128,768]{2,1,0:T(8,128)(2,1)}, u32[]{:S(2)}) copy-start(bf16[4,128,768]{2,1,0:T(8,128)(2,1)} %get-tuple-element.22) | copy-start | bytes 2359300
  215.7 3.3 %copy-start = (bf16[4,128,768]{2,1,0:T(8,128)(2,1)S(1)}, bf16[4,128,768]{2,1,0:T(8,128)(2,1)}, u32[]{:S(2)}) copy-start(bf16[4,128,768]{2,1,0:T(8,128)(2,1)} %get-tuple-element.95) | copy-start | bytes 2359300

commit v2 on v1

--- a/solution.py
+++ b/solution.py
@@ -373,6 +373,7 @@
 HALF = WIDTH // 2
 KINDS = 3
 VECTOR_ROWS = 16
+SHORT, LONG = 24, 96
 ROW_OUTPUT, ROW_OUTER, ROW_GAIN1, ROW_SHIFT1, ROW_GAIN2, ROW_SHIFT2, ROW_INNER = 4, 5, 6, 7, 8, 9, 10
 BF16 = jnp.bfloat16
 F32 = jnp.float32
@@ -380,7 +381,7 @@
 
 def fits(sizes):
     fsdp = sizes[FSDP]
-    return sizes[TENSOR] == 4 and fsdp % 2 == 0 and WIDTH % (16 * fsdp) == 0
+    return sizes[TENSOR] == 4 and fsdp == WIDTH // LONG
 
 
 class Place:
@@ -455,38 +456,18 @@
         copy.wait_recv()
 
 
-def vector_peers(place):
-    peers = []
-    stride = 1
-    while stride < place.nz:
-        z = place.z
-        other = z + stride - 2 * stride * ((z // stride) % 2)
-        peers.append((other * 2 + place.x, place.t))
-        stride *= 2
-    peers.insert(1, place.core)
-    return peers + [place.along_x, place.along_y]
-
-
-class Exchange:
-    def __init__(self, net, place, total, slots):
-        self.total, self.slots = total, slots
-        self.copies = [net.plan(total, slots.at[i], peer) for i, peer in enumerate(vector_peers(place))]
-
-    def start(self, index):
-        self.copies[index].start()
-
-    def finish(self, index):
-        self.copies[index].wait()
-        self.total[...] += self.slots[index]
-
-    def rest(self, index):
-        for later in range(index, len(self.copies)):
-            self.start(later)
-            self.finish(later)
+def wait_local(copies):
+    for copy in copies:
+        copy.wait()
 
 
 def dot(left, right):
     return lax.dot_general(left, right, (((1,), (0,)), ((), ())), preferred_element_type=F32)
+
+
+def turn(value, shift):
+    shift %= value.shape[1]
+    return pltpu.roll(value, shift, 1) if shift else value
 
 
 class Layer:
@@ -542,6 +523,42 @@
 
     def head_value(self, t, h):
         return self.pick(self.joint[t, :, 256:512], h * 64, h * 64 + 64)
+
+    def unpack(self, v):
+        nz = v.shape[2]
+        short = jnp.zeros((8, WIDTH), F32)
+        inner = [jnp.zeros((1, WIDTH), F32) for _ in range(4)]
+        for f in range(2 * nz):
+            for t in range(4):
+                rank = f * 4 + t
+                block = v[t // 2, t % 2, f // 2, f % 2]
+                wide = jnp.concatenate([self.pick(block, 0, SHORT), jnp.zeros((8, WIDTH - 128), F32)], axis=1)
+                short += turn(wide, rank * SHORT)
+                wide = jnp.concatenate([self.pick(block[0:1], 32, 128), jnp.zeros((1, WIDTH - 128), F32)], axis=1)
+                inner[rank * LONG // WIDTH] += turn(wide, rank * LONG % WIDTH - 32)
+        for t in range(4):
+            query = self.pick(turn(short[0:1], -192 * t), 0, 128) + self.pick(turn(short[0:1], 320 - 192 * t), 448, 512)
+            self.vec[t:t + 1] = query + self.pick(turn(short[1:2], 256 - 192 * t), 256, 448)
+            self.vec[ROW_INNER + t:ROW_INNER + t + 1] = inner[t]
+        self.vec[ROW_OUTPUT:ROW_INNER] = short[2:8]
+
+    def pack(self, parts):
+        nz = parts.shape[2]
+        query, value = jnp.zeros((1, WIDTH), F32), jnp.zeros((1, WIDTH), F32)
+        for t in range(4):
+            row = self.sums[t:t + 1]
+            query += turn(self.pick(row, 0, 128), 192 * t) + turn(self.pick(row, 448, 512), 192 * t - 320)
+            value += turn(self.pick(row, 256, 448), 192 * t - 256)
+        short = jnp.concatenate([query, value, self.sums[ROW_OUTPUT:ROW_INNER]], axis=0)
+        top = lax.broadcasted_iota(jnp.int32, (8, 1), 0) == 0
+        for f in range(2 * nz):
+            for t in range(4):
+                rank = f * 4 + t
+                block = self.pick(turn(short, -rank * SHORT)[:, 0:128], 0, SHORT)
+                index = ROW_INNER + rank * LONG // WIDTH
+                inner = turn(self.sums[index:index + 1], 32 - rank * LONG % WIDTH)[:, 0:128]
+                inner = jnp.broadcast_to(self.pick(inner, 32, 128), (8, 128))
+                parts[t // 2, t % 2, f // 2, f % 2] = block + jnp.where(top, inner, 0.0)
 
     def project(self, t):
         self.joint[t] = (dot(self.rows[...], self.weight(0, t)) + self.row(t)).astype(BF16)
@@ -728,59 +745,80 @@
 
 
 class Gather:
-    def __init__(self, net, place, own, w, k):
+    def __init__(self, net, place, own, w, k, own_v=None, v=None):
         p = place
         a, b = pl.ds(0, HALF), pl.ds(HALF, HALF)
-        own_a, own_b = own.at[k, :, a], own.at[k, :, b]
+        own_a, own_b = own.at[:, a], own.at[:, b]
         mine_a, mine_b = (w.at[k, p.y, p.c, p.z, p.x, :, cols] for cols in (a, b))
         steps = range(1, p.nz)
+        backs = range(p.nz)
         self.az = [net.plan(own_a, mine_a, p.along_z(step)) for step in steps]
         self.by = [net.plan(own_b, mine_b, p.along_y)]
         self.ax = [net.plan(own_a, mine_a, p.along_x)]
         self.ax += [net.keep(w.at[k, p.y, p.c, p.z_back(step), p.x, :, a], p.along_x) for step in steps]
-        self.ay = [net.keep(w.at[k, p.y, p.c, :, x, :, a], p.along_y) for x in (p.x, 1 - p.x)]
+        self.ay = [net.plan(own_a, mine_a, p.along_y)]
+        self.ay += [net.keep(w.at[k, p.y, p.c, p.z_back(step), p.x, :, a], p.along_y) for step in steps]
+        self.ay += [net.keep(w.at[k, p.y, p.c, p.z_back(step), 1 - p.x, :, a], p.along_y) for step in backs]
         self.ac = [net.keep(w.at[k, y, p.c, :, :, :, a], p.core) for y in (p.y, 1 - p.y)]
         self.bz = [net.keep(w.at[k, :, p.c, p.z, p.x, :, b], p.along_z(step)) for step in steps]
-        self.bx = [net.keep(w.at[k, :, p.c, p.z_back(step), p.x, :, b], p.along_x) for step in range(p.nz)]
+        self.bx = [net.keep(w.at[k, :, p.c, p.z_back(step), p.x, :, b], p.along_x) for step in backs]
         self.bc = [net.keep(w.at[k, :, p.c, :, x, :, b], p.core) for x in (p.x, 1 - p.x)]
-
-    def b_y_to_z(self):
+        self.vz, self.vx, self.vy, self.vc = [], [], [], []
+        if v is not None:
+            mine = v.at[p.y, p.c, p.z, p.x]
+            self.vz = [net.plan(own_v, mine, p.along_z(step)) for step in steps]
+            self.vx = [net.plan(own_v, mine, p.along_x)]
+            self.vx += [net.keep(v.at[p.y, p.c, p.z_back(step), p.x], p.along_x) for step in steps]
+            self.vy = [net.keep(v.at[p.y, p.c], p.along_y)]
+            self.vc = [net.keep(v.at[y, p.c], p.core) for y in (p.y, 1 - p.y)]
+
+    def first(self):
+        start_all(self.by + self.vz + self.vx[:1] + self.az)
+        self.ax[0].start()
+        self.ay[0].start()
+
+    def b_y(self):
         wait_all(self.by)
         start_all(self.bz)
         self.bx[0].start()
 
-    def a_z_to_x(self):
-        for arrived, onward in zip(self.az, self.ax[1:]):
-            arrived.wait_recv()
-            onward.start()
-        self.ay[0].start()
-
-    def a_x_to_y(self):
-        wait_all(self.ax)
-        self.ay[1].start()
-        self.ac[0].start()
-
-    def b_z_to_x(self):
-        for arrived, onward in zip(self.bz, self.bx[1:]):
-            arrived.wait_recv()
-            onward.start()
+    def a_z(self, i):
+        if self.vz:
+            self.vz[i].wait_recv()
+            self.vx[i + 1].start()
+        self.az[i].wait_recv()
+        self.ax[i + 1].start()
+        self.ay[i + 1].start()
+
+    def a_x(self, i):
+        self.ax[i].wait_recv()
+        self.ay[len(self.ax) + i].start()
+
+    def a_own(self):
+        wait_all(self.vx)
+        start_all(self.vy + self.vc[:1] + self.ac[:1])
+
+    def a_y(self):
+        wait_all(self.vy + self.ay)
+        start_all(self.vc[1:] + self.ac[1:])
+
+    def b_z(self, i):
+        self.bz[i].wait_recv()
+        self.bx[i + 1].start()
+
+    def b_own(self):
         self.bc[0].start()
 
-    def a_y_to_core(self):
-        wait_all(self.ay)
-        self.ac[1].start()
-
-    def b_x_to_core(self):
+    def b_x(self):
         wait_all(self.bx)
         self.bc[1].start()
 
     def done(self):
-        wait_all(self.ac)
-        wait_all(self.bc)
+        wait_all(self.ac + self.bc + self.vc)
 
     def sent(self):
-        for copies in (self.az, self.ax, self.ay, self.ac, self.by, self.bz, self.bx, self.bc):
-            sent_all(copies)
+        sent_all(self.az + self.ax + self.ay + self.ac + self.by + self.bz + self.bx + self.bc)
+        sent_all(self.vz + self.vx + self.vy + self.vc)
 
 
 class Reduce:
@@ -793,7 +831,9 @@
         self.xs = xs = (1 - p.x, p.x)
         self.zs = zs = [p.z_at((step + 1) % p.nz) for step in range(p.nz)]
         self.c = [net.plan(self.w.at[y, 1 - p.c], self.core.at[y], p.core) for y in ys]
-        self.ay = [net.plan(self.core.at[ys[0], :, x, :, self.a], self.ya.at[:, x], p.along_y) for x in xs]
+        self.ay = [
+            [net.plan(self.core.at[ys[0], z, x, :, self.a], self.ya.at[z, x], p.along_y) for z in zs] for x in xs
+        ]
         self.bx = [
             [net.plan(self.core.at[y, z, xs[0], :, self.b], self.xb.at[y, z], p.along_x) for z in zs] for y in ys
         ]
@@ -807,6 +847,9 @@
     def add(self, target, source):
         target[...] = (target[...].astype(F32) + source[...].astype(F32)).astype(BF16)
 
+    def to_core(self, half):
+        self.c[half].start()
+
     def core_half(self, half):
         y = self.ys[half]
         self.c[half].wait_recv()
@@ -815,45 +858,40 @@
             self.add(self.core.at[y, z], self.w.at[y, self.place.c, z])
 
         each(self.place.nz, body)
+        start_all(self.bx[half])
         if half == 0:
-            start_all(self.ay)
-        start_all(self.bx[half])
-
-    def a_y(self, index):
-        self.ay[index].wait_recv()
-        x = self.xs[index]
-
-        def body(z):
-            self.add(self.ya.at[z, x], self.core.at[self.ys[1], z, x, :, self.a])
-
-        each(self.place.nz, body)
-        if index == 0:
-            start_all(self.ax)
-
-    def b_x(self, half):
+            start_all(self.ay[0] + self.ay[1])
+
+    def a_y(self, side, i):
+        self.ay[side][i].wait_recv()
+        z, x = self.zs[i], self.xs[side]
+        self.add(self.ya.at[z, x], self.core.at[self.ys[1], z, x, :, self.a])
+        if side == 0:
+            self.ax[i].start()
+
+    def b_x(self, half, i):
+        y, z = self.ys[half], self.zs[i]
+        self.bx[half][i].wait_recv()
+        self.add(self.xb.at[y, z], self.core.at[y, z, self.xs[1], :, self.b])
+        if i < self.place.nz - 1:
+            self.bz[half][i].start()
+
+    def a_x(self, i):
+        z = self.zs[i]
+        self.ax[i].wait_recv()
+        self.add(self.xa.at[z], self.ya.at[z, self.xs[1]])
+        if i < self.place.nz - 1:
+            self.az[i].start()
+
+    def b_z(self, half):
         y = self.ys[half]
-        for i, z in enumerate(self.zs):
-            self.bx[half][i].wait_recv()
-            self.add(self.xb.at[y, z], self.core.at[y, z, self.xs[1], :, self.b])
-            if i < self.place.nz - 1:
-                self.bz[half][i].start()
-
-    def a_x(self):
-        for i, z in enumerate(self.zs):
-            self.ax[i].wait_recv()
-            self.add(self.xa.at[z], self.ya.at[z, self.xs[1]])
-            if i < self.place.nz - 1:
-                self.az[i].start()
-
-    def b_z(self):
-        for half, y in enumerate(self.ys):
-            wait_all(self.bz[half])
-            total = self.xb[y, self.place.z].astype(F32)
-            for i in range(self.place.nz - 1):
-                total += self.zb[i, y].astype(F32)
-            self.yb[y] = total.astype(BF16)
-            if half == 0:
-                start_all(self.by)
+        wait_all(self.bz[half])
+        total = self.xb[y, self.place.z].astype(F32)
+        for i in range(self.place.nz - 1):
+            total += self.zb[i, y].astype(F32)
+        self.yb[y] = total.astype(BF16)
+        if half == 0:
+            start_all(self.by)
 
     def a_z(self):
         wait_all(self.az)
@@ -867,8 +905,49 @@
         self.result[:, self.b] = self.yb[self.ys[1]].astype(F32) + self.yb[2].astype(F32)
 
     def sent(self):
-        for copies in (self.c, self.ay, *self.bx, *self.bz, self.by, self.ax, self.az):
+        for copies in (self.c, *self.ay, *self.bx, *self.bz, self.by, self.ax, self.az):
             sent_all(copies)
+
+
+class Back:
+    def __init__(self, net, place, parts, landings, result):
+        p = self.place = place
+        self.parts, self.result = parts, result
+        self.core, self.side, self.pair, self.line = landings
+        self.c = net.plan(parts.at[:, 1 - p.c], self.core, p.core)
+        self.y = net.plan(self.core.at[1 - p.y], self.side, p.along_y)
+        self.x = net.plan(self.side.at[:, 1 - p.x], self.pair, p.along_x)
+        self.z = [
+            net.plan(self.pair.at[p.z_at(step)], self.line.at[step - 1], p.along_z(step)) for step in range(1, p.nz)
+        ]
+
+    def first(self):
+        self.c.start()
+
+    def core_done(self):
+        self.c.wait_recv()
+        self.core[...] += self.parts[:, self.place.c]
+        self.y.start()
+
+    def y_done(self):
+        self.y.wait_recv()
+        self.side[...] += self.core[self.place.y]
+        self.x.start()
+
+    def x_done(self):
+        self.x.wait_recv()
+        self.pair[...] += self.side[:, self.place.x]
+        start_all(self.z)
+
+    def z_done(self):
+        wait_all(self.z)
+        total = self.pair[self.place.z]
+        for i in range(self.place.nz - 1):
+            total += self.line[i]
+        self.result[...] = total
+
+    def sent(self):
+        sent_all([self.c, self.y, self.x] + self.z)
 
 
 def ticks(i, table):
@@ -880,16 +959,23 @@
 
 
 def layer_kernel(nz, *refs):
-    own, tokens, cotangent, lengths, vec_in, result, outs, backs, totals = refs[:9]
-    rest = list(refs[9:])
+    tokens, lengths, cotangent, w_query, w_key, w_value, w_output, w_inner, w_outer = refs[:9]
+    short_in, long_in = refs[9:12] + refs[13:18], refs[12]
+    result, outs, backs, totals = refs[18:22]
+    rest = list(refs[22:])
     buffers, rest = rest[:BUFFER_COUNT], rest[BUFFER_COUNT:]
-    landings, (slots, back_slots, send_sems, recv_sems, local_sems) = rest[:7], rest[7:]
+    landings, back_landings = rest[:7], rest[7:11]
+    v, parts, vec_in, raw_query, raw_key, raw_value, raw_output, own_joint = rest[11:19]
+    send_sems, recv_sems, local_sems = rest[19:]
     place = Place(nz)
     net = Net(send_sems, recv_sems)
     t = place.t
     quarter = tokens.shape[1]
     layer = Layer(buffers, lengths[t])
-    joint, inner, outer = [Gather(net, place, own, layer.w, k) for k in range(KINDS)]
+    joint = Gather(net, place, own_joint, layer.w, 0, vec_in, v)
+    inner = Gather(net, place, w_inner, layer.w, 1)
+    outer = Gather(net, place, w_outer, layer.w, 2)
+    sums = Back(net, place, parts, back_landings, totals)
     to_joint, to_inner, to_outer = [Reduce(net, place, layer.w, landings, result, k) for k in range(KINDS)]
 
     def quarter_of(ref, index):
@@ -909,155 +995,218 @@
     back_in = swap_in(cotangent, layer.back)
     out_out = swap_out(layer.out, outs)
     back_out = swap_out(layer.back, backs)
-    vec = Exchange(net, place, layer.vec, slots)
-    sums = Exchange(net, place, totals, back_slots)
     pairs = [
         (tokens.at[t], quarter_of(layer.rows, t)),
         (cotangent.at[t], quarter_of(layer.back, t)),
-        *[(own.at[k], layer.w.at[k, place.y, place.c, place.z, place.x]) for k in range(KINDS)],
+        *[
+            (own, layer.w.at[k, place.y, place.c, place.z, place.x])
+            for k, own in enumerate((own_joint, w_inner, w_outer))
+        ],
+        (vec_in, v.at[place.y, place.c, place.z, place.x]),
         (quarter_of(layer.out, t), outs.at[t]),
         (quarter_of(layer.back, t), backs.at[t]),
+        (w_query, raw_query),
+        (w_key, raw_key),
+        (w_value, raw_value),
+        (w_output, raw_output),
     ]
     local = [pltpu.make_async_copy(*pair, local_sems.at[i]) for i, pair in enumerate(pairs)]
 
+    def pack_vectors():
+        vec_in[...] = jnp.zeros((8, 128), F32)
+        for i, ref in enumerate(short_in):
+            vec_in[i:i + 1, 0:SHORT] = ref[...].reshape(1, SHORT)
+        vec_in[0:1, 32:128] = long_in[...].reshape(1, LONG)
+
+    def pack_own():
+        own_joint[...] = pack_joint(raw_query[...], raw_key[...], raw_value[...], raw_output[...].T)
+
     def order(i):
-        return (1 - place.y + i) % 2 * 2 + (1 - place.c + i // 2) % 2
-
-    layer.vec[...] = vec_in[...]
+        return (1 - place.y + i // 2) % 2 * 2 + (1 - place.c + i) % 2
+
+    start_all(local[8:])
+    pack_vectors()
     greet(place)
-    vec.start(0)
-    start_all(joint.by + inner.by + outer.by)
-    start_all(joint.az)
-    joint.ax[0].start()
+    wait_local(local[8:12])
+    pack_own()
+    joint.first()
+    start_all(local[0:6])
+    wait_local(local[0:6])
     start_all(token_in)
-    start_all(local[:5])
-    vec.finish(0)
-    vec.start(1)
-    vec.finish(1)
-    vec.start(2)
-    for copy in local[:5]:
-        copy.wait()
-    joint.b_y_to_z()
-    joint.a_z_to_x()
-    vec.finish(2)
-    vec.start(3)
-    start_all(inner.az)
-    inner.ax[0].start()
-    inner.b_y_to_z()
-    vec.finish(3)
-    vec.rest(4)
-    joint.a_x_to_y()
-    joint.b_z_to_x()
-    start_all(outer.az)
-    outer.ax[0].start()
-    outer.b_y_to_z()
-    inner.a_z_to_x()
-    joint.a_y_to_core()
-    joint.b_x_to_core()
+    joint.b_y()
+    joint.a_x(0)
+    inner.first()
+    joint.a_z(0)
+    inner.a_x(0)
+    joint.a_z(1)
+    joint.a_x(1)
+    joint.a_z(2)
     wait_all(token_in)
+    joint.a_x(2)
+    joint.a_x(3)
+    joint.a_own()
+    inner.b_y()
+    outer.first()
+    joint.b_z(0)
+    outer.a_x(0)
+    joint.b_z(1)
+    joint.b_z(2)
+    joint.b_own()
+    joint.a_y()
+    outer.b_y()
+    inner.a_z(0)
+    joint.b_x()
+    inner.a_z(1)
+    joint.done()
+    layer.unpack(v)
     layer.start()
     layer.rows_turned[...] = layer.rows[...].T
     layer.clear_sums()
-    joint.done()
-    each(4, layer.project)
-    inner.a_x_to_y()
-
+    def project(i):
+        layer.project(i)
+        ticks(i, {
+            0: [(inner.a_z, 2)],
+            1: [(inner.a_x, 1)],
+        })
+
+    each(4, project)
+    inner.a_x(2)
     def attend(i):
         layer.attend(i)
         ticks(i, {
-            0: [(inner.b_z_to_x,)],
-            1: [(outer.a_z_to_x,)],
-            2: [(inner.a_y_to_core,), (inner.b_x_to_core,)],
-            3: [(outer.a_x_to_y,), (start_all, back_in)],
+            0: [(inner.a_x, 3), (inner.a_own,)],
+            1: [(inner.b_z, 0)],
+            2: [(inner.a_y,)],
         })
 
     each(4, attend)
+    inner.b_z(1)
     layer.norm_first()
     layer.first_turned[...] = layer.first_low[...].T
+    inner.b_z(2)
+    inner.b_own()
+    outer.a_z(0)
+    outer.a_z(1)
+    inner.b_x()
+    outer.a_z(2)
+    outer.a_x(1)
     inner.done()
-    outer.b_z_to_x()
-    each(4, layer.feed_inner)
-    outer.a_y_to_core()
-    outer.b_x_to_core()
+    def feed_inner(i):
+        layer.feed_inner(i)
+        ticks(i, {
+            0: [(outer.a_x, 2), (outer.b_z, 0)],
+            1: [(outer.a_x, 3), (outer.a_own,), (start_all, back_in)],
+            2: [(outer.b_z, 1)],
+        })
+
+    each(4, feed_inner)
+    outer.a_y()
+    outer.b_z(2)
+    outer.b_own()
+    outer.b_x()
     outer.done()
-    each(4, layer.feed_outer)
+    def feed_outer(i):
+        layer.feed_outer(i)
+
+    each(4, feed_outer)
     wait_all(back_in)
     layer.norm_second()
     start_all(out_out)
-    local[5].start()
+    local[6].start()
     outer.sent()
-
     def outer_back(i):
         layer.outer_back(order(i))
         ticks(i, {
-            0: [(to_outer.c[0].start,)],
-            1: [(to_outer.c[1].start,)],
-            2: [(to_outer.core_half, 0)],
-            3: [(to_outer.core_half, 1)],
+            0: [(to_outer.to_core, 0)],
+            2: [(to_outer.to_core, 1), (to_outer.core_half, 0)],
         })
 
     each(4, outer_back)
     inner.sent()
-
     def inner_back(i):
         layer.inner_back(order(i))
         ticks(i, {
-            0: [(to_inner.c[0].start,)],
-            1: [(to_inner.c[1].start,)],
-            2: [(to_outer.a_y, 0), (to_inner.core_half, 0)],
-            3: [(to_inner.core_half, 1)],
+            0: [(to_inner.to_core, 0), (to_outer.core_half, 1), (to_outer.b_x, 0, 0)],
+            1: [(to_outer.b_x, 0, 1), (to_outer.a_y, 0, 0)],
+            2: [(to_inner.to_core, 1), (to_inner.core_half, 0), (to_outer.b_x, 0, 2), (to_outer.a_y, 0, 1), (to_outer.b_x, 0, 3)],
         })
 
     each(4, inner_back)
-    to_outer.b_x(0)
+    to_outer.a_y(0, 2)
+    to_outer.b_x(1, 0)
     layer.norm_first_back()
-    to_outer.a_y(1)
+    to_inner.core_half(1)
+    to_outer.a_y(0, 3)
+    to_outer.b_x(1, 1)
+    to_outer.a_y(1, 0)
     joint.sent()
-
     def attend_back(i):
         layer.attend_back(order(i))
         ticks(i, {
-            0: [(to_outer.b_x, 1), (to_outer.a_x,)],
-            1: [(to_inner.b_x, 1), (to_inner.a_y, 1), (to_inner.a_x,)],
-            2: [(to_outer.b_y,), (to_inner.b_z,), (to_inner.a_z,)],
-            3: [(to_inner.b_y,)],
+            0: [(to_outer.b_x, 1, 2), (to_outer.a_y, 1, 1), (to_outer.b_z, 0), (to_outer.b_x, 1, 3), (to_outer.a_y, 1, 2), (to_outer.a_x, 0)],
+            1: [(to_inner.a_y, 0, 0), (to_inner.b_x, 0, 1), (to_inner.a_y, 0, 1), (to_inner.b_x, 0, 2)],
+            2: [(to_outer.a_x, 1), (to_outer.a_x, 2), (to_inner.a_y, 0, 3), (to_inner.a_y, 1, 0)],
+            3: [(to_inner.a_y, 1, 2), (to_inner.b_x, 1, 1), (to_inner.b_z, 0), (to_inner.a_y, 1, 3), (to_inner.b_x, 1, 2)],
         })
         layer.joint_back(order(i))
         ticks(i, {
-            0: [(to_joint.c[0].start,), (to_inner.a_y, 0), (to_inner.b_x, 0)],
-            1: [(to_joint.c[1].start,), (to_outer.b_z,), (to_outer.a_z,)],
-            2: [(to_joint.core_half, 0)],
-            3: [(to_joint.core_half, 1)],
+            0: [(to_joint.to_core, 0), (to_outer.a_y, 1, 3), (to_inner.b_x, 0, 0)],
+            1: [(to_joint.core_half, 0), (to_outer.b_z, 1), (to_inner.a_y, 0, 2), (to_inner.b_x, 0, 3)],
+            2: [(to_joint.to_core, 1), (to_inner.a_y, 1, 1), (to_inner.b_x, 1, 0)],
         })
 
     each(4, attend_back)
-    wait_all(back_in[:0])
+    to_joint.core_half(1)
+    to_outer.b_y()
+    to_outer.a_x(3)
+    to_inner.b_x(1, 3)
+    to_joint.a_y(0, 0)
+    layer.pack(parts)
+    sums.first()
+    to_joint.a_y(0, 1)
     layer.finish()
     start_all(back_out)
-    local[6].start()
-    totals[...] = layer.sums[...]
-    sums.start(0)
-    to_joint.a_y(0)
-    to_joint.b_x(0)
-    sums.finish(0)
-    sums.start(1)
-    to_joint.a_y(1)
-    to_joint.b_x(1)
-    sums.finish(1)
-    sums.start(2)
-    to_joint.a_x()
-    sums.finish(2)
-    sums.start(3)
-    to_joint.b_z()
+    local[7].start()
+    to_inner.a_x(0)
+    sums.core_done()
+    to_outer.a_z()
+    to_outer.sent()
+    to_joint.a_y(0, 2)
+    to_inner.a_x(1)
+    to_joint.a_y(0, 3)
+    to_joint.b_x(0, 0)
+    to_joint.a_y(1, 0)
+    to_joint.b_x(0, 1)
+    to_joint.a_y(1, 1)
+    to_joint.b_x(0, 2)
+    to_joint.a_y(1, 2)
+    to_joint.b_x(0, 3)
+    to_inner.b_z(1)
+    to_joint.a_y(1, 3)
+    to_inner.a_x(2)
+    to_inner.b_y()
+    to_inner.a_x(3)
+    to_joint.b_x(1, 0)
+    to_joint.b_x(1, 1)
+    to_joint.b_x(1, 2)
+    to_joint.b_x(1, 3)
+    to_joint.a_x(0)
+    sums.y_done()
+    to_joint.a_x(1)
+    to_joint.b_z(0)
+    to_joint.a_x(2)
+    to_inner.a_z()
+    to_inner.sent()
+    to_joint.a_x(3)
+    sums.x_done()
+    to_joint.b_z(1)
+    to_joint.b_y()
     to_joint.a_z()
-    sums.finish(3)
-    sums.rest(4)
-    to_joint.b_y()
-    for copy in local[5:]:
-        copy.wait()
+    to_joint.sent()
+    sums.z_done()
+    sums.sent()
+    wait_local(local[6:8])
     wait_all(out_out + back_out)
-    for stage in (to_outer, to_inner, to_joint):
-        stage.sent()
     sent_all(token_in + back_in + out_out + back_out)
 
 
@@ -1066,32 +1215,67 @@
 LIMIT = 67043328
 
 
-def whole_layer(own, tokens, cotangent, lengths, vectors):
+def whole_layer(tokens, *rest):
     nz = lax.axis_size(FSDP) // 2
     part = WIDTH // (2 * nz)
     seq = tokens.shape[1] * 4
-    steps = 3 + (nz - 1).bit_length()
-    count = 176
+    count = 208
     return pl.pallas_call(
         partial(layer_kernel, nz),
         out_shape=(
             jax.ShapeDtypeStruct((KINDS, part, WIDTH), F32),
             jax.ShapeDtypeStruct(tokens.shape, BF16),
             jax.ShapeDtypeStruct(tokens.shape, BF16),
-            jax.ShapeDtypeStruct((VECTOR_ROWS, WIDTH), F32),
+            jax.ShapeDtypeStruct((8, 128), F32),
         ),
-        in_specs=[ANY_SPEC, ANY_SPEC, ANY_SPEC, pl.BlockSpec(memory_space=pltpu.SMEM), VMEM_SPEC],
+        in_specs=[ANY_SPEC, pl.BlockSpec(memory_space=pltpu.SMEM)] + [ANY_SPEC] * 7 + [VMEM_SPEC] * 9,
         out_specs=(VMEM_SPEC, ANY_SPEC, ANY_SPEC, VMEM_SPEC),
         scratch_shapes=buffer_shapes(nz, seq) + landing_shapes(nz) + [
-            pltpu.VMEM((steps, VECTOR_ROWS, WIDTH), F32),
-            pltpu.VMEM((steps, VECTOR_ROWS, WIDTH), F32),
+            pltpu.VMEM((2, nz, 2, 8, 128), F32),
+            pltpu.VMEM((nz, 2, 8, 128), F32),
+            pltpu.VMEM((nz, 8, 128), F32),
+            pltpu.VMEM((nz - 1, 8, 128), F32),
+            pltpu.VMEM((2, 2, nz, 2, 8, 128), F32),
+            pltpu.VMEM((2, 2, nz, 2, 8, 128), F32),
+            pltpu.VMEM((8, 128), F32),
+            *[pltpu.VMEM((part, WIDTH // 4), BF16)] * 3,
+            pltpu.VMEM((WIDTH // 4, part), BF16),
+            pltpu.VMEM((part, WIDTH), BF16),
             pltpu.SemaphoreType.DMA((count,)),
             pltpu.SemaphoreType.DMA((count,)),
-            pltpu.SemaphoreType.DMA((8,)),
+            pltpu.SemaphoreType.DMA((16,)),
         ],
         compiler_params=pltpu.CompilerParams(collective_id=0, has_side_effects=True, vmem_limit_bytes=LIMIT),
         name="whole_layer",
-    )(own, tokens, cotangent, lengths, vectors)
+    )(tokens, *rest)
+
+
+def finish_kernel(sums, outs, backs, totals, *results):
+    output, input_grad, g_query, g_key, g_value, g_output, g_inner, g_outer = results[:8]
+    output[...] = outs[...]
+    input_grad[...] = backs[...].astype(F32)
+    g_query[...], g_key[...], g_value[...], g_turned = unpack_joint(sums[0])
+    g_output[...] = g_turned.T
+    g_inner[...] = sums[1]
+    g_outer[...] = sums[2]
+    short = [0, 1, 2, None, 3, 4, 5, 6, 7]
+    for row, ref in zip(short, results[8:]):
+        ref[...] = (totals[0:1, 32:128] if row is None else totals[row:row + 1, 0:SHORT]).reshape(ref.shape)
+
+
+def finish_layer(sums, outs, backs, totals):
+    part = sums.shape[1]
+    share = WIDTH // 4
+    shapes = [outs.shape, backs.shape] + [(part, share)] * 3 + [(share, part), (part, WIDTH), (part, WIDTH)]
+    shapes += [(SHORT,)] * 3 + [(LONG,)] + [(SHORT,)] * 5
+    return pl.pallas_call(
+        finish_kernel,
+        out_shape=[jax.ShapeDtypeStruct(shape, F32 if i else BF16) for i, shape in enumerate(shapes)],
+        in_specs=[VMEM_SPEC] * 4,
+        out_specs=[VMEM_SPEC] * len(shapes),
+        compiler_params=pltpu.CompilerParams(vmem_limit_bytes=LIMIT // 2),
+        name="finish_layer",
+    )(sums, outs, backs, totals)
 
 
 def pack_joint(q, k, v, o):
@@ -1106,59 +1290,10 @@
     return q, k, joint[:, 256:448], joint[:, 512:704]
 
 
-def local_fast(
-    tokens, lengths, cotangent, w_query, w_key, w_value, w_output, w_inner, w_outer,
-    b_query, b_value, b_output, b_inner, b_outer, gain_first, shift_first, gain_second, shift_second,
-):
-    tensor_rank = lax.axis_index(TENSOR)
-    rank = lax.axis_index(FSDP) * 4 + tensor_rank
-    own = jnp.stack([pack_joint(w_query, w_key, w_value, w_output.T), w_inner, w_outer.T])
-    size = b_query.shape[0]
-    zeros = jnp.zeros((VECTOR_ROWS, WIDTH), F32)
-    short = jnp.stack([b_output, b_outer, gain_first, shift_first, gain_second, shift_second])
-    placed = lax.dynamic_update_slice(zeros, short, (ROW_OUTPUT, rank * size))
-    start = rank * b_inner.shape[0]
-    placed = lax.dynamic_update_slice(placed, b_inner[None], (ROW_INNER + start // WIDTH, start % WIDTH))
-    start = rank * size
-    head_row, within = start // 192, start % 192
-    spot = jnp.arange(WIDTH)
-    query_spot = jnp.where(spot < 128, spot, jnp.where((spot >= 448) & (spot < 512), spot - 320, -1))
-    value_spot = jnp.where((spot >= 256) & (spot < 448), spot - 256, -1)
-
-    def spread(values, spots):
-        match = (spots[None, :] == within + jnp.arange(size)[:, None]).astype(F32)
-        return jnp.sum(match * values[:, None], axis=0)
-
-    joint_row = spread(b_query, query_spot) + spread(b_value, value_spot)
-    placed = lax.dynamic_update_slice(placed, joint_row[None], (head_row, 0))
-    sums, outs, backs, totals = whole_layer(own, tokens, cotangent, lengths, placed)
-    w_q, w_k, w_v, w_o = unpack_joint(sums[0])
-    short_own = lax.dynamic_slice(totals, (ROW_OUTPUT, rank * size), short.shape)
-    start = rank * b_inner.shape[0]
-    inner_own = lax.dynamic_slice(totals, (ROW_INNER + start // WIDTH, start % WIDTH), (1, b_inner.shape[0]))[0]
-    joint_own = lax.dynamic_index_in_dim(totals, head_row, keepdims=False)
-    bias_q = jnp.concatenate([joint_own[0:128], joint_own[448:512]])
-    query_own = lax.dynamic_slice(bias_q, (within,), (size,))
-    value_own = lax.dynamic_slice(joint_own, (256 + within,), (size,))
-    return (
-        outs,
-        backs.astype(F32),
-        w_q,
-        w_k,
-        w_v,
-        w_o.T,
-        sums[1],
-        sums[2].T,
-        query_own,
-        value_own,
-        short_own[0],
-        inner_own,
-        short_own[1],
-        short_own[2],
-        short_own[3],
-        short_own[4],
-        short_own[5],
-    )
+def local_fast(*given):
+    given = given[:8] + (given[8].T,) + given[9:]
+    results = finish_layer(*whole_layer(*given))
+    return (*results[:7], results[7].T, *results[8:])
 
 
 def solution(mesh):

time: 221 us -> 173 us (0.78)
  Pallas kernels: 192 us -> 167 us
  local copies, waits for them, and re-layouts: 21.8 us -> 4.1 us
  other arithmetic: 5.14 us -> 0 us
    pallas_call x1, Pallas kernels: 192 us -> 166 us  [whole_layer(): pl.pallas_call(partial(layer_kernel, nz), out_shape=(jax.ShapeDtypeStruct...]
    dynamic_update_slice x3 -> x0, local copies, waits for them, and re-layouts: 5.27 us -> none  [the longest x1 2.57 us: local_fast(): placed = lax.dynamic_update_slice(zeros, short, (ROW_OUTPUT, rank * size))]
    slice x8 -> x0, local copies, waits for them, and re-layouts: 4.46 us -> none  [the longest x2 1.41 us: local_fast(): bias_q = jnp.concatenate([joint_own[0:128], joint_own[448:512]])]
    transpose x2 -> x0, local copies, waits for them, and re-layouts: 2.74 us -> none  [the longest x1 2.08 us: local_fast(): sums[2]]
    dynamic_slice x3 -> x0, local copies, waits for them, and re-layouts: 2.65 us -> none  [the longest x1 1.28 us: local_fast(): value_own = lax.dynamic_slice(joint_own, (256 + within,), (size,))]
where the time goes in v2:
time: 173 us; the launch traced here: 172 us
  Pallas kernels  167 us (97%)
  local copies, waits for them, and re-layouts  4.1 us (2%)
    pallas_call x1, Pallas kernels, whole_layer(): pl.pallas_call(partial(layer_kernel, nz), out_shape=(jax.ShapeDtypeStruct...  166 us
    unnamed x8, local copies, waits for them, and re-layouts  4.1 us

profile of v2, /device:TPU:0, one launch (start us, length us, event | category | flops | bytes accessed | tf_op | source)
XLA Modules:
  0.0 172.4 jit_solution(9204117199262225514)
XLA Ops:
  0.7 165.6 %whole_layer.1 = (f32[3,96,768]{2,1,0:T(8,128)}, bf16[4,128,768]{2,1,0:T(8,128)(2,1)}, bf16[4,128,768]{2,1,0:T(8,128)(2,1)}, f32[8,128]{1,0:T(8,128)}) custom-call(bf16[4,128,768]{2,1,0:T(8,128)(2,1)} %refs_0_.1, s32[4]{0:T(128)} %refs_1_.1, bf16[4,128,768]{2,1,0:T(8,128)(2,1)} %refs_2_.1, bf16[96,192]{1,0:T(8,128)(2,1)} %refs_3_.1, ...), custom_call_target="tpu_custom_call" | custom-call | tf_op jit(solution)/shard_map/whole_layer/pallas_call | solution.py:1223
  166.2 0.0 copy-start
  166.3 1.2 copy-done
  167.4 0.0 copy-start.1
  167.4 1.1 copy-done.1
  168.6 0.0 copy-start.2
  168.6 1.1 copy-done.2
  169.7 0.0 copy-start.3
  169.7 0.7 copy-done.3
  170.4 1.9 %finish_layer.1 = (bf16[4,128,768]{2,1,0:T(8,128)(2,1)}, f32[4,128,768]{2,1,0:T(8,128)}, f32[96,192]{1,0:T(8,128)}, f32[96,192]{1,0:T(8,128)}, f32[96,192]{1,0:T...) custom-call(f32[3,96,768]{2,1,0:T(8,128)S(1)} %copy-done, ...), custom_call_target="tpu_custom_call" | custom-call | tf_op jit(solution)/shard_map/finish_layer/pallas_call | solution.py:1271
Async XLA Ops:
  166.2 1.2 copy-start
  167.4 1.1 copy-start.1
  168.6 1.1 copy-start.2
  169.7 0.7 copy-start.3

commit v3 on v2

--- a/solution.py
+++ b/solution.py
@@ -372,6 +372,14 @@
 HIDDEN = 3072
 HALF = WIDTH // 2
 KINDS = 3
+FLOWS = (
+    (0, 0, 384, "zyx", "yxz"),
+    (0, 384, 384, "zyx", "xzy"),
+    (1, 0, 512, "zxy", "yxz"),
+    (1, 512, 256, "zyx", "xyz"),
+    (2, 0, 384, "zxy", "yxz"),
+    (2, 384, 384, "yzx", "xzy"),
+)
 VECTOR_ROWS = 16
 SHORT, LONG = 24, 96
 ROW_OUTPUT, ROW_OUTER, ROW_GAIN1, ROW_SHIFT1, ROW_GAIN2, ROW_SHIFT2, ROW_INNER = 4, 5, 6, 7, 8, 9, 10
@@ -410,36 +418,66 @@
         return (self.f, (self.t + step) % 4)
 
 
+class Trip:
+    def __init__(self, copy, send_sem, recv_sem):
+        self.copy, self.send_sem, self.recv_sem = copy, send_sem, recv_sem
+
+    def start(self):
+        self.copy.start()
+
+    def wait_recv(self):
+        self.copy.wait_recv()
+
+
 class Net:
     def __init__(self, send_sems, recv_sems):
-        self.send_sems = send_sems
-        self.recv_sems = recv_sems
-        self.count = 0
-
-    def plan(self, source, target, device):
+        self.send_sems, self.recv_sems = send_sems, recv_sems
+        self.sends = self.recvs = 0
+
+    def lane(self):
+        self.sends += 1
+        return self.send_sems.at[self.sends - 1]
+
+    def door(self):
+        self.recvs += 1
+        return self.recv_sems.at[self.recvs - 1]
+
+    def plan(self, source, target, device, lane, door=None):
+        door = self.door() if door is None else door
         copy = pltpu.make_async_remote_copy(
-            src_ref=source,
-            dst_ref=target,
-            send_sem=self.send_sems.at[self.count],
-            recv_sem=self.recv_sems.at[self.count],
-            device_id=device,
-            device_id_type=MESH,
+            src_ref=source, dst_ref=target, send_sem=lane, recv_sem=door, device_id=device, device_id_type=MESH
         )
-        self.count += 1
-        return copy
-
-    def keep(self, ref, device):
-        return self.plan(ref, ref, device)
+        return Trip(copy, lane, door)
+
+    def keep(self, ref, device, lane, door=None):
+        return self.plan(ref, ref, device, lane, door)
+
+
+class Meter:
+    def __init__(self, low, wide):
+        self.low, self.wide = low, wide
+
+    def low_rows(self, rows):
+        for count in (1, 2, 3, 4):
+            if rows % (16 * count) == 0 and rows // count <= self.low.shape[1]:
+                return self.low.at[0:count, 0:rows // count]
+        raise ValueError(rows)
+
+    def tiles(self, count):
+        return self.wide.at[0:8 * count]
+
+
+def arrived(trips, size):
+    pltpu.make_async_copy(size, size, trips[0].recv_sem).wait()
+
+
+def departed(trips, size):
+    pltpu.make_async_copy(size, size, trips[0].send_sem).wait()
 
 
 def start_all(copies):
     for copy in copies:
         copy.start()
-
-
-def sent_all(copies):
-    for copy in copies:
-        copy.wait_send()
 
 
 def greet(place):
@@ -449,11 +487,6 @@
     for peer in peers:
         pl.semaphore_signal(barrier, inc=1, device_id=peer, device_id_type=MESH)
     pl.semaphore_wait(barrier, len(peers))
-
-
-def wait_all(copies):
-    for copy in copies:
-        copy.wait_recv()
 
 
 def wait_local(copies):
@@ -730,195 +763,157 @@
     return [pltpu.VMEM(*shape) for shape in shapes]
 
 
-def landing_shapes(nz):
+BLOCKS = 15
+SEND_COUNT = 15
+DOOR_COUNT = 197
+
+
+def flow_shapes(nz):
     part = WIDTH // (2 * nz)
-    shapes = [
-        (KINDS, 2, nz, 2, part, WIDTH),
-        (KINDS, nz, 2, part, HALF),
-        (KINDS, nz, part, HALF),
-        (KINDS, nz - 1, part, HALF),
-        (KINDS, 2, nz, part, HALF),
-        (KINDS, nz - 1, 2, part, HALF),
-        (KINDS, 3, part, HALF),
-    ]
-    return [pltpu.VMEM(shape, BF16) for shape in shapes]
-
-
-class Gather:
-    def __init__(self, net, place, own, w, k, own_v=None, v=None):
+    shapes = [pltpu.VMEM((KINDS, 2, nz, 2, part, WIDTH), BF16)]
+    return shapes + [pltpu.VMEM((BLOCKS, part, flow[2]), BF16) for flow in FLOWS]
+
+
+def axis_steps(place, axis):
+    p = place
+    if axis == "x":
+        return [(1, 1 - p.x, p.along_x, 1 - p.x)]
+    if axis == "y":
+        return [(1, 1 - p.y, p.along_y, 1 - p.y)]
+    return [(step, p.z_at(step), p.along_z(step), p.z_back(step)) for step in range(1, p.nz)]
+
+
+class Flow:
+    def __init__(self, net, place, order, own, region, lane, core_lane, core_door):
         p = place
-        a, b = pl.ds(0, HALF), pl.ds(HALF, HALF)
-        own_a, own_b = own.at[:, a], own.at[:, b]
-        mine_a, mine_b = (w.at[k, p.y, p.c, p.z, p.x, :, cols] for cols in (a, b))
-        steps = range(1, p.nz)
-        backs = range(p.nz)
-        self.az = [net.plan(own_a, mine_a, p.along_z(step)) for step in steps]
-        self.by = [net.plan(own_b, mine_b, p.along_y)]
-        self.ax = [net.plan(own_a, mine_a, p.along_x)]
-        self.ax += [net.keep(w.at[k, p.y, p.c, p.z_back(step), p.x, :, a], p.along_x) for step in steps]
-        self.ay = [net.plan(own_a, mine_a, p.along_y)]
-        self.ay += [net.keep(w.at[k, p.y, p.c, p.z_back(step), p.x, :, a], p.along_y) for step in steps]
-        self.ay += [net.keep(w.at[k, p.y, p.c, p.z_back(step), 1 - p.x, :, a], p.along_y) for step in backs]
-        self.ac = [net.keep(w.at[k, y, p.c, :, :, :, a], p.core) for y in (p.y, 1 - p.y)]
-        self.bz = [net.keep(w.at[k, :, p.c, p.z, p.x, :, b], p.along_z(step)) for step in steps]
-        self.bx = [net.keep(w.at[k, :, p.c, p.z_back(step), p.x, :, b], p.along_x) for step in backs]
-        self.bc = [net.keep(w.at[k, :, p.c, :, x, :, b], p.core) for x in (p.x, 1 - p.x)]
-        self.vz, self.vx, self.vy, self.vc = [], [], [], []
-        if v is not None:
-            mine = v.at[p.y, p.c, p.z, p.x]
-            self.vz = [net.plan(own_v, mine, p.along_z(step)) for step in steps]
-            self.vx = [net.plan(own_v, mine, p.along_x)]
-            self.vx += [net.keep(v.at[p.y, p.c, p.z_back(step), p.x], p.along_x) for step in steps]
-            self.vy = [net.keep(v.at[p.y, p.c], p.along_y)]
-            self.vc = [net.keep(v.at[y, p.c], p.core) for y in (p.y, 1 - p.y)]
+        self.pieces = [(None, [])]
+        spots = [({"x": p.x, "y": p.y, "z": p.z}, own)]
+        for axis in order:
+            for index, (spot, source) in enumerate(list(spots)):
+                for _, _, device, behind in axis_steps(p, axis):
+                    trip = net.plan(region(spot) if source is None else source, region(spot), device, lane)
+                    self.pieces[index][1].append(trip)
+                    self.pieces.append((trip, []))
+                    spots.append(({**spot, axis: behind}, None))
+        mine = {"x": p.x, "y": p.y, "z": p.z}[order[2]]
+        sides = [mine] + [behind for _, _, _, behind in axis_steps(p, order[2])]
+        every = slice(None)
+        self.cores = [
+            net.keep(region({"x": every, "y": every, "z": every, order[2]: side}), p.core, core_lane, core_door)
+            for side in sides
+        ]
+        self.trips = [trip for _, onward in self.pieces for trip in onward]
 
     def first(self):
-        start_all(self.by + self.vz + self.vx[:1] + self.az)
-        self.ax[0].start()
-        self.ay[0].start()
-
-    def b_y(self):
-        wait_all(self.by)
-        start_all(self.bz)
-        self.bx[0].start()
-
-    def a_z(self, i):
-        if self.vz:
-            self.vz[i].wait_recv()
-            self.vx[i + 1].start()
-        self.az[i].wait_recv()
-        self.ax[i + 1].start()
-        self.ay[i + 1].start()
-
-    def a_x(self, i):
-        self.ax[i].wait_recv()
-        self.ay[len(self.ax) + i].start()
-
-    def a_own(self):
-        wait_all(self.vx)
-        start_all(self.vy + self.vc[:1] + self.ac[:1])
-
-    def a_y(self):
-        wait_all(self.vy + self.ay)
-        start_all(self.vc[1:] + self.ac[1:])
-
-    def b_z(self, i):
-        self.bz[i].wait_recv()
-        self.bx[i + 1].start()
-
-    def b_own(self):
-        self.bc[0].start()
-
-    def b_x(self):
-        wait_all(self.bx)
-        self.bc[1].start()
-
-    def done(self):
-        wait_all(self.ac + self.bc + self.vc)
-
-    def sent(self):
-        sent_all(self.az + self.ax + self.ay + self.ac + self.by + self.bz + self.bx + self.bc)
-        sent_all(self.vz + self.vx + self.vy + self.vc)
-
-
-class Reduce:
-    def __init__(self, net, place, w, landings, result, k):
-        p = self.place = place
-        self.core, self.ya, self.xa, self.za, self.xb, self.zb, self.yb = (ref.at[k] for ref in landings)
-        self.w, self.result = w.at[k], result.at[k]
-        self.a, self.b = pl.ds(0, HALF), pl.ds(HALF, HALF)
-        self.ys = ys = (1 - p.y, p.y)
-        self.xs = xs = (1 - p.x, p.x)
-        self.zs = zs = [p.z_at((step + 1) % p.nz) for step in range(p.nz)]
-        self.c = [net.plan(self.w.at[y, 1 - p.c], self.core.at[y], p.core) for y in ys]
-        self.ay = [
-            [net.plan(self.core.at[ys[0], z, x, :, self.a], self.ya.at[z, x], p.along_y) for z in zs] for x in xs
-        ]
-        self.bx = [
-            [net.plan(self.core.at[y, z, xs[0], :, self.b], self.xb.at[y, z], p.along_x) for z in zs] for y in ys
-        ]
-        self.bz = [
-            [net.plan(self.xb.at[y, zs[i]], self.zb.at[i, y], p.along_z(i + 1)) for i in range(p.nz - 1)] for y in ys
-        ]
-        self.by = [net.plan(self.yb.at[ys[0]], self.yb.at[2], p.along_y)]
-        self.ax = [net.plan(self.ya.at[z, xs[0]], self.xa.at[z], p.along_x) for z in zs]
-        self.az = [net.plan(self.xa.at[zs[i]], self.za.at[i], p.along_z(i + 1)) for i in range(p.nz - 1)]
-
-    def add(self, target, source):
-        target[...] = (target[...].astype(F32) + source[...].astype(F32)).astype(BF16)
+        start_all(self.pieces[0][1])
+
+    def piece(self, index):
+        trip, onward = self.pieces[index]
+        trip.wait_recv()
+        start_all(onward)
+
+    def to_core(self, index):
+        self.cores[index].start()
+
+
+class Cores:
+    def __init__(self, net, place, w, core, k):
+        self.place = place
+        self.w, self.core = w.at[k], core.at[k]
+        self.ys = (1 - place.y, place.y)
+        lane = net.lane()
+        self.c = [net.plan(self.w.at[y, 1 - place.c], self.core.at[y], place.core, lane) for y in self.ys]
 
     def to_core(self, half):
         self.c[half].start()
 
-    def core_half(self, half):
+    def half(self, half):
         y = self.ys[half]
         self.c[half].wait_recv()
 
         def body(z):
-            self.add(self.core.at[y, z], self.w.at[y, self.place.c, z])
+            target, source = self.core.at[y, z], self.w.at[y, self.place.c, z]
+            target[...] = (target[...].astype(F32) + source[...].astype(F32)).astype(BF16)
 
         each(self.place.nz, body)
-        start_all(self.bx[half])
-        if half == 0:
-            start_all(self.ay[0] + self.ay[1])
-
-    def a_y(self, side, i):
-        self.ay[side][i].wait_recv()
-        z, x = self.zs[i], self.xs[side]
-        self.add(self.ya.at[z, x], self.core.at[self.ys[1], z, x, :, self.a])
-        if side == 0:
-            self.ax[i].start()
-
-    def b_x(self, half, i):
-        y, z = self.ys[half], self.zs[i]
-        self.bx[half][i].wait_recv()
-        self.add(self.xb.at[y, z], self.core.at[y, z, self.xs[1], :, self.b])
-        if i < self.place.nz - 1:
-            self.bz[half][i].start()
-
-    def a_x(self, i):
-        z = self.zs[i]
-        self.ax[i].wait_recv()
-        self.add(self.xa.at[z], self.ya.at[z, self.xs[1]])
-        if i < self.place.nz - 1:
-            self.az[i].start()
-
-    def b_z(self, half):
-        y = self.ys[half]
-        wait_all(self.bz[half])
-        total = self.xb[y, self.place.z].astype(F32)
-        for i in range(self.place.nz - 1):
-            total += self.zb[i, y].astype(F32)
-        self.yb[y] = total.astype(BF16)
-        if half == 0:
-            start_all(self.by)
-
-    def a_z(self):
-        wait_all(self.az)
-        total = self.xa[self.place.z].astype(F32)
-        for i in range(self.place.nz - 1):
-            total += self.za[i].astype(F32)
-        self.result[:, self.a] = total
-
-    def b_y(self):
-        wait_all(self.by)
-        self.result[:, self.b] = self.yb[self.ys[1]].astype(F32) + self.yb[2].astype(F32)
-
-    def sent(self):
-        for copies in (self.c, *self.ay, *self.bx, *self.bz, self.by, self.ax, self.az):
-            sent_all(copies)
+
+
+class Sink:
+    def __init__(self, net, place, order, core, landing, result, cols, lane, meter):
+        p = place
+        self.meter = meter
+        self.core, self.landing, self.result, self.cols = core, landing, result, cols
+        here = {"x": p.x, "y": p.y, "z": p.z}
+        ahead = {axis: {0: here[axis], **{step: spot for step, spot, _, _ in axis_steps(p, axis)}} for axis in here}
+        sizes = {"x": 2, "y": 2, "z": p.nz}
+        self.spot = lambda block: tuple(ahead[axis][block[axis]] for axis in ("y", "z", "x"))
+        self.order = order
+        self.tasks = []
+        self.starts = ([], [])
+        blocks = [{}]
+        for axis in ("y", "z", "x"):
+            steps = [i for i in range(1, sizes[axis])] + [0]
+            blocks = [{**block, axis: step} for block in blocks for step in steps]
+        slot = 0
+        self.trips = []
+        waits = {}
+        for stage, axis in enumerate(order):
+            later = order[stage + 1:]
+            kept = [block for block in blocks if block[axis] == 0]
+            kept.sort(key=lambda block: [block[other] == 0 for other in later])
+            devices = {step: device for step, _, device, _ in axis_steps(p, axis)}
+            for block in kept:
+                arrivals = []
+                door = net.door()
+                for step in range(1, sizes[axis]):
+                    away = {**block, axis: step}
+                    copy = net.plan(self.part(away), landing.at[slot], devices[step], lane, door)
+                    self.trips.append(copy)
+                    if stage == 0:
+                        self.starts[0 if away["y"] else 1].append(copy)
+                    else:
+                        waits[tuple(sorted(away.items()))].append(copy)
+                    arrivals.append((copy, slot))
+                    slot += 1
+                onward = []
+                waits[tuple(sorted(block.items()))] = onward
+                self.tasks.append((block, arrivals, onward))
+            blocks = kept
+
+    def part(self, block):
+        return self.core.at[(*self.spot(block), slice(None), self.cols)]
+
+    def start(self, half):
+        start_all(self.starts[half])
+
+    def add(self, index):
+        block, arrivals, onward = self.tasks[index]
+        target = self.part(block)
+        total = target[...].astype(F32)
+        rows = self.landing.shape[1] * self.landing.shape[2] // WIDTH
+        arrived([trip for trip, _ in arrivals], self.meter.low_rows(rows * len(arrivals)))
+        for _, slot in arrivals:
+            total += self.landing[slot].astype(F32)
+        if index < len(self.tasks) - 1:
+            target[...] = total.astype(BF16)
+            start_all(onward)
+        else:
+            self.result[:, self.cols] = total
 
 
 class Back:
-    def __init__(self, net, place, parts, landings, result):
+    def __init__(self, net, place, parts, landings, result, meter):
         p = self.place = place
-        self.parts, self.result = parts, result
+        self.parts, self.result, self.meter = parts, result, meter
         self.core, self.side, self.pair, self.line = landings
-        self.c = net.plan(parts.at[:, 1 - p.c], self.core, p.core)
-        self.y = net.plan(self.core.at[1 - p.y], self.side, p.along_y)
-        self.x = net.plan(self.side.at[:, 1 - p.x], self.pair, p.along_x)
+        lane = net.lane()
+        self.c = net.plan(parts.at[:, 1 - p.c], self.core, p.core, lane)
+        self.y = net.plan(self.core.at[1 - p.y], self.side, p.along_y, lane)
+        self.x = net.plan(self.side.at[:, 1 - p.x], self.pair, p.along_x, lane)
+        door = net.door()
         self.z = [
-            net.plan(self.pair.at[p.z_at(step)], self.line.at[step - 1], p.along_z(step)) for step in range(1, p.nz)
+            net.plan(self.pair.at[p.z_at(step)], self.line.at[step - 1], p.along_z(step), lane, door)
+            for step in range(1, p.nz)
         ]
 
     def first(self):
@@ -940,14 +935,14 @@
         start_all(self.z)
 
     def z_done(self):
-        wait_all(self.z)
+        arrived(self.z, self.meter.tiles(len(self.z)))
         total = self.pair[self.place.z]
         for i in range(self.place.nz - 1):
             total += self.line[i]
         self.result[...] = total
 
     def sent(self):
-        sent_all([self.c, self.y, self.x] + self.z)
+        departed([self.c, self.y, self.x] + self.z, self.meter.tiles(8 * self.place.nz - 1))
 
 
 def ticks(i, table):
@@ -964,43 +959,91 @@
     result, outs, backs, totals = refs[18:22]
     rest = list(refs[22:])
     buffers, rest = rest[:BUFFER_COUNT], rest[BUFFER_COUNT:]
-    landings, back_landings = rest[:7], rest[7:11]
-    v, parts, vec_in, raw_query, raw_key, raw_value, raw_output, own_joint = rest[11:19]
-    send_sems, recv_sems, local_sems = rest[19:]
+    core_landing, landings, rest = rest[0], rest[1:1 + len(FLOWS)], rest[1 + len(FLOWS):]
+    back_landings = rest[:4]
+    v, parts, vec_in, raw_query, raw_key, raw_value, raw_output, own_joint = rest[4:12]
+    raw_short, raw_long = rest[12:20], rest[20]
+    send_sems, recv_sems, local_sems = rest[21:]
     place = Place(nz)
     net = Net(send_sems, recv_sems)
     t = place.t
     quarter = tokens.shape[1]
     layer = Layer(buffers, lengths[t])
-    joint = Gather(net, place, own_joint, layer.w, 0, vec_in, v)
-    inner = Gather(net, place, w_inner, layer.w, 1)
-    outer = Gather(net, place, w_outer, layer.w, 2)
-    sums = Back(net, place, parts, back_landings, totals)
-    to_joint, to_inner, to_outer = [Reduce(net, place, layer.w, landings, result, k) for k in range(KINDS)]
+    owns = (own_joint, w_inner, w_outer)
+    g, r = [], []
+    meter = Meter(layer.joint, layer.factor)
+    cores = [Cores(net, place, layer.w, core_landing, k) for k in range(KINDS)]
+    lanes = [[net.lane() for k in range(KINDS)] for _ in range(3)]
+    doors = [net.door() for k in range(KINDS)]
+    for (k, first, width, order_in, order_out), landing in zip(FLOWS, landings):
+        cols = pl.ds(first, width)
+
+        def region(spot, k=k, cols=cols):
+            return layer.w.at[k, spot["y"], place.c, spot["z"], spot["x"], :, cols]
+
+        g.append(Flow(net, place, order_in, owns[k].at[:, cols], region, lanes[0][k], lanes[1][k], doors[k]))
+        sink = (core_landing.at[k], landing, result.at[k], cols, lanes[2][k], meter)
+        r.append(Sink(net, place, order_out, *sink))
+    one = net.lane()
+    vecs = Flow(
+        net, place, FLOWS[0][3], vec_in, lambda spot: v.at[spot["y"], place.c, spot["z"], spot["x"]],
+        one, one, net.door(),
+    )
+    sums = Back(net, place, parts, back_landings, totals, meter)
+
+    def of_kind(flows, k):
+        return [flow for flow, row in zip(flows, FLOWS) if row[0] == k]
+
+    def trips_of(flows):
+        return [trip for flow in flows for trip in flow.trips]
+
+    def cores_of(flows):
+        return [trip for flow in flows for trip in flow.cores]
+
+    def gathered(k):
+        arrived(cores_of(of_kind(g, k)), meter.low_rows(2 * WIDTH))
+
+    def passed_on(k):
+        flows = of_kind(g, k)
+        departed(trips_of(flows), meter.low_rows(2 * WIDTH - own_joint.shape[0]))
+        departed(cores_of(flows), meter.low_rows(2 * WIDTH))
+
+    def reduced(k):
+        departed(trips_of(of_kind(r, k)), meter.low_rows(2 * WIDTH - own_joint.shape[0]))
+        departed(cores[k].c, meter.low_rows(2 * WIDTH))
+
+    def vectors_in():
+        arrived(vecs.cores, meter.tiles(4 * nz))
+
+    def vectors_sent():
+        departed(vecs.trips + vecs.cores, meter.tiles(8 * nz - 1))
 
     def quarter_of(ref, index):
         return ref.at[pl.ds(pl.multiple_of(index * quarter, quarter), quarter)]
 
-    def swap_in(source, target):
-        return [
-            net.plan(source.at[(t + step) % 4], quarter_of(target, t), place.in_group(step)) for step in (2, 1, 3)
-        ]
-
-    def swap_out(source, target):
-        return [
-            net.plan(quarter_of(source, (t + step) % 4), target.at[t], place.in_group(step)) for step in (2, 1, 3)
-        ]
-
-    token_in = swap_in(tokens, layer.rows)
-    back_in = swap_in(cotangent, layer.back)
-    out_out = swap_out(layer.out, outs)
-    back_out = swap_out(layer.back, backs)
+    swap_lane = net.lane()
+
+    def swap(source, target):
+        door = net.door()
+        return [net.plan(source(step), target, place.in_group(step), swap_lane, door) for step in (2, 1, 3)]
+
+    def swapped(trips):
+        arrived(trips, meter.low_rows(3 * quarter))
+
+    token_in = swap(lambda step: tokens.at[(t + step) % 4], quarter_of(layer.rows, t))
+    back_in = swap(lambda step: cotangent.at[(t + step) % 4], quarter_of(layer.back, t))
+    out_out = swap(lambda step: quarter_of(layer.out, (t + step) % 4), outs.at[t])
+    back_out = swap(lambda step: quarter_of(layer.back, (t + step) % 4), backs.at[t])
+
+    def swaps_sent():
+        departed(token_in + back_in + out_out + back_out, meter.low_rows(12 * quarter))
+
     pairs = [
         (tokens.at[t], quarter_of(layer.rows, t)),
         (cotangent.at[t], quarter_of(layer.back, t)),
         *[
             (own, layer.w.at[k, place.y, place.c, place.z, place.x])
-            for k, own in enumerate((own_joint, w_inner, w_outer))
+            for k, own in enumerate(owns)
         ],
         (vec_in, v.at[place.y, place.c, place.z, place.x]),
         (quarter_of(layer.out, t), outs.at[t]),
@@ -1009,205 +1052,277 @@
         (w_key, raw_key),
         (w_value, raw_value),
         (w_output, raw_output),
+        *zip(short_in, raw_short),
+        (long_in, raw_long),
     ]
     local = [pltpu.make_async_copy(*pair, local_sems.at[i]) for i, pair in enumerate(pairs)]
 
     def pack_vectors():
         vec_in[...] = jnp.zeros((8, 128), F32)
-        for i, ref in enumerate(short_in):
+        for i, ref in enumerate(raw_short):
             vec_in[i:i + 1, 0:SHORT] = ref[...].reshape(1, SHORT)
-        vec_in[0:1, 32:128] = long_in[...].reshape(1, LONG)
+        vec_in[0:1, 32:128] = raw_long[...].reshape(1, LONG)
 
     def pack_own():
         own_joint[...] = pack_joint(raw_query[...], raw_key[...], raw_value[...], raw_output[...].T)
 
+    def near(i):
+        return (place.y + i) % 2 * 2 + (place.c + i // 2) % 2
+
     def order(i):
         return (1 - place.y + i // 2) % 2 * 2 + (1 - place.c + i) % 2
 
     start_all(local[8:])
+    greet(place)
+    wait_local(local[8:])
     pack_vectors()
-    greet(place)
-    wait_local(local[8:12])
     pack_own()
-    joint.first()
-    start_all(local[0:6])
-    wait_local(local[0:6])
+    vecs.first()
+    g[0].first()
+    start_all(local[:6])
+    wait_local(local[:6])
+    g[1].first()
     start_all(token_in)
-    joint.b_y()
-    joint.a_x(0)
-    inner.first()
-    joint.a_z(0)
-    inner.a_x(0)
-    joint.a_z(1)
-    joint.a_x(1)
-    joint.a_z(2)
-    wait_all(token_in)
-    joint.a_x(2)
-    joint.a_x(3)
-    joint.a_own()
-    inner.b_y()
-    outer.first()
-    joint.b_z(0)
-    outer.a_x(0)
-    joint.b_z(1)
-    joint.b_z(2)
-    joint.b_own()
-    joint.a_y()
-    outer.b_y()
-    inner.a_z(0)
-    joint.b_x()
-    inner.a_z(1)
-    joint.done()
+    g[2].first()
+    g[3].first()
+    g[4].first()
+    g[5].first()
+    vecs.piece(4)
+    vecs.piece(8)
+    vecs.piece(2)
+    g[0].piece(4)
+    vecs.piece(1)
+    vecs.piece(3)
+    g[0].piece(8)
+    g[1].piece(4)
+    g[1].piece(8)
+    g[2].piece(4)
+    g[3].piece(8)
+    g[0].piece(1)
+    g[4].piece(4)
+    g[0].piece(2)
+    g[5].piece(8)
+    vecs.piece(12)
+    vecs.piece(10)
+    g[0].piece(3)
+    g[0].piece(12)
+    vecs.piece(9)
+    vecs.piece(11)
+    swapped(token_in)
+    g[1].piece(12)
+    g[2].piece(8)
+    g[0].piece(9)
+    g[3].piece(4)
+    g[1].piece(1)
+    g[0].piece(10)
+    g[4].piece(8)
+    g[1].piece(2)
+    vecs.piece(6)
+    vecs.piece(5)
+    vecs.piece(7)
+    vecs.to_core(0)
+    g[0].piece(11)
+    g[5].piece(1)
+    g[1].piece(3)
+    g[3].piece(12)
+    g[2].piece(12)
+    g[1].piece(9)
+    g[0].piece(5)
+    vecs.piece(14)
+    vecs.piece(13)
+    vecs.piece(15)
+    vecs.to_core(1)
+    g[1].piece(10)
+    vectors_in()
+    g[4].piece(12)
     layer.unpack(v)
     layer.start()
     layer.rows_turned[...] = layer.rows[...].T
     layer.clear_sums()
+    g[0].piece(6)
+    g[2].piece(1)
+    g[5].piece(9)
+    g[1].piece(11)
+    g[0].piece(7)
+    g[0].to_core(0)
+    g[0].piece(13)
+    g[2].piece(2)
+    g[1].piece(5)
+    g[0].piece(14)
+    g[2].piece(3)
+    g[1].piece(6)
+    g[2].piece(5)
+    g[1].piece(7)
+    g[1].to_core(0)
+    g[0].piece(15)
+    g[0].to_core(1)
+    g[3].piece(1)
+    g[2].piece(9)
+    g[2].piece(6)
+    g[3].piece(2)
+    g[3].piece(3)
+    g[2].piece(10)
+    g[1].piece(13)
+    g[2].piece(11)
+    g[2].piece(7)
+    g[2].to_core(0)
+    g[4].piece(1)
+    g[1].piece(14)
+    g[2].piece(13)
+    g[3].piece(5)
+    g[1].piece(15)
+    g[1].to_core(1)
     def project(i):
-        layer.project(i)
+        layer.project(near(i))
         ticks(i, {
-            0: [(inner.a_z, 2)],
-            1: [(inner.a_x, 1)],
+            0: [(g[3].piece, 9), (g[4].piece, 2)],
+            1: [(g[2].piece, 14), (g[3].piece, 10), (g[4].piece, 3), (gathered, 0)],
+            2: [(g[3].piece, 6), (g[3].piece, 11)],
         })
 
     each(4, project)
-    inner.a_x(2)
+    g[3].piece(7)
+    g[3].to_core(0)
     def attend(i):
         layer.attend(i)
         ticks(i, {
-            0: [(inner.a_x, 3), (inner.a_own,)],
-            1: [(inner.b_z, 0)],
-            2: [(inner.a_y,)],
+            0: [(g[3].piece, 13), (g[2].piece, 15), (g[2].to_core, 1), (g[5].piece, 2), (g[4].piece, 5), (g[5].piece, 3), (g[5].piece, 4)],
+            1: [(g[4].piece, 6), (g[4].piece, 9)],
+            2: [(g[3].piece, 14), (g[4].piece, 7), (g[4].to_core, 0), (g[4].piece, 10), (g[5].piece, 5), (g[5].piece, 6), (g[4].piece, 11), (g[5].piece, 7), (g[3].piece, 15), (g[3].to_core, 1), (g[5].to_core, 0), (start_all, back_in)],
         })
 
     each(4, attend)
-    inner.b_z(1)
+    g[4].piece(13)
+    g[5].piece(10)
     layer.norm_first()
     layer.first_turned[...] = layer.first_low[...].T
-    inner.b_z(2)
-    inner.b_own()
-    outer.a_z(0)
-    outer.a_z(1)
-    inner.b_x()
-    outer.a_z(2)
-    outer.a_x(1)
-    inner.done()
+    g[4].piece(14)
+    g[5].piece(11)
     def feed_inner(i):
-        layer.feed_inner(i)
+        layer.feed_inner(near(i))
         ticks(i, {
-            0: [(outer.a_x, 2), (outer.b_z, 0)],
-            1: [(outer.a_x, 3), (outer.a_own,), (start_all, back_in)],
-            2: [(outer.b_z, 1)],
+            0: [(g[4].piece, 15), (g[4].to_core, 1)],
+            1: [(g[5].piece, 12), (gathered, 1)],
+            2: [(g[5].piece, 13)],
         })
 
     each(4, feed_inner)
-    outer.a_y()
-    outer.b_z(2)
-    outer.b_own()
-    outer.b_x()
-    outer.done()
+    g[5].piece(14)
+    g[5].piece(15)
+    g[5].to_core(1)
     def feed_outer(i):
-        layer.feed_outer(i)
+        layer.feed_outer(near(i))
+        ticks(i, {
+            1: [(gathered, 2)],
+        })
 
     each(4, feed_outer)
-    wait_all(back_in)
+    swapped(back_in)
     layer.norm_second()
     start_all(out_out)
     local[6].start()
-    outer.sent()
+    passed_on(2)
     def outer_back(i):
         layer.outer_back(order(i))
         ticks(i, {
-            0: [(to_outer.to_core, 0)],
-            2: [(to_outer.to_core, 1), (to_outer.core_half, 0)],
+            0: [(cores[2].to_core, 0)],
+            2: [(cores[2].to_core, 1), (cores[2].half, 0), (r[4].start, 0), (r[5].start, 0)],
         })
 
     each(4, outer_back)
-    inner.sent()
+    passed_on(1)
     def inner_back(i):
         layer.inner_back(order(i))
         ticks(i, {
-            0: [(to_inner.to_core, 0), (to_outer.core_half, 1), (to_outer.b_x, 0, 0)],
-            1: [(to_outer.b_x, 0, 1), (to_outer.a_y, 0, 0)],
-            2: [(to_inner.to_core, 1), (to_inner.core_half, 0), (to_outer.b_x, 0, 2), (to_outer.a_y, 0, 1), (to_outer.b_x, 0, 3)],
+            0: [(cores[1].to_core, 0), (cores[2].half, 1), (r[4].start, 1), (r[5].start, 1), (r[5].add, 0)],
+            1: [(r[5].add, 1), (r[4].add, 0)],
+            2: [(cores[1].to_core, 1), (cores[1].half, 0), (r[3].start, 0), (r[2].start, 0), (r[5].add, 2), (r[4].add, 1), (r[5].add, 6)],
         })
 
     each(4, inner_back)
-    to_outer.a_y(0, 2)
-    to_outer.b_x(1, 0)
+    r[4].add(2)
+    r[5].add(3)
     layer.norm_first_back()
-    to_inner.core_half(1)
-    to_outer.a_y(0, 3)
-    to_outer.b_x(1, 1)
-    to_outer.a_y(1, 0)
-    joint.sent()
+    cores[1].half(1)
+    r[3].start(1)
+    r[2].start(1)
+    r[4].add(3)
+    r[5].add(4)
+    r[4].add(4)
+    vectors_sent()
+    passed_on(0)
     def attend_back(i):
         layer.attend_back(order(i))
         ticks(i, {
-            0: [(to_outer.b_x, 1, 2), (to_outer.a_y, 1, 1), (to_outer.b_z, 0), (to_outer.b_x, 1, 3), (to_outer.a_y, 1, 2), (to_outer.a_x, 0)],
-            1: [(to_inner.a_y, 0, 0), (to_inner.b_x, 0, 1), (to_inner.a_y, 0, 1), (to_inner.b_x, 0, 2)],
-            2: [(to_outer.a_x, 1), (to_outer.a_x, 2), (to_inner.a_y, 0, 3), (to_inner.a_y, 1, 0)],
-            3: [(to_inner.a_y, 1, 2), (to_inner.b_x, 1, 1), (to_inner.b_z, 0), (to_inner.a_y, 1, 3), (to_inner.b_x, 1, 2)],
+            0: [(r[5].add, 5), (r[4].add, 5), (r[5].add, 8), (r[5].add, 7), (r[4].add, 6), (r[4].add, 8)],
+            1: [(r[3].add, 1), (r[3].add, 2), (r[2].add, 0), (r[3].add, 3)],
+            2: [(r[4].add, 10), (r[2].add, 2), (r[3].add, 4), (r[3].add, 5), (r[2].add, 3), (r[3].add, 6)],
+            3: [(r[4].add, 11), (r[2].add, 5), (r[4].add, 12), (r[2].add, 8)],
         })
         layer.joint_back(order(i))
         ticks(i, {
-            0: [(to_joint.to_core, 0), (to_outer.a_y, 1, 3), (to_inner.b_x, 0, 0)],
-            1: [(to_joint.core_half, 0), (to_outer.b_z, 1), (to_inner.a_y, 0, 2), (to_inner.b_x, 0, 3)],
-            2: [(to_joint.to_core, 1), (to_inner.a_y, 1, 1), (to_inner.b_x, 1, 0)],
+            0: [(cores[0].to_core, 0), (r[3].add, 0), (r[4].add, 7)],
+            1: [(cores[0].half, 0), (r[0].start, 0), (r[1].start, 0), (r[5].add, 9), (r[2].add, 1), (r[4].add, 9)],
+            2: [(cores[0].to_core, 1), (r[3].add, 7), (r[2].add, 4)],
         })
 
     each(4, attend_back)
-    to_joint.core_half(1)
-    to_outer.b_y()
-    to_outer.a_x(3)
-    to_inner.b_x(1, 3)
-    to_joint.a_y(0, 0)
+    cores[0].half(1)
+    r[0].start(1)
+    r[1].start(1)
+    r[1].add(0)
+    r[2].add(6)
     layer.pack(parts)
     sums.first()
-    to_joint.a_y(0, 1)
+    r[1].add(1)
+    r[2].add(7)
     layer.finish()
     start_all(back_out)
     local[7].start()
-    to_inner.a_x(0)
     sums.core_done()
-    to_outer.a_z()
-    to_outer.sent()
-    to_joint.a_y(0, 2)
-    to_inner.a_x(1)
-    to_joint.a_y(0, 3)
-    to_joint.b_x(0, 0)
-    to_joint.a_y(1, 0)
-    to_joint.b_x(0, 1)
-    to_joint.a_y(1, 1)
-    to_joint.b_x(0, 2)
-    to_joint.a_y(1, 2)
-    to_joint.b_x(0, 3)
-    to_inner.b_z(1)
-    to_joint.a_y(1, 3)
-    to_inner.a_x(2)
-    to_inner.b_y()
-    to_inner.a_x(3)
-    to_joint.b_x(1, 0)
-    to_joint.b_x(1, 1)
-    to_joint.b_x(1, 2)
-    to_joint.b_x(1, 3)
-    to_joint.a_x(0)
+    r[5].add(10)
+    reduced(2)
+    r[1].add(2)
+    r[3].add(8)
+    r[1].add(6)
+    r[3].add(9)
+    r[3].add(10)
+    r[2].add(9)
+    r[3].add(11)
+    r[0].add(0)
+    r[2].add(10)
+    r[0].add(1)
+    r[2].add(11)
+    r[0].add(2)
+    r[1].add(8)
+    r[1].add(3)
+    r[0].add(3)
+    r[1].add(4)
+    r[0].add(4)
+    r[1].add(5)
+    r[0].add(5)
+    r[3].add(12)
+    r[1].add(7)
+    r[0].add(6)
+    r[0].add(8)
+    r[0].add(7)
+    r[0].add(9)
+    r[0].add(10)
+    r[0].add(11)
+    r[2].add(12)
+    reduced(1)
     sums.y_done()
-    to_joint.a_x(1)
-    to_joint.b_z(0)
-    to_joint.a_x(2)
-    to_inner.a_z()
-    to_inner.sent()
-    to_joint.a_x(3)
+    r[1].add(9)
     sums.x_done()
-    to_joint.b_z(1)
-    to_joint.b_y()
-    to_joint.a_z()
-    to_joint.sent()
+    r[1].add(10)
+    r[0].add(12)
     sums.z_done()
+    reduced(0)
     sums.sent()
     wait_local(local[6:8])
-    wait_all(out_out + back_out)
-    sent_all(token_in + back_in + out_out + back_out)
+    swapped(out_out)
+    swapped(back_out)
+    swaps_sent()
 
 
 VMEM_SPEC = pl.BlockSpec(memory_space=pltpu.VMEM)
@@ -1219,7 +1334,6 @@
     nz = lax.axis_size(FSDP) // 2
     part = WIDTH // (2 * nz)
     seq = tokens.shape[1] * 4
-    count = 208
     return pl.pallas_call(
         partial(layer_kernel, nz),
         out_shape=(
@@ -1228,9 +1342,9 @@
             jax.ShapeDtypeStruct(tokens.shape, BF16),
             jax.ShapeDtypeStruct((8, 128), F32),
         ),
-        in_specs=[ANY_SPEC, pl.BlockSpec(memory_space=pltpu.SMEM)] + [ANY_SPEC] * 7 + [VMEM_SPEC] * 9,
+        in_specs=[ANY_SPEC, pl.BlockSpec(memory_space=pltpu.SMEM)] + [ANY_SPEC] * 16,
         out_specs=(VMEM_SPEC, ANY_SPEC, ANY_SPEC, VMEM_SPEC),
-        scratch_shapes=buffer_shapes(nz, seq) + landing_shapes(nz) + [
+        scratch_shapes=buffer_shapes(nz, seq) + flow_shapes(nz) + [
             pltpu.VMEM((2, nz, 2, 8, 128), F32),
             pltpu.VMEM((nz, 2, 8, 128), F32),
             pltpu.VMEM((nz, 8, 128), F32),
@@ -1241,26 +1355,42 @@
             *[pltpu.VMEM((part, WIDTH // 4), BF16)] * 3,
             pltpu.VMEM((WIDTH // 4, part), BF16),
             pltpu.VMEM((part, WIDTH), BF16),
-            pltpu.SemaphoreType.DMA((count,)),
-            pltpu.SemaphoreType.DMA((count,)),
-            pltpu.SemaphoreType.DMA((16,)),
+            *[pltpu.VMEM((SHORT,), F32)] * 8,
+            pltpu.VMEM((LONG,), F32),
+            pltpu.SemaphoreType.DMA((SEND_COUNT,)),
+            pltpu.SemaphoreType.DMA((DOOR_COUNT,)),
+            pltpu.SemaphoreType.DMA((24,)),
         ],
         compiler_params=pltpu.CompilerParams(collective_id=0, has_side_effects=True, vmem_limit_bytes=LIMIT),
         name="whole_layer",
     )(tokens, *rest)
 
 
-def finish_kernel(sums, outs, backs, totals, *results):
-    output, input_grad, g_query, g_key, g_value, g_output, g_inner, g_outer = results[:8]
-    output[...] = outs[...]
+def finish_kernel(count, *refs):
+    given, results, rest = refs[:4], refs[4:4 + count], refs[4 + count:]
+    (sums, outs, backs, totals), made, (sems, sent) = rest[:4], rest[4:-2], rest[-2:]
+    arrivals = [pltpu.make_async_copy(ref, spot, sems.at[i]) for i, (ref, spot) in enumerate(zip(given, rest))]
+    start_all(arrivals)
+    input_grad, g_query, g_key, g_value, g_output, g_inner, g_outer = made[:7]
+    copies = [pltpu.make_async_copy(outs, results[0], sent.at[0])]
+    copies += [pltpu.make_async_copy(*pair, sent.at[i + 1]) for i, pair in enumerate(zip(made, results[1:]))]
+    arrivals[2].wait()
     input_grad[...] = backs[...].astype(F32)
+    copies[1].start()
+    arrivals[1].wait()
+    copies[0].start()
+    arrivals[0].wait()
+    g_inner[...] = sums[1]
+    g_outer[...] = sums[2]
     g_query[...], g_key[...], g_value[...], g_turned = unpack_joint(sums[0])
     g_output[...] = g_turned.T
-    g_inner[...] = sums[1]
-    g_outer[...] = sums[2]
+    start_all(copies[2:8])
+    arrivals[3].wait()
     short = [0, 1, 2, None, 3, 4, 5, 6, 7]
-    for row, ref in zip(short, results[8:]):
+    for row, ref in zip(short, made[7:]):
         ref[...] = (totals[0:1, 32:128] if row is None else totals[row:row + 1, 0:SHORT]).reshape(ref.shape)
+    start_all(copies[8:])
+    wait_local(copies)
 
 
 def finish_layer(sums, outs, backs, totals):
@@ -1268,14 +1398,18 @@
     share = WIDTH // 4
     shapes = [outs.shape, backs.shape] + [(part, share)] * 3 + [(share, part), (part, WIDTH), (part, WIDTH)]
     shapes += [(SHORT,)] * 3 + [(LONG,)] + [(SHORT,)] * 5
+    given = (sums, outs, backs, totals)
     return pl.pallas_call(
-        finish_kernel,
+        partial(finish_kernel, len(shapes)),
         out_shape=[jax.ShapeDtypeStruct(shape, F32 if i else BF16) for i, shape in enumerate(shapes)],
-        in_specs=[VMEM_SPEC] * 4,
-        out_specs=[VMEM_SPEC] * len(shapes),
-        compiler_params=pltpu.CompilerParams(vmem_limit_bytes=LIMIT // 2),
+        in_specs=[ANY_SPEC] * 4,
+        out_specs=[ANY_SPEC] * len(shapes),
+        scratch_shapes=[pltpu.VMEM(ref.shape, ref.dtype) for ref in given]
+        + [pltpu.VMEM(shape, F32) for shape in shapes[1:]]
+        + [pltpu.SemaphoreType.DMA((4,)), pltpu.SemaphoreType.DMA((len(shapes),))],
+        compiler_params=pltpu.CompilerParams(vmem_limit_bytes=LIMIT),
         name="finish_layer",
-    )(sums, outs, backs, totals)
+    )(*given)
 
 
 def pack_joint(q, k, v, o):

time: 173 us -> 158 us (0.913)
  Pallas kernels: 167 us -> 157 us
  local copies, waits for them, and re-layouts: 4.1 us -> 0 us
    pallas_call x1, Pallas kernels: 166 us -> 153 us  [whole_layer(): pl.pallas_call(partial(layer_kernel, nz), out_shape=(jax.ShapeDtypeStruct...]
    unnamed x8 -> x0, local copies, waits for them, and re-layouts: 4.1 us -> none
    pallas_call x1, Pallas kernels: 1.88 us -> 3.66 us  [finish_layer(): pl.pallas_call(partial(finish_kernel, len(shapes)), out_shape=[jax.ShapeD...]
where the time goes in v3:
time: 158 us
  Pallas kernels  157 us (99%)
    pallas_call x1, Pallas kernels, whole_layer(): pl.pallas_call(partial(layer_kernel, nz), out_shape=(jax.ShapeDtypeStruct...  153 us
    pallas_call x1, Pallas kernels, finish_layer(): pl.pallas_call(partial(finish_kernel, len(shapes)), out_shape=[jax.ShapeD...  3.66 us

profile of v3, /device:TPU:0, one launch (start us, length us, event | category | flops | bytes accessed | tf_op | source)
XLA Modules:
  0.0 157.8 jit_solution(5805431422302895580)
XLA Ops:
  0.7 153.3 %whole_layer.1 = (f32[3,96,768]{2,1,0:T(8,128)}, bf16[4,128,768]{2,1,0:T(8,128)(2,1)}, bf16[4,128,768]{2,1,0:T(8,128)(2,1)}, f32[8,128]{1,0:T(8,128)}) custom-call(bf16[4,128,768]{2,1,0:T(8,128)(2,1)} %refs_0_.1, s32[4]{0:T(128)} %refs_1_.1, bf16[4,128,768]{2,1,0:T(8,128)(2,1)} %refs_2_.1, bf16[96,192]{1,0:T(8,128)(2,1)} %refs_3_.1, ...), custom_call_target="tpu_custom_call" | custom-call | tf_op jit(solution)/shard_map/whole_layer/pallas_call | solution.py:1337
  154.0 3.7 %finish_layer.1 = (bf16[4,128,768]{2,1,0:T(8,128)(2,1)}, f32[4,128,768]{2,1,0:T(8,128)}, f32[96,192]{1,0:T(8,128)}, f32[96,192]{1,0:T(8,128)}, f32[96,192]{1,0:T...) custom-call(f32[3,96,768]{2,1,0:T(8,128)} %get-tuple-element.38.refs, ...), custom_call_target="tpu_custom_call" | custom-call | tf_op jit(solution)/shard_map/finish_layer/pallas_call | solution.py:1402

commit v4 on v3

--- a/solution.py
+++ b/solution.py
@@ -373,12 +373,13 @@
 HALF = WIDTH // 2
 KINDS = 3
 FLOWS = (
-    (0, 0, 384, "zyx", "yxz"),
-    (0, 384, 384, "zyx", "xzy"),
-    (1, 0, 512, "zxy", "yxz"),
-    (1, 512, 256, "zyx", "xyz"),
-    (2, 0, 384, "zxy", "yxz"),
-    (2, 384, 384, "yzx", "xzy"),
+    (0, 0, 512, "zyx", "xyz"),
+    (0, 512, 256, "zyx", "xyz"),
+    (1, 0, 256, "zxy", "xyz"),
+    (1, 256, 512, "zxy", "yxz"),
+    (2, 0, 256, "zyx", "yxz"),
+    (2, 256, 256, "zyx", "zxy"),
+    (2, 512, 256, "yxz", "xzy"),
 )
 VECTOR_ROWS = 16
 SHORT, LONG = 24, 96
@@ -765,7 +766,7 @@
 
 BLOCKS = 15
 SEND_COUNT = 15
-DOOR_COUNT = 197
+DOOR_COUNT = 227
 
 
 def flow_shapes(nz):
@@ -817,25 +818,34 @@
 
 
 class Cores:
-    def __init__(self, net, place, w, core, k):
-        self.place = place
+    def __init__(self, net, place, w, core, k, meter):
+        self.place, self.meter = place, meter
         self.w, self.core = w.at[k], core.at[k]
         self.ys = (1 - place.y, place.y)
+        steps = list(range(1, place.nz)) + [0]
+        self.parts = steps[:place.nz // 2], steps[place.nz // 2:]
+        self.c = []
         lane = net.lane()
-        self.c = [net.plan(self.w.at[y, 1 - place.c], self.core.at[y], place.core, lane) for y in self.ys]
+        for y in self.ys:
+            for part in self.parts:
+                door = net.door()
+                spots = [place.z_at(step) for step in part]
+                self.c.append([
+                    net.plan(self.w.at[y, 1 - place.c, z], self.core.at[y, z], place.core, lane, door) for z in spots
+                ])
+        self.trips = [trip for trips in self.c for trip in trips]
 
     def to_core(self, half):
-        self.c[half].start()
-
-    def half(self, half):
+        start_all(self.c[2 * half] + self.c[2 * half + 1])
+
+    def half(self, half, part):
         y = self.ys[half]
-        self.c[half].wait_recv()
-
-        def body(z):
+        trips = self.c[2 * half + part]
+        arrived(trips, self.meter.low_rows(2 * self.core.shape[-2] * len(trips)))
+        for step in self.parts[part]:
+            z = self.place.z_at(step)
             target, source = self.core.at[y, z], self.w.at[y, self.place.c, z]
             target[...] = (target[...].astype(F32) + source[...].astype(F32)).astype(BF16)
-
-        each(self.place.nz, body)
 
 
 class Sink:
@@ -849,7 +859,7 @@
         self.spot = lambda block: tuple(ahead[axis][block[axis]] for axis in ("y", "z", "x"))
         self.order = order
         self.tasks = []
-        self.starts = ([], [])
+        self.starts = [[], [], [], []]
         blocks = [{}]
         for axis in ("y", "z", "x"):
             steps = [i for i in range(1, sizes[axis])] + [0]
@@ -870,7 +880,8 @@
                     copy = net.plan(self.part(away), landing.at[slot], devices[step], lane, door)
                     self.trips.append(copy)
                     if stage == 0:
-                        self.starts[0 if away["y"] else 1].append(copy)
+                        soon = 0 < away["z"] <= p.nz // 2
+                        self.starts[(0 if away["y"] else 2) + (0 if soon else 1)].append(copy)
                     else:
                         waits[tuple(sorted(away.items()))].append(copy)
                     arrivals.append((copy, slot))
@@ -883,8 +894,8 @@
     def part(self, block):
         return self.core.at[(*self.spot(block), slice(None), self.cols)]
 
-    def start(self, half):
-        start_all(self.starts[half])
+    def start(self, half, part):
+        start_all(self.starts[2 * half + part])
 
     def add(self, index):
         block, arrivals, onward = self.tasks[index]
@@ -956,14 +967,14 @@
 def layer_kernel(nz, *refs):
     tokens, lengths, cotangent, w_query, w_key, w_value, w_output, w_inner, w_outer = refs[:9]
     short_in, long_in = refs[9:12] + refs[13:18], refs[12]
-    result, outs, backs, totals = refs[18:22]
+    result_out, outs, backs, totals_out = refs[18:22]
     rest = list(refs[22:])
     buffers, rest = rest[:BUFFER_COUNT], rest[BUFFER_COUNT:]
     core_landing, landings, rest = rest[0], rest[1:1 + len(FLOWS)], rest[1 + len(FLOWS):]
     back_landings = rest[:4]
     v, parts, vec_in, raw_query, raw_key, raw_value, raw_output, own_joint = rest[4:12]
-    raw_short, raw_long = rest[12:20], rest[20]
-    send_sems, recv_sems, local_sems = rest[21:]
+    raw_short, raw_long, result, totals = rest[12:20], rest[20], rest[21], rest[22]
+    send_sems, recv_sems, local_sems = rest[23:]
     place = Place(nz)
     net = Net(send_sems, recv_sems)
     t = place.t
@@ -972,7 +983,7 @@
     owns = (own_joint, w_inner, w_outer)
     g, r = [], []
     meter = Meter(layer.joint, layer.factor)
-    cores = [Cores(net, place, layer.w, core_landing, k) for k in range(KINDS)]
+    cores = [Cores(net, place, layer.w, core_landing, k, meter) for k in range(KINDS)]
     lanes = [[net.lane() for k in range(KINDS)] for _ in range(3)]
     doors = [net.door() for k in range(KINDS)]
     for (k, first, width, order_in, order_out), landing in zip(FLOWS, landings):
@@ -1010,7 +1021,7 @@
 
     def reduced(k):
         departed(trips_of(of_kind(r, k)), meter.low_rows(2 * WIDTH - own_joint.shape[0]))
-        departed(cores[k].c, meter.low_rows(2 * WIDTH))
+        departed(cores[k].trips, meter.low_rows(2 * WIDTH))
 
     def vectors_in():
         arrived(vecs.cores, meter.tiles(4 * nz))
@@ -1048,6 +1059,8 @@
         (vec_in, v.at[place.y, place.c, place.z, place.x]),
         (quarter_of(layer.out, t), outs.at[t]),
         (quarter_of(layer.back, t), backs.at[t]),
+        *[(result.at[k], result_out.at[k]) for k in range(KINDS)],
+        (totals, totals_out),
         (w_query, raw_query),
         (w_key, raw_key),
         (w_value, raw_value),
@@ -1072,138 +1085,157 @@
     def order(i):
         return (1 - place.y + i // 2) % 2 * 2 + (1 - place.c + i) % 2
 
-    start_all(local[8:])
+    start_all(local[12:])
     greet(place)
-    wait_local(local[8:])
+    wait_local(local[12:])
     pack_vectors()
     pack_own()
     vecs.first()
+    g[1].first()
     g[0].first()
     start_all(local[:6])
     wait_local(local[:6])
-    g[1].first()
     start_all(token_in)
-    g[2].first()
-    g[3].first()
-    g[4].first()
-    g[5].first()
     vecs.piece(4)
     vecs.piece(8)
+    g[1].piece(4)
+    g[1].piece(8)
     vecs.piece(2)
-    g[0].piece(4)
     vecs.piece(1)
     vecs.piece(3)
+    g[0].piece(4)
+    vecs.piece(12)
     g[0].piece(8)
-    g[1].piece(4)
-    g[1].piece(8)
-    g[2].piece(4)
-    g[3].piece(8)
-    g[0].piece(1)
-    g[4].piece(4)
-    g[0].piece(2)
-    g[5].piece(8)
-    vecs.piece(12)
+    g[1].piece(12)
     vecs.piece(10)
-    g[0].piece(3)
-    g[0].piece(12)
     vecs.piece(9)
     vecs.piece(11)
+    g[1].piece(1)
+    g[1].piece(2)
+    g[0].piece(12)
+    g[1].piece(3)
+    g[1].piece(9)
+    g[1].piece(10)
+    g[1].piece(11)
     swapped(token_in)
-    g[1].piece(12)
-    g[2].piece(8)
-    g[0].piece(9)
-    g[3].piece(4)
-    g[1].piece(1)
-    g[0].piece(10)
-    g[4].piece(8)
-    g[1].piece(2)
     vecs.piece(6)
     vecs.piece(5)
     vecs.piece(7)
     vecs.to_core(0)
-    g[0].piece(11)
-    g[5].piece(1)
-    g[1].piece(3)
-    g[3].piece(12)
-    g[2].piece(12)
-    g[1].piece(9)
-    g[0].piece(5)
+    g[0].piece(1)
+    g[2].first()
+    g[3].first()
+    g[1].piece(5)
     vecs.piece(14)
     vecs.piece(13)
     vecs.piece(15)
     vecs.to_core(1)
-    g[1].piece(10)
+    g[1].piece(6)
     vectors_in()
-    g[4].piece(12)
     layer.unpack(v)
     layer.start()
     layer.rows_turned[...] = layer.rows[...].T
     layer.clear_sums()
+    g[1].piece(7)
+    g[1].to_core(0)
+    g[0].piece(2)
+    g[0].piece(9)
+    g[0].piece(3)
+    g[0].piece(5)
+    g[2].piece(4)
+    g[2].piece(8)
+    g[3].piece(4)
+    g[2].piece(1)
+    g[3].piece(8)
+    g[1].piece(13)
+    g[2].piece(2)
+    g[1].piece(14)
+    g[2].piece(3)
     g[0].piece(6)
-    g[2].piece(1)
-    g[5].piece(9)
-    g[1].piece(11)
+    g[1].piece(15)
+    g[1].to_core(1)
     g[0].piece(7)
     g[0].to_core(0)
+    g[0].piece(10)
+    g[2].piece(12)
+    g[0].piece(11)
+    g[3].piece(1)
+    g[4].first()
+    g[5].first()
+    g[6].first()
+    g[3].piece(12)
+    g[3].piece(2)
+    g[2].piece(9)
     g[0].piece(13)
-    g[2].piece(2)
-    g[1].piece(5)
+    g[2].piece(10)
+    g[2].piece(5)
+    g[3].piece(3)
+    g[2].piece(11)
+    g[2].piece(6)
+    g[2].piece(7)
+    g[2].to_core(0)
+    g[3].piece(9)
+    g[4].piece(4)
     g[0].piece(14)
-    g[2].piece(3)
-    g[1].piece(6)
-    g[2].piece(5)
-    g[1].piece(7)
-    g[1].to_core(0)
+    g[4].piece(1)
+    g[5].piece(4)
+    g[4].piece(2)
+    g[4].piece(3)
+    g[6].piece(1)
     g[0].piece(15)
     g[0].to_core(1)
-    g[3].piece(1)
-    g[2].piece(9)
-    g[2].piece(6)
-    g[3].piece(2)
-    g[3].piece(3)
-    g[2].piece(10)
-    g[1].piece(13)
-    g[2].piece(11)
-    g[2].piece(7)
-    g[2].to_core(0)
-    g[4].piece(1)
-    g[1].piece(14)
-    g[2].piece(13)
-    g[3].piece(5)
-    g[1].piece(15)
-    g[1].to_core(1)
     def project(i):
         layer.project(near(i))
         ticks(i, {
-            0: [(g[3].piece, 9), (g[4].piece, 2)],
-            1: [(g[2].piece, 14), (g[3].piece, 10), (g[4].piece, 3), (gathered, 0)],
-            2: [(g[3].piece, 6), (g[3].piece, 11)],
+            1: [(g[3].piece, 10), (g[3].piece, 5), (gathered, 0)],
+            2: [(g[2].piece, 13), (g[5].piece, 1), (g[4].piece, 8)],
         })
 
     each(4, project)
-    g[3].piece(7)
-    g[3].to_core(0)
+    g[5].piece(8)
+    g[5].piece(2)
     def attend(i):
         layer.attend(i)
         ticks(i, {
-            0: [(g[3].piece, 13), (g[2].piece, 15), (g[2].to_core, 1), (g[5].piece, 2), (g[4].piece, 5), (g[5].piece, 3), (g[5].piece, 4)],
-            1: [(g[4].piece, 6), (g[4].piece, 9)],
-            2: [(g[3].piece, 14), (g[4].piece, 7), (g[4].to_core, 0), (g[4].piece, 10), (g[5].piece, 5), (g[5].piece, 6), (g[4].piece, 11), (g[5].piece, 7), (g[3].piece, 15), (g[3].to_core, 1), (g[5].to_core, 0), (start_all, back_in)],
+            0: [(g[3].piece, 11), (g[2].piece, 14), (g[6].piece, 2), (g[5].piece, 3)],
+            1: [(g[2].piece, 15), (g[2].to_core, 1), (g[3].piece, 6), (g[4].piece, 5), (g[6].piece, 4)],
+            2: [(g[3].piece, 7), (g[3].to_core, 0), (g[6].piece, 5), (g[4].piece, 6), (g[6].piece, 6), (g[4].piece, 7), (g[4].to_core, 0), (g[4].piece, 12)],
         })
 
     each(4, attend)
-    g[4].piece(13)
-    g[5].piece(10)
+    g[3].piece(13)
+    g[4].piece(9)
+    g[5].piece(12)
+    g[5].piece(5)
+    g[6].piece(7)
+    g[4].piece(10)
     layer.norm_first()
     layer.first_turned[...] = layer.first_low[...].T
-    g[4].piece(14)
+    g[6].piece(8)
+    g[5].piece(6)
+    g[6].piece(9)
+    g[4].piece(11)
+    g[5].piece(7)
+    g[5].to_core(0)
+    g[6].piece(3)
+    g[6].to_core(0)
+    start_all(back_in)
+    g[5].piece(9)
+    g[6].piece(10)
+    g[6].piece(11)
+    g[3].piece(14)
+    g[6].piece(12)
+    g[5].piece(10)
     g[5].piece(11)
+    g[3].piece(15)
+    g[3].to_core(1)
+    g[4].piece(13)
     def feed_inner(i):
         layer.feed_inner(near(i))
         ticks(i, {
-            0: [(g[4].piece, 15), (g[4].to_core, 1)],
-            1: [(g[5].piece, 12), (gathered, 1)],
-            2: [(g[5].piece, 13)],
+            0: [(g[4].piece, 14)],
+            1: [(g[4].piece, 15), (g[4].to_core, 1), (g[6].piece, 13), (g[6].to_core, 1), (gathered, 1)],
+            2: [(g[5].piece, 13), (g[6].piece, 14), (g[6].to_core, 2), (g[6].piece, 15), (g[6].to_core, 3)],
         })
 
     each(4, feed_inner)
@@ -1226,106 +1258,124 @@
         layer.outer_back(order(i))
         ticks(i, {
             0: [(cores[2].to_core, 0)],
-            2: [(cores[2].to_core, 1), (cores[2].half, 0), (r[4].start, 0), (r[5].start, 0)],
+            1: [(cores[2].half, 0, 0), (r[6].start, 0, 0), (r[5].start, 0, 0), (r[4].start, 0, 0)],
+            2: [(cores[2].to_core, 1), (cores[2].half, 0, 1), (r[6].start, 0, 1), (r[5].start, 0, 1), (r[4].start, 0, 1)],
         })
 
     each(4, outer_back)
+    cores[2].half(1, 0)
+    r[6].start(1, 0)
+    r[5].start(1, 0)
+    r[4].start(1, 0)
+    r[6].add(0)
+    r[6].add(1)
     passed_on(1)
     def inner_back(i):
         layer.inner_back(order(i))
         ticks(i, {
-            0: [(cores[1].to_core, 0), (cores[2].half, 1), (r[4].start, 1), (r[5].start, 1), (r[5].add, 0)],
-            1: [(r[5].add, 1), (r[4].add, 0)],
-            2: [(cores[1].to_core, 1), (cores[1].half, 0), (r[3].start, 0), (r[2].start, 0), (r[5].add, 2), (r[4].add, 1), (r[5].add, 6)],
+            0: [(cores[1].to_core, 0), (cores[2].half, 1, 1), (r[6].start, 1, 1), (r[5].start, 1, 1), (r[4].start, 1, 1), (r[6].add, 2), (r[6].add, 6)],
+            1: [(cores[1].half, 0, 0), (r[2].start, 0, 0), (r[3].start, 0, 0), (r[6].add, 3), (r[4].add, 0), (r[6].add, 4), (r[4].add, 1)],
+            2: [(cores[1].to_core, 1), (cores[1].half, 0, 1), (r[2].start, 0, 1), (r[3].start, 0, 1), (r[6].add, 5), (r[4].add, 4), (r[6].add, 7), (r[4].add, 5)],
         })
 
     each(4, inner_back)
+    cores[1].half(1, 0)
+    r[2].start(1, 0)
+    r[3].start(1, 0)
+    r[2].add(0)
+    r[2].add(1)
     r[4].add(2)
-    r[5].add(3)
+    r[5].add(0)
+    r[4].add(3)
     layer.norm_first_back()
-    cores[1].half(1)
-    r[3].start(1)
-    r[2].start(1)
-    r[4].add(3)
-    r[5].add(4)
-    r[4].add(4)
+    cores[1].half(1, 1)
+    r[2].start(1, 1)
+    r[3].start(1, 1)
+    r[4].add(8)
+    r[4].add(6)
+    r[4].add(9)
+    r[4].add(7)
+    r[5].add(2)
     vectors_sent()
     passed_on(0)
     def attend_back(i):
         layer.attend_back(order(i))
         ticks(i, {
-            0: [(r[5].add, 5), (r[4].add, 5), (r[5].add, 8), (r[5].add, 7), (r[4].add, 6), (r[4].add, 8)],
-            1: [(r[3].add, 1), (r[3].add, 2), (r[2].add, 0), (r[3].add, 3)],
-            2: [(r[4].add, 10), (r[2].add, 2), (r[3].add, 4), (r[3].add, 5), (r[2].add, 3), (r[3].add, 6)],
-            3: [(r[4].add, 11), (r[2].add, 5), (r[4].add, 12), (r[2].add, 8)],
+            0: [(r[2].add, 2), (r[2].add, 3), (r[2].add, 4), (r[3].add, 0)],
+            1: [(r[2].add, 6), (r[5].add, 4), (r[4].add, 11), (r[3].add, 4), (r[3].add, 5)],
+            2: [(r[5].add, 1), (r[5].add, 3), (r[3].add, 8), (r[3].add, 3), (r[3].add, 9)],
+            3: [(r[2].add, 8), (r[2].add, 9), (r[0].add, 0), (r[6].add, 9), (r[3].add, 7)],
         })
         layer.joint_back(order(i))
         ticks(i, {
-            0: [(cores[0].to_core, 0), (r[3].add, 0), (r[4].add, 7)],
-            1: [(cores[0].half, 0), (r[0].start, 0), (r[1].start, 0), (r[5].add, 9), (r[2].add, 1), (r[4].add, 9)],
-            2: [(cores[0].to_core, 1), (r[3].add, 7), (r[2].add, 4)],
+            0: [(cores[0].to_core, 0), (r[2].add, 5), (r[4].add, 10), (r[3].add, 1)],
+            1: [(cores[0].half, 0, 0), (r[1].start, 0, 0), (r[0].start, 0, 0), (cores[0].half, 0, 1), (r[1].start, 0, 1), (r[0].start, 0, 1), (r[2].add, 7), (r[3].add, 2)],
+            2: [(cores[0].to_core, 1), (r[1].add, 0), (r[6].add, 8), (r[1].add, 1), (r[3].add, 6)],
         })
 
     each(4, attend_back)
-    cores[0].half(1)
-    r[0].start(1)
-    r[1].start(1)
-    r[1].add(0)
-    r[2].add(6)
+    cores[0].half(1, 0)
+    r[1].start(1, 0)
+    r[0].start(1, 0)
+    cores[0].half(1, 1)
+    r[1].start(1, 1)
+    r[0].start(1, 1)
+    r[2].add(10)
+    r[2].add(11)
+    r[0].add(1)
+    r[1].add(2)
     layer.pack(parts)
     sums.first()
-    r[1].add(1)
-    r[2].add(7)
+    r[1].add(3)
     layer.finish()
     start_all(back_out)
     local[7].start()
     sums.core_done()
-    r[5].add(10)
+    r[0].add(2)
+    r[6].add(10)
+    r[4].add(12)
+    r[0].add(3)
+    r[3].add(10)
+    r[5].add(5)
+    r[5].add(6)
+    local[10].start()
     reduced(2)
-    r[1].add(2)
-    r[3].add(8)
+    r[3].add(11)
+    r[1].add(4)
+    r[1].add(8)
+    r[2].add(12)
+    r[1].add(5)
+    r[1].add(9)
+    r[3].add(12)
+    local[9].start()
+    reduced(1)
+    r[0].add(4)
+    r[0].add(8)
+    r[0].add(5)
+    r[0].add(9)
     r[1].add(6)
-    r[3].add(9)
-    r[3].add(10)
-    r[2].add(9)
-    r[3].add(11)
-    r[0].add(0)
-    r[2].add(10)
-    r[0].add(1)
-    r[2].add(11)
-    r[0].add(2)
-    r[1].add(8)
-    r[1].add(3)
-    r[0].add(3)
-    r[1].add(4)
-    r[0].add(4)
-    r[1].add(5)
-    r[0].add(5)
-    r[3].add(12)
+    r[1].add(10)
     r[1].add(7)
+    r[1].add(11)
+    sums.y_done()
     r[0].add(6)
-    r[0].add(8)
+    r[0].add(10)
     r[0].add(7)
-    r[0].add(9)
-    r[0].add(10)
+    sums.x_done()
     r[0].add(11)
-    r[2].add(12)
-    reduced(1)
-    sums.y_done()
-    r[1].add(9)
-    sums.x_done()
-    r[1].add(10)
+    r[1].add(12)
     r[0].add(12)
     sums.z_done()
+    local[11].start()
+    local[8].start()
     reduced(0)
     sums.sent()
-    wait_local(local[6:8])
+    wait_local(local[6:12])
     swapped(out_out)
     swapped(back_out)
     swaps_sent()
 
 
-VMEM_SPEC = pl.BlockSpec(memory_space=pltpu.VMEM)
 ANY_SPEC = pl.BlockSpec(memory_space=pl.ANY)
 LIMIT = 67043328
 
@@ -1343,7 +1393,7 @@
             jax.ShapeDtypeStruct((8, 128), F32),
         ),
         in_specs=[ANY_SPEC, pl.BlockSpec(memory_space=pltpu.SMEM)] + [ANY_SPEC] * 16,
-        out_specs=(VMEM_SPEC, ANY_SPEC, ANY_SPEC, VMEM_SPEC),
+        out_specs=(ANY_SPEC,) * 4,
         scratch_shapes=buffer_shapes(nz, seq) + flow_shapes(nz) + [
             pltpu.VMEM((2, nz, 2, 8, 128), F32),
             pltpu.VMEM((nz, 2, 8, 128), F32),
@@ -1357,9 +1407,11 @@
             pltpu.VMEM((part, WIDTH), BF16),
             *[pltpu.VMEM((SHORT,), F32)] * 8,
             pltpu.VMEM((LONG,), F32),
+            pltpu.VMEM((KINDS, part, WIDTH), F32),
+            pltpu.VMEM((8, 128), F32),
             pltpu.SemaphoreType.DMA((SEND_COUNT,)),
             pltpu.SemaphoreType.DMA((DOOR_COUNT,)),
-            pltpu.SemaphoreType.DMA((24,)),
+            pltpu.SemaphoreType.DMA((25,)),
         ],
         compiler_params=pltpu.CompilerParams(collective_id=0, has_side_effects=True, vmem_limit_bytes=LIMIT),
         name="whole_layer",

time: 158 us -> 150 us (0.949)
  Pallas kernels: 157 us -> 149 us
    pallas_call x1, Pallas kernels: 153 us -> 146 us  [whole_layer(): pl.pallas_call(partial(layer_kernel, nz), out_shape=(jax.ShapeDtypeStruct...]
where the time goes in v4:
time: 150 us
  Pallas kernels  149 us (99%)
    pallas_call x1, Pallas kernels, whole_layer(): pl.pallas_call(partial(layer_kernel, nz), out_shape=(jax.ShapeDtypeStruct...  146 us
    pallas_call x1, Pallas kernels, finish_layer(): pl.pallas_call(partial(finish_kernel, len(shapes)), out_shape=[jax.ShapeD...  3.66 us

profile of v4, /device:TPU:0, one launch (start us, length us, event | category | flops | bytes accessed | tf_op | source)
XLA Modules:
  0.0 150.1 jit_solution(9258254338251920006)
XLA Ops:
  0.7 145.6 %whole_layer.1 = (f32[3,96,768]{2,1,0:T(8,128)}, bf16[4,128,768]{2,1,0:T(8,128)(2,1)}, bf16[4,128,768]{2,1,0:T(8,128)(2,1)}, f32[8,128]{1,0:T(8,128)}) custom-call(bf16[4,128,768]{2,1,0:T(8,128)(2,1)} %refs_0_.1, s32[4]{0:T(128)} %refs_1_.1, bf16[4,128,768]{2,1,0:T(8,128)(2,1)} %refs_2_.1, bf16[96,192]{1,0:T(8,128)(2,1)} %refs_3_.1, ...), custom_call_target="tpu_custom_call" | custom-call | tf_op jit(solution)/shard_map/whole_layer/pallas_call | solution.py:1387
  146.3 3.7 %finish_layer.1 = (bf16[4,128,768]{2,1,0:T(8,128)(2,1)}, f32[4,128,768]{2,1,0:T(8,128)}, f32[96,192]{1,0:T(8,128)}, f32[96,192]{1,0:T(8,128)}, f32[96,192]{1,0:T...) custom-call(f32[3,96,768]{2,1,0:T(8,128)} %get-tuple-element.38.refs, ...), custom_call_target="tpu_custom_call" | custom-call | tf_op jit(solution)/shard_map/finish_layer/pallas_call | solution.py:1454

commit v5 on v4

--- a/solution.py
+++ b/solution.py
@@ -377,8 +377,8 @@
     (0, 512, 256, "zyx", "xyz"),
     (1, 0, 256, "zxy", "xyz"),
     (1, 256, 512, "zxy", "yxz"),
-    (2, 0, 256, "zyx", "yxz"),
-    (2, 256, 256, "zyx", "zxy"),
+    (2, 0, 256, "zyx", "zxy"),
+    (2, 256, 256, "zyx", "yxz"),
     (2, 512, 256, "yxz", "xzy"),
 )
 VECTOR_ROWS = 16
@@ -509,11 +509,11 @@
         (
             self.w, self.rows, self.back, self.rows_turned, self.joint, self.probs, self.context, self.acc,
             self.normed, self.factor, self.first_low, self.first_turned, self.active, self.slope, self.grad_low,
-            self.grad_turned, self.out, self.vec, self.sums,
+            self.grad_turned, self.out, self.vec, self.sums, self.early,
         ) = refs
         self.length = length
         self.seq = self.rows.shape[0]
-        self.block = 128
+        self.block = self.seq
 
     def weight(self, kind, t):
         return self.w[kind, t // 2, t % 2].reshape(WIDTH, WIDTH)
@@ -649,24 +649,36 @@
             normed, factor = normalize(self.acc[rows])
             valid = self.row_valid(i)
             gain = self.row(ROW_GAIN2)
+            self.first_low[rows] = normed.astype(BF16)
             self.out[rows] = ((normed * gain + self.row(ROW_SHIFT2)) * valid).astype(BF16)
             out_grad = self.back[rows].astype(F32) * valid
-            self.add_sum(ROW_GAIN2, out_grad * normed)
-            self.add_sum(ROW_SHIFT2, out_grad)
             sum_grad = normalize_back(out_grad * gain, normed, factor)
             self.acc[rows] = sum_grad
-            low = sum_grad.astype(BF16)
-            self.grad_low[rows] = low
-            self.add_sum(ROW_OUTER, low.astype(F32))
+            self.grad_low[rows] = sum_grad.astype(BF16)
 
         self.blocks(body)
-        self.grad_turned[...] = self.grad_low[...].T
-
-    def outer_back(self, t):
+
+    def second_sums(self):
+        def body(rows, i):
+            out_grad = self.back[rows].astype(F32) * self.row_valid(i)
+            self.add_sum(ROW_GAIN2, out_grad * self.first_low[rows].astype(F32))
+            self.add_sum(ROW_SHIFT2, out_grad)
+            self.add_sum(ROW_OUTER, self.grad_low[rows].astype(F32))
+
+        self.blocks(body)
+
+    def outer_slope(self, t):
         grad = (dot(self.grad_low[...], self.weight(2, t)) * self.slope[t].astype(F32)).astype(BF16)
         self.slope[t] = grad
         self.add_sum(ROW_INNER + t, grad.astype(F32))
-        self.store_grad(2, t, dot(self.grad_turned[...], self.active[t]))
+
+    def outer_back(self, t):
+        self.outer_slope(t)
+        self.store_grad(2, t, dot_rows(self.grad_low[...], self.active[t]))
+
+    def outer_early(self, t):
+        value = dot_rows(self.grad_low[...], self.active[t])
+        self.early[...] = value.astype(BF16).reshape(self.early.shape)
 
     def inner_back(self, t):
         grad = self.slope[t]
@@ -734,7 +746,7 @@
     lax.fori_loop(0, count, step, 0)
 
 
-BUFFER_COUNT = 19
+BUFFER_COUNT = 20
 
 
 def buffer_shapes(nz, seq):
@@ -760,6 +772,7 @@
         (low, BF16),
         ((VECTOR_ROWS, WIDTH), F32),
         ((VECTOR_ROWS, WIDTH), F32),
+        ((nz, 2, part, WIDTH), BF16),
     ]
     return [pltpu.VMEM(*shape) for shape in shapes]
 
@@ -818,7 +831,7 @@
 
 
 class Cores:
-    def __init__(self, net, place, w, core, k, meter):
+    def __init__(self, net, place, w, core, k, meter, early=None):
         self.place, self.meter = place, meter
         self.w, self.core = w.at[k], core.at[k]
         self.ys = (1 - place.y, place.y)
@@ -830,9 +843,8 @@
             for part in self.parts:
                 door = net.door()
                 spots = [place.z_at(step) for step in part]
-                self.c.append([
-                    net.plan(self.w.at[y, 1 - place.c, z], self.core.at[y, z], place.core, lane, door) for z in spots
-                ])
+                source = self.w.at[y, 1 - place.c] if early is None or self.c[1:] else early
+                self.c.append([net.plan(source.at[z], self.core.at[y, z], place.core, lane, door) for z in spots])
         self.trips = [trip for trips in self.c for trip in trips]
 
     def to_core(self, half):
@@ -983,7 +995,8 @@
     owns = (own_joint, w_inner, w_outer)
     g, r = [], []
     meter = Meter(layer.joint, layer.factor)
-    cores = [Cores(net, place, layer.w, core_landing, k, meter) for k in range(KINDS)]
+    cores = [Cores(net, place, layer.w, core_landing, k, meter) for k in (0, 1)]
+    cores.append(Cores(net, place, layer.w, core_landing, 2, meter, layer.early))
     lanes = [[net.lane() for k in range(KINDS)] for _ in range(3)]
     doors = [net.door() for k in range(KINDS)]
     for (k, first, width, order_in, order_out), landing in zip(FLOWS, landings):
@@ -1093,155 +1106,157 @@
     vecs.first()
     g[1].first()
     g[0].first()
+    g[2].first()
+    g[1].piece(4)
+    start_all(token_in)
+    vecs.piece(2)
     start_all(local[:6])
     wait_local(local[:6])
-    start_all(token_in)
+    g[1].piece(8)
+    g[3].first()
+    g[5].first()
+    g[4].first()
+    g[0].piece(8)
+    vecs.piece(1)
+    g[1].piece(2)
+    g[6].first()
+    vecs.piece(3)
+    vecs.piece(8)
+    g[3].piece(4)
+    g[1].piece(1)
+    g[1].piece(3)
+    g[5].piece(8)
+    vecs.piece(11)
     vecs.piece(4)
-    vecs.piece(8)
-    g[1].piece(4)
-    g[1].piece(8)
-    vecs.piece(2)
-    vecs.piece(1)
-    vecs.piece(3)
     g[0].piece(4)
+    g[2].piece(4)
+    g[4].piece(8)
+    g[1].piece(12)
     vecs.piece(12)
-    g[0].piece(8)
-    g[1].piece(12)
-    vecs.piece(10)
+    g[2].piece(8)
+    g[6].piece(2)
     vecs.piece(9)
-    vecs.piece(11)
-    g[1].piece(1)
-    g[1].piece(2)
+    g[1].piece(11)
+    vecs.piece(6)
+    g[0].piece(1)
     g[0].piece(12)
-    g[1].piece(3)
-    g[1].piece(9)
-    g[1].piece(10)
-    g[1].piece(11)
-    swapped(token_in)
-    vecs.piece(6)
+    g[5].piece(4)
+    g[0].piece(2)
+    g[6].piece(1)
     vecs.piece(5)
     vecs.piece(7)
+    g[5].piece(12)
+    g[4].piece(4)
+    g[1].piece(9)
+    g[3].piece(12)
+    vecs.piece(10)
+    g[6].piece(3)
+    swapped(token_in)
+    vecs.piece(14)
+    g[2].piece(1)
+    g[1].piece(5)
+    g[1].piece(7)
+    g[1].piece(10)
+    g[0].piece(9)
+    g[0].piece(10)
+    vecs.piece(15)
+    vecs.piece(13)
     vecs.to_core(0)
-    g[0].piece(1)
-    g[2].first()
-    g[3].first()
-    g[1].piece(5)
-    vecs.piece(14)
-    vecs.piece(13)
-    vecs.piece(15)
+    g[0].piece(3)
+    g[3].piece(8)
+    g[6].to_core(0)
+    g[2].piece(12)
     vecs.to_core(1)
+    g[2].piece(2)
+    g[4].piece(12)
     g[1].piece(6)
     vectors_in()
+    g[2].piece(5)
     layer.unpack(v)
     layer.start()
     layer.rows_turned[...] = layer.rows[...].T
     layer.clear_sums()
-    g[1].piece(7)
+    g[2].piece(3)
+    g[1].piece(13)
+    g[2].piece(6)
+    g[1].piece(15)
+    g[0].piece(7)
+    g[0].piece(5)
+    g[1].piece(14)
+    g[1].to_core(1)
+    g[0].piece(6)
+    g[2].piece(7)
+    g[2].piece(9)
+    g[3].piece(1)
+    g[0].piece(11)
+    g[2].to_core(0)
+    g[2].piece(10)
+    g[0].piece(13)
+    g[0].to_core(0)
     g[1].to_core(0)
-    g[0].piece(2)
-    g[0].piece(9)
-    g[0].piece(3)
-    g[0].piece(5)
-    g[2].piece(4)
-    g[2].piece(8)
-    g[3].piece(4)
-    g[2].piece(1)
-    g[3].piece(8)
-    g[1].piece(13)
-    g[2].piece(2)
-    g[1].piece(14)
-    g[2].piece(3)
-    g[0].piece(6)
-    g[1].piece(15)
-    g[1].to_core(1)
-    g[0].piece(7)
-    g[0].to_core(0)
-    g[0].piece(10)
-    g[2].piece(12)
-    g[0].piece(11)
-    g[3].piece(1)
-    g[4].first()
-    g[5].first()
-    g[6].first()
-    g[3].piece(12)
+    g[3].piece(3)
+    g[0].piece(14)
+    g[2].piece(11)
+    g[0].piece(15)
+    g[2].piece(15)
     g[3].piece(2)
-    g[2].piece(9)
-    g[0].piece(13)
-    g[2].piece(10)
-    g[2].piece(5)
-    g[3].piece(3)
-    g[2].piece(11)
-    g[2].piece(6)
-    g[2].piece(7)
-    g[2].to_core(0)
-    g[3].piece(9)
-    g[4].piece(4)
-    g[0].piece(14)
-    g[4].piece(1)
-    g[5].piece(4)
-    g[4].piece(2)
-    g[4].piece(3)
-    g[6].piece(1)
-    g[0].piece(15)
     g[0].to_core(1)
+    g[5].piece(3)
     def project(i):
         layer.project(near(i))
         ticks(i, {
-            1: [(g[3].piece, 10), (g[3].piece, 5), (gathered, 0)],
-            2: [(g[2].piece, 13), (g[5].piece, 1), (g[4].piece, 8)],
+            1: [(g[2].piece, 14), (g[2].piece, 13), (gathered, 0), (g[3].piece, 9), (g[5].piece, 1)],
+            2: [(g[3].piece, 5), (g[3].piece, 11)],
         })
 
     each(4, project)
-    g[5].piece(8)
     g[5].piece(2)
+    g[3].piece(10)
+    g[3].piece(7)
     def attend(i):
         layer.attend(i)
         ticks(i, {
-            0: [(g[3].piece, 11), (g[2].piece, 14), (g[6].piece, 2), (g[5].piece, 3)],
-            1: [(g[2].piece, 15), (g[2].to_core, 1), (g[3].piece, 6), (g[4].piece, 5), (g[6].piece, 4)],
-            2: [(g[3].piece, 7), (g[3].to_core, 0), (g[6].piece, 5), (g[4].piece, 6), (g[6].piece, 6), (g[4].piece, 7), (g[4].to_core, 0), (g[4].piece, 12)],
+            0: [(g[3].piece, 13), (g[4].piece, 1), (g[3].piece, 6), (g[3].to_core, 0), (g[5].piece, 7), (g[4].piece, 2)],
+            1: [(g[5].piece, 6), (g[2].to_core, 1), (g[5].piece, 5), (g[6].piece, 6), (g[4].piece, 3), (start_all, back_in), (g[6].piece, 4), (g[5].piece, 9), (g[5].to_core, 0)],
+            2: [(g[5].piece, 11)],
         })
 
     each(4, attend)
-    g[3].piece(13)
-    g[4].piece(9)
-    g[5].piece(12)
-    g[5].piece(5)
-    g[6].piece(7)
+    g[6].piece(10)
+    g[3].piece(15)
     g[4].piece(10)
     layer.norm_first()
     layer.first_turned[...] = layer.first_low[...].T
-    g[6].piece(8)
-    g[5].piece(6)
-    g[6].piece(9)
-    g[4].piece(11)
-    g[5].piece(7)
-    g[5].to_core(0)
-    g[6].piece(3)
-    g[6].to_core(0)
-    start_all(back_in)
-    g[5].piece(9)
-    g[6].piece(10)
-    g[6].piece(11)
+    g[6].piece(5)
+    g[4].piece(6)
     g[3].piece(14)
-    g[6].piece(12)
+    g[5].piece(13)
+    g[4].piece(5)
     g[5].piece(10)
-    g[5].piece(11)
-    g[3].piece(15)
     g[3].to_core(1)
-    g[4].piece(13)
     def feed_inner(i):
         layer.feed_inner(near(i))
         ticks(i, {
-            0: [(g[4].piece, 14)],
-            1: [(g[4].piece, 15), (g[4].to_core, 1), (g[6].piece, 13), (g[6].to_core, 1), (gathered, 1)],
-            2: [(g[5].piece, 13), (g[6].piece, 14), (g[6].to_core, 2), (g[6].piece, 15), (g[6].to_core, 3)],
+            0: [(g[5].piece, 14), (g[5].piece, 15), (g[5].to_core, 1), (g[4].piece, 9)],
+            1: [(g[4].piece, 7), (gathered, 1)],
+            2: [(g[4].to_core, 0), (g[4].piece, 11), (g[6].piece, 7)],
         })
 
     each(4, feed_inner)
-    g[5].piece(14)
-    g[5].piece(15)
-    g[5].to_core(1)
+    g[6].piece(9)
+    g[6].piece(12)
+    g[6].piece(13)
+    g[6].to_core(1)
+    g[6].piece(15)
+    g[6].to_core(3)
+    g[6].piece(14)
+    g[4].piece(15)
+    g[6].piece(11)
+    g[6].piece(8)
+    g[6].to_core(2)
+    g[4].piece(13)
+    g[4].piece(14)
+    g[4].to_core(1)
     def feed_outer(i):
         layer.feed_outer(near(i))
         ticks(i, {
@@ -1253,93 +1268,97 @@
     layer.norm_second()
     start_all(out_out)
     local[6].start()
+    layer.outer_early(order(0))
     passed_on(2)
+    cores[2].to_core(0)
     def outer_back(i):
-        layer.outer_back(order(i))
+        layer.outer_back(order(i + 1))
         ticks(i, {
-            0: [(cores[2].to_core, 0)],
-            1: [(cores[2].half, 0, 0), (r[6].start, 0, 0), (r[5].start, 0, 0), (r[4].start, 0, 0)],
-            2: [(cores[2].to_core, 1), (cores[2].half, 0, 1), (r[6].start, 0, 1), (r[5].start, 0, 1), (r[4].start, 0, 1)],
+            0: [(cores[2].half, 0, 0), (r[6].start, 0, 0), (r[5].start, 0, 0), (r[4].start, 0, 0)],
+            1: [(passed_on, 1), (cores[2].to_core, 1), (cores[2].half, 0, 1), (r[6].start, 0, 1), (r[5].start, 0, 1), (r[4].start, 0, 1)],
         })
 
-    each(4, outer_back)
+    each(3, outer_back)
     cores[2].half(1, 0)
     r[6].start(1, 0)
     r[5].start(1, 0)
     r[4].start(1, 0)
-    r[6].add(0)
-    r[6].add(1)
-    passed_on(1)
+    layer.outer_slope(order(0))
     def inner_back(i):
         layer.inner_back(order(i))
         ticks(i, {
-            0: [(cores[1].to_core, 0), (cores[2].half, 1, 1), (r[6].start, 1, 1), (r[5].start, 1, 1), (r[4].start, 1, 1), (r[6].add, 2), (r[6].add, 6)],
-            1: [(cores[1].half, 0, 0), (r[2].start, 0, 0), (r[3].start, 0, 0), (r[6].add, 3), (r[4].add, 0), (r[6].add, 4), (r[4].add, 1)],
-            2: [(cores[1].to_core, 1), (cores[1].half, 0, 1), (r[2].start, 0, 1), (r[3].start, 0, 1), (r[6].add, 5), (r[4].add, 4), (r[6].add, 7), (r[4].add, 5)],
+            0: [(cores[1].to_core, 0), (cores[2].half, 1, 1), (r[6].start, 1, 1), (r[5].start, 1, 1), (r[4].start, 1, 1), (r[6].add, 2), (r[6].add, 0)],
+            1: [(cores[1].half, 0, 0), (r[2].start, 0, 0), (r[3].start, 0, 0)],
+            2: [(cores[1].to_core, 1), (r[6].add, 1), (r[5].add, 4), (cores[1].half, 0, 1), (r[2].start, 0, 1), (r[3].start, 0, 1), (r[2].add, 0), (r[5].add, 1), (r[6].add, 6)],
         })
 
     each(4, inner_back)
+    r[5].add(0)
+    r[6].add(3)
+    r[5].add(5)
+    r[5].add(3)
+    vectors_sent()
+    r[6].add(4)
+    r[6].add(5)
+    layer.second_sums()
+    r[5].add(2)
     cores[1].half(1, 0)
     r[2].start(1, 0)
     r[3].start(1, 0)
-    r[2].add(0)
-    r[2].add(1)
-    r[4].add(2)
-    r[5].add(0)
-    r[4].add(3)
-    layer.norm_first_back()
     cores[1].half(1, 1)
     r[2].start(1, 1)
     r[3].start(1, 1)
-    r[4].add(8)
-    r[4].add(6)
-    r[4].add(9)
-    r[4].add(7)
-    r[5].add(2)
-    vectors_sent()
+    layer.norm_first_back()
+    r[2].add(1)
     passed_on(0)
+    r[5].add(7)
+    r[5].add(8)
+    r[4].add(0)
+    r[5].add(9)
     def attend_back(i):
         layer.attend_back(order(i))
         ticks(i, {
-            0: [(r[2].add, 2), (r[2].add, 3), (r[2].add, 4), (r[3].add, 0)],
-            1: [(r[2].add, 6), (r[5].add, 4), (r[4].add, 11), (r[3].add, 4), (r[3].add, 5)],
-            2: [(r[5].add, 1), (r[5].add, 3), (r[3].add, 8), (r[3].add, 3), (r[3].add, 9)],
-            3: [(r[2].add, 8), (r[2].add, 9), (r[0].add, 0), (r[6].add, 9), (r[3].add, 7)],
+            2: [(r[4].add, 1), (r[4].add, 2), (r[6].add, 8), (r[2].add, 3), (r[2].add, 6), (r[3].add, 2), (cores[0].half, 0, 1), (r[1].start, 0, 1), (r[0].start, 0, 1), (r[5].add, 10), (r[4].add, 4)],
+            3: [(cores[0].to_core, 1), (r[3].add, 6), (r[3].add, 3), (r[3].add, 7), (r[3].add, 9), (r[1].add, 1), (r[5].add, 11), (r[0].add, 0)],
         })
         layer.joint_back(order(i))
         ticks(i, {
-            0: [(cores[0].to_core, 0), (r[2].add, 5), (r[4].add, 10), (r[3].add, 1)],
-            1: [(cores[0].half, 0, 0), (r[1].start, 0, 0), (r[0].start, 0, 0), (cores[0].half, 0, 1), (r[1].start, 0, 1), (r[0].start, 0, 1), (r[2].add, 7), (r[3].add, 2)],
-            2: [(cores[0].to_core, 1), (r[1].add, 0), (r[6].add, 8), (r[1].add, 1), (r[3].add, 6)],
+            0: [(r[3].add, 0), (r[2].add, 4), (cores[0].to_core, 0), (r[3].add, 1), (r[2].add, 5), (r[2].add, 2), (r[5].add, 6)],
+            1: [(cores[0].half, 0, 0), (r[1].start, 0, 0), (r[0].start, 0, 0), (r[2].add, 7), (r[6].add, 7), (r[3].add, 4), (r[3].add, 5)],
+            2: [(r[4].add, 3), (r[3].add, 8)],
         })
 
     each(4, attend_back)
     cores[0].half(1, 0)
     r[1].start(1, 0)
     r[0].start(1, 0)
+    r[2].add(10)
+    r[1].add(0)
+    r[1].add(3)
+    layer.pack(parts)
+    r[2].add(9)
+    r[6].add(9)
+    r[1].add(2)
+    sums.first()
+    r[0].add(1)
+    r[2].add(8)
+    layer.finish()
+    r[0].add(2)
+    r[4].add(5)
+    r[4].add(6)
+    r[6].add(10)
+    r[2].add(11)
+    sums.core_done()
+    start_all(back_out)
+    local[7].start()
+    r[5].add(12)
+    local[10].start()
     cores[0].half(1, 1)
     r[1].start(1, 1)
     r[0].start(1, 1)
-    r[2].add(10)
-    r[2].add(11)
-    r[0].add(1)
-    r[1].add(2)
-    layer.pack(parts)
-    sums.first()
-    r[1].add(3)
-    layer.finish()
-    start_all(back_out)
-    local[7].start()
-    sums.core_done()
-    r[0].add(2)
-    r[6].add(10)
-    r[4].add(12)
     r[0].add(3)
+    reduced(2)
     r[3].add(10)
-    r[5].add(5)
-    r[5].add(6)
-    local[10].start()
-    reduced(2)
     r[3].add(11)
     r[1].add(4)
     r[1].add(8)
@@ -1419,30 +1438,43 @@
 
 
 def finish_kernel(count, *refs):
-    given, results, rest = refs[:4], refs[4:4 + count], refs[4 + count:]
-    (sums, outs, backs, totals), made, (sems, sent) = rest[:4], rest[4:-2], rest[-2:]
-    arrivals = [pltpu.make_async_copy(ref, spot, sems.at[i]) for i, (ref, spot) in enumerate(zip(given, rest))]
-    start_all(arrivals)
-    input_grad, g_query, g_key, g_value, g_output, g_inner, g_outer = made[:7]
-    copies = [pltpu.make_async_copy(outs, results[0], sent.at[0])]
-    copies += [pltpu.make_async_copy(*pair, sent.at[i + 1]) for i, pair in enumerate(zip(made, results[1:]))]
-    arrivals[2].wait()
-    input_grad[...] = backs[...].astype(F32)
-    copies[1].start()
-    arrivals[1].wait()
-    copies[0].start()
-    arrivals[0].wait()
-    g_inner[...] = sums[1]
-    g_outer[...] = sums[2]
+    sums_in, outs_in, backs_in, totals_in = refs[:4]
+    results, rest = refs[4:4 + count], refs[4 + count:]
+    sums, outs, backs, totals, input_grad, g_query, g_key, g_value, g_output = rest[:9]
+    vectors, (sems, sent) = rest[9:-2], rest[-2:]
+    quarters = range(backs.shape[0])
+    pairs = [(backs_in.at[i], backs.at[i]) for i in quarters] + [(sums_in.at[k], sums.at[k]) for k in range(KINDS)]
+    pairs += [(totals_in, totals), (outs_in, outs)]
+    reads = [pltpu.make_async_copy(*pair, sems.at[i]) for i, pair in enumerate(pairs)]
+    start_all(reads)
+    writes = []
+
+    def write(source, target):
+        writes.append(pltpu.make_async_copy(source, target, sent.at[len(writes)]))
+        writes[-1].start()
+
+    for i in quarters:
+        reads[i].wait()
+        input_grad[i] = backs[i].astype(F32)
+        write(input_grad.at[i], results[1].at[i])
+    joint_read, inner_read, outer_read, totals_read, outs_read = reads[len(quarters):]
+    joint_read.wait()
     g_query[...], g_key[...], g_value[...], g_turned = unpack_joint(sums[0])
     g_output[...] = g_turned.T
-    start_all(copies[2:8])
-    arrivals[3].wait()
+    for ref, target in zip((g_query, g_key, g_value, g_output), results[2:6]):
+        write(ref, target)
+    inner_read.wait()
+    write(sums.at[1], results[6])
+    outer_read.wait()
+    write(sums.at[2], results[7])
+    totals_read.wait()
     short = [0, 1, 2, None, 3, 4, 5, 6, 7]
-    for row, ref in zip(short, made[7:]):
+    for row, ref, target in zip(short, vectors, results[8:]):
         ref[...] = (totals[0:1, 32:128] if row is None else totals[row:row + 1, 0:SHORT]).reshape(ref.shape)
-    start_all(copies[8:])
-    wait_local(copies)
+        write(ref, target)
+    outs_read.wait()
+    write(outs, results[0])
+    wait_local(writes)
 
 
 def finish_layer(sums, outs, backs, totals):
@@ -1451,14 +1483,15 @@
     shapes = [outs.shape, backs.shape] + [(part, share)] * 3 + [(share, part), (part, WIDTH), (part, WIDTH)]
     shapes += [(SHORT,)] * 3 + [(LONG,)] + [(SHORT,)] * 5
     given = (sums, outs, backs, totals)
+    reads, writes = backs.shape[0] + KINDS + 2, backs.shape[0] + len(shapes) - 1
     return pl.pallas_call(
         partial(finish_kernel, len(shapes)),
         out_shape=[jax.ShapeDtypeStruct(shape, F32 if i else BF16) for i, shape in enumerate(shapes)],
-        in_specs=[ANY_SPEC] * 4,
+        in_specs=[ANY_SPEC] * len(given),
         out_specs=[ANY_SPEC] * len(shapes),
         scratch_shapes=[pltpu.VMEM(ref.shape, ref.dtype) for ref in given]
-        + [pltpu.VMEM(shape, F32) for shape in shapes[1:]]
-        + [pltpu.SemaphoreType.DMA((4,)), pltpu.SemaphoreType.DMA((len(shapes),))],
+        + [pltpu.VMEM(shape, F32) for shape in shapes[1:6] + shapes[8:]]
+        + [pltpu.SemaphoreType.DMA((reads,)), pltpu.SemaphoreType.DMA((writes,))],
         compiler_params=pltpu.CompilerParams(vmem_limit_bytes=LIMIT),
         name="finish_layer",
     )(*given)

time: 150 us -> 148 us (0.987)
  Pallas kernels: 149 us -> 147 us
where the time goes in v5:
time: 148 us
  Pallas kernels  147 us (99%)
    pallas_call x1, Pallas kernels, whole_layer(): pl.pallas_call(partial(layer_kernel, nz), out_shape=(jax.ShapeDtypeStruct...  144 us
    pallas_call x1, Pallas kernels, finish_layer(): pl.pallas_call(partial(finish_kernel, len(shapes)), out_shape=[jax.ShapeD...  2.97 us

profile of v5, /device:TPU:0, one launch (start us, length us, event | category | flops | bytes accessed | tf_op | source)
XLA Modules:
  0.0 148.2 jit_solution(2934288682622997814)
XLA Ops:
  0.7 144.4 %whole_layer.1 = (f32[3,96,768]{2,1,0:T(8,128)}, bf16[4,128,768]{2,1,0:T(8,128)(2,1)}, bf16[4,128,768]{2,1,0:T(8,128)(2,1)}, f32[8,128]{1,0:T(8,128)}) custom-call(bf16[4,128,768]{2,1,0:T(8,128)(2,1)} %refs_0_.1, s32[4]{0:T(128)} %refs_1_.1, bf16[4,128,768]{2,1,0:T(8,128)(2,1)} %refs_2_.1, bf16[96,192]{1,0:T(8,128)(2,1)} %refs_3_.1, ...), custom_call_target="tpu_custom_call" | custom-call | tf_op jit(solution)/shard_map/whole_layer/pallas_call | solution.py:1406
  145.1 3.0 %finish_layer.1 = (bf16[4,128,768]{2,1,0:T(8,128)(2,1)}, f32[4,128,768]{2,1,0:T(8,128)}, f32[96,192]{1,0:T(8,128)}, f32[96,192]{1,0:T(8,128)}, f32[96,192]{1,0:T...) custom-call(f32[3,96,768]{2,1,0:T(8,128)} %get-tuple-element.38.refs, ...), custom_call_target="tpu_custom_call" | custom-call | tf_op jit(solution)/shard_map/finish_layer/pallas_call | solution.py:1487

commit v6 on v5

--- a/solution.py
+++ b/solution.py
@@ -1108,12 +1108,12 @@
     g[0].first()
     g[2].first()
     g[1].piece(4)
-    start_all(token_in)
     vecs.piece(2)
+    g[1].piece(8)
+    g[3].first()
     start_all(local[:6])
     wait_local(local[:6])
-    g[1].piece(8)
-    g[3].first()
+    start_all(token_in)
     g[5].first()
     g[4].first()
     g[0].piece(8)
@@ -1122,15 +1122,15 @@
     g[6].first()
     vecs.piece(3)
     vecs.piece(8)
+    g[1].piece(1)
     g[3].piece(4)
-    g[1].piece(1)
     g[1].piece(3)
     g[5].piece(8)
     vecs.piece(11)
     vecs.piece(4)
     g[0].piece(4)
+    g[4].piece(8)
     g[2].piece(4)
-    g[4].piece(8)
     g[1].piece(12)
     vecs.piece(12)
     g[2].piece(8)
@@ -1147,82 +1147,82 @@
     vecs.piece(7)
     g[5].piece(12)
     g[4].piece(4)
+    g[3].piece(12)
     g[1].piece(9)
-    g[3].piece(12)
     vecs.piece(10)
-    g[6].piece(3)
     swapped(token_in)
     vecs.piece(14)
     g[2].piece(1)
     g[1].piece(5)
+    g[1].piece(10)
     g[1].piece(7)
-    g[1].piece(10)
+    g[0].piece(10)
     g[0].piece(9)
-    g[0].piece(10)
     vecs.piece(15)
     vecs.piece(13)
     vecs.to_core(0)
     g[0].piece(3)
+    g[6].piece(3)
+    g[6].to_core(0)
+    g[4].piece(12)
     g[3].piece(8)
-    g[6].to_core(0)
     g[2].piece(12)
+    g[2].piece(2)
+    g[1].piece(6)
     vecs.to_core(1)
-    g[2].piece(2)
-    g[4].piece(12)
-    g[1].piece(6)
+    g[2].piece(5)
     vectors_in()
-    g[2].piece(5)
     layer.unpack(v)
     layer.start()
     layer.rows_turned[...] = layer.rows[...].T
     layer.clear_sums()
     g[2].piece(3)
+    g[1].piece(15)
     g[1].piece(13)
     g[2].piece(6)
-    g[1].piece(15)
-    g[0].piece(7)
     g[0].piece(5)
     g[1].piece(14)
     g[1].to_core(1)
+    g[0].piece(7)
     g[0].piece(6)
     g[2].piece(7)
+    g[3].piece(1)
     g[2].piece(9)
-    g[3].piece(1)
     g[0].piece(11)
     g[2].to_core(0)
-    g[2].piece(10)
     g[0].piece(13)
     g[0].to_core(0)
-    g[1].to_core(0)
+    g[0].piece(15)
+    g[2].piece(10)
     g[3].piece(3)
     g[0].piece(14)
     g[2].piece(11)
-    g[0].piece(15)
     g[2].piece(15)
+    g[1].to_core(0)
     g[3].piece(2)
+    g[5].piece(3)
     g[0].to_core(1)
-    g[5].piece(3)
     def project(i):
         layer.project(near(i))
         ticks(i, {
-            1: [(g[2].piece, 14), (g[2].piece, 13), (gathered, 0), (g[3].piece, 9), (g[5].piece, 1)],
+            1: [(g[2].piece, 14), (gathered, 0), (g[2].piece, 13), (g[5].piece, 1), (g[3].piece, 9)],
             2: [(g[3].piece, 5), (g[3].piece, 11)],
         })
 
     each(4, project)
     g[5].piece(2)
     g[3].piece(10)
-    g[3].piece(7)
     def attend(i):
         layer.attend(i)
         ticks(i, {
-            0: [(g[3].piece, 13), (g[4].piece, 1), (g[3].piece, 6), (g[3].to_core, 0), (g[5].piece, 7), (g[4].piece, 2)],
-            1: [(g[5].piece, 6), (g[2].to_core, 1), (g[5].piece, 5), (g[6].piece, 6), (g[4].piece, 3), (start_all, back_in), (g[6].piece, 4), (g[5].piece, 9), (g[5].to_core, 0)],
-            2: [(g[5].piece, 11)],
+            0: [(g[3].piece, 7), (g[3].piece, 6), (g[3].to_core, 0), (g[5].piece, 7), (g[4].piece, 2)],
+            1: [(g[4].piece, 1), (g[5].piece, 6), (g[2].to_core, 1), (g[5].piece, 5), (g[3].piece, 13), (g[6].piece, 6), (g[4].piece, 3), (g[5].to_core, 0), (g[5].piece, 9), (start_all, back_in)],
         })
 
     each(4, attend)
+    g[6].piece(4)
     g[6].piece(10)
+    g[5].piece(11)
     g[3].piece(15)
     g[4].piece(10)
     layer.norm_first()
@@ -1237,25 +1237,25 @@
     def feed_inner(i):
         layer.feed_inner(near(i))
         ticks(i, {
-            0: [(g[5].piece, 14), (g[5].piece, 15), (g[5].to_core, 1), (g[4].piece, 9)],
+            0: [(g[5].piece, 15), (g[5].piece, 14), (g[5].to_core, 1), (g[4].piece, 9)],
             1: [(g[4].piece, 7), (gathered, 1)],
             2: [(g[4].to_core, 0), (g[4].piece, 11), (g[6].piece, 7)],
         })
 
     each(4, feed_inner)
-    g[6].piece(9)
     g[6].piece(12)
     g[6].piece(13)
     g[6].to_core(1)
+    g[6].piece(9)
     g[6].piece(15)
     g[6].to_core(3)
+    g[4].piece(13)
     g[6].piece(14)
-    g[4].piece(15)
     g[6].piece(11)
     g[6].piece(8)
     g[6].to_core(2)
-    g[4].piece(13)
     g[4].piece(14)
+    g[4].piece(15)
     g[4].to_core(1)
     def feed_outer(i):
         layer.feed_outer(near(i))
@@ -1289,11 +1289,10 @@
         ticks(i, {
             0: [(cores[1].to_core, 0), (cores[2].half, 1, 1), (r[6].start, 1, 1), (r[5].start, 1, 1), (r[4].start, 1, 1), (r[6].add, 2), (r[6].add, 0)],
             1: [(cores[1].half, 0, 0), (r[2].start, 0, 0), (r[3].start, 0, 0)],
-            2: [(cores[1].to_core, 1), (r[6].add, 1), (r[5].add, 4), (cores[1].half, 0, 1), (r[2].start, 0, 1), (r[3].start, 0, 1), (r[2].add, 0), (r[5].add, 1), (r[6].add, 6)],
+            2: [(cores[1].to_core, 1), (r[6].add, 1), (r[5].add, 4), (cores[1].half, 0, 1), (r[2].start, 0, 1), (r[3].start, 0, 1), (r[2].add, 0), (r[5].add, 1), (r[6].add, 6), (r[5].add, 0)],
         })
 
     each(4, inner_back)
-    r[5].add(0)
     r[6].add(3)
     r[5].add(5)
     r[5].add(3)
@@ -1308,9 +1307,9 @@
     cores[1].half(1, 1)
     r[2].start(1, 1)
     r[3].start(1, 1)
+    passed_on(0)
     layer.norm_first_back()
     r[2].add(1)
-    passed_on(0)
     r[5].add(7)
     r[5].add(8)
     r[4].add(0)
@@ -1318,13 +1317,14 @@
     def attend_back(i):
         layer.attend_back(order(i))
         ticks(i, {
-            2: [(r[4].add, 1), (r[4].add, 2), (r[6].add, 8), (r[2].add, 3), (r[2].add, 6), (r[3].add, 2), (cores[0].half, 0, 1), (r[1].start, 0, 1), (r[0].start, 0, 1), (r[5].add, 10), (r[4].add, 4)],
+            1: [(r[2].add, 7), (r[3].add, 4)],
+            2: [(r[4].add, 1), (r[4].add, 2), (r[2].add, 3), (r[6].add, 8), (r[2].add, 6), (r[4].add, 4), (r[3].add, 2), (cores[0].half, 0, 1), (r[1].start, 0, 1), (r[0].start, 0, 1)],
             3: [(cores[0].to_core, 1), (r[3].add, 6), (r[3].add, 3), (r[3].add, 7), (r[3].add, 9), (r[1].add, 1), (r[5].add, 11), (r[0].add, 0)],
         })
         layer.joint_back(order(i))
         ticks(i, {
-            0: [(r[3].add, 0), (r[2].add, 4), (cores[0].to_core, 0), (r[3].add, 1), (r[2].add, 5), (r[2].add, 2), (r[5].add, 6)],
-            1: [(cores[0].half, 0, 0), (r[1].start, 0, 0), (r[0].start, 0, 0), (r[2].add, 7), (r[6].add, 7), (r[3].add, 4), (r[3].add, 5)],
+            0: [(r[2].add, 4), (r[3].add, 0), (r[3].add, 1), (cores[0].to_core, 0), (r[2].add, 5), (r[5].add, 6)],
+            1: [(r[2].add, 2), (cores[0].half, 0, 0), (r[1].start, 0, 0), (r[0].start, 0, 0), (r[6].add, 7), (r[5].add, 10), (r[3].add, 5)],
             2: [(r[4].add, 3), (r[3].add, 8)],
         })
 
@@ -1332,31 +1332,31 @@
     cores[0].half(1, 0)
     r[1].start(1, 0)
     r[0].start(1, 0)
+    r[1].add(3)
     r[2].add(10)
     r[1].add(0)
-    r[1].add(3)
     layer.pack(parts)
     r[2].add(9)
+    r[1].add(2)
     r[6].add(9)
-    r[1].add(2)
-    sums.first()
     r[0].add(1)
     r[2].add(8)
+    sums.first()
     layer.finish()
     r[0].add(2)
     r[4].add(5)
+    r[6].add(10)
     r[4].add(6)
-    r[6].add(10)
     r[2].add(11)
     sums.core_done()
     start_all(back_out)
     local[7].start()
     r[5].add(12)
     local[10].start()
+    r[0].add(3)
     cores[0].half(1, 1)
     r[1].start(1, 1)
     r[0].start(1, 1)
-    r[0].add(3)
     reduced(2)
     r[3].add(10)
     r[3].add(11)

time: 148 us -> 148 us (level)
  no operation moved by 1% of the time
where the time goes in v6:
time: 148 us; the launch traced here: 147 us
  Pallas kernels  147 us (99%)
    pallas_call x1, Pallas kernels, whole_layer(): pl.pallas_call(partial(layer_kernel, nz), out_shape=(jax.ShapeDtypeStruct...  144 us
    pallas_call x1, Pallas kernels, finish_layer(): pl.pallas_call(partial(finish_kernel, len(shapes)), out_shape=[jax.ShapeD...  2.97 us

profile of v6, /device:TPU:0, one launch (start us, length us, event | category | flops | bytes accessed | tf_op | source)
XLA Modules:
  0.0 147.5 jit_solution(4865268687881597811)
XLA Ops:
  0.7 143.6 %whole_layer.1 = (f32[3,96,768]{2,1,0:T(8,128)}, bf16[4,128,768]{2,1,0:T(8,128)(2,1)}, bf16[4,128,768]{2,1,0:T(8,128)(2,1)}, f32[8,128]{1,0:T(8,128)}) custom-call(bf16[4,128,768]{2,1,0:T(8,128)(2,1)} %refs_0_.1, s32[4]{0:T(128)} %refs_1_.1, bf16[4,128,768]{2,1,0:T(8,128)(2,1)} %refs_2_.1, bf16[96,192]{1,0:T(8,128)(2,1)} %refs_3_.1, ...), custom_call_target="tpu_custom_call" | custom-call | tf_op jit(solution)/shard_map/whole_layer/pallas_call | solution.py:1406
  144.3 3.0 %finish_layer.1 = (bf16[4,128,768]{2,1,0:T(8,128)(2,1)}, f32[4,128,768]{2,1,0:T(8,128)}, f32[96,192]{1,0:T(8,128)}, f32[96,192]{1,0:T(8,128)}, f32[96,192]{1,0:T...) custom-call(f32[3,96,768]{2,1,0:T(8,128)} %get-tuple-element.38.refs, ...), custom_call_target="tpu_custom_call" | custom-call | tf_op jit(solution)/shard_map/finish_layer/pallas_call | solution.py:1487

commit v7 on v5

--- a/solution.py
+++ b/solution.py
@@ -1106,22 +1106,21 @@
     vecs.first()
     g[1].first()
     g[0].first()
+    start_all(token_in)
+    g[1].piece(4)
+    vecs.piece(2)
     g[2].first()
-    g[1].piece(4)
-    start_all(token_in)
-    vecs.piece(2)
+    g[1].piece(8)
+    g[0].piece(8)
     start_all(local[:6])
     wait_local(local[:6])
-    g[1].piece(8)
     g[3].first()
     g[5].first()
+    vecs.piece(1)
     g[4].first()
-    g[0].piece(8)
-    vecs.piece(1)
+    vecs.piece(3)
     g[1].piece(2)
     g[6].first()
-    vecs.piece(3)
-    vecs.piece(8)
     g[3].piece(4)
     g[1].piece(1)
     g[1].piece(3)
@@ -1129,38 +1128,39 @@
     vecs.piece(11)
     vecs.piece(4)
     g[0].piece(4)
-    g[2].piece(4)
     g[4].piece(8)
     g[1].piece(12)
     vecs.piece(12)
+    vecs.piece(8)
+    g[6].piece(2)
+    vecs.piece(6)
     g[2].piece(8)
-    g[6].piece(2)
+    g[2].piece(4)
+    g[1].piece(11)
     vecs.piece(9)
-    g[1].piece(11)
-    vecs.piece(6)
     g[0].piece(1)
-    g[0].piece(12)
     g[5].piece(4)
     g[0].piece(2)
     g[6].piece(1)
     vecs.piece(5)
+    g[0].piece(12)
     vecs.piece(7)
     g[5].piece(12)
     g[4].piece(4)
+    g[6].piece(3)
     g[1].piece(9)
+    swapped(token_in)
+    g[0].piece(10)
     g[3].piece(12)
     vecs.piece(10)
-    g[6].piece(3)
-    swapped(token_in)
     vecs.piece(14)
+    g[0].piece(9)
+    g[1].piece(5)
     g[2].piece(1)
-    g[1].piece(5)
     g[1].piece(7)
     g[1].piece(10)
-    g[0].piece(9)
-    g[0].piece(10)
+    vecs.piece(13)
     vecs.piece(15)
-    vecs.piece(13)
     vecs.to_core(0)
     g[0].piece(3)
     g[3].piece(8)
@@ -1169,69 +1169,71 @@
     vecs.to_core(1)
     g[2].piece(2)
     g[4].piece(12)
+    g[2].piece(5)
     g[1].piece(6)
     vectors_in()
-    g[2].piece(5)
     layer.unpack(v)
     layer.start()
     layer.rows_turned[...] = layer.rows[...].T
     layer.clear_sums()
+    g[1].piece(13)
     g[2].piece(3)
-    g[1].piece(13)
     g[2].piece(6)
     g[1].piece(15)
+    g[0].piece(5)
     g[0].piece(7)
-    g[0].piece(5)
+    g[2].piece(10)
     g[1].piece(14)
     g[1].to_core(1)
     g[0].piece(6)
+    g[3].piece(1)
+    g[2].piece(9)
+    g[0].piece(11)
     g[2].piece(7)
-    g[2].piece(9)
-    g[3].piece(1)
-    g[0].piece(11)
     g[2].to_core(0)
-    g[2].piece(10)
+    g[1].to_core(0)
+    g[0].to_core(0)
+    g[3].piece(3)
+    g[2].piece(11)
+    g[0].piece(14)
+    g[0].piece(15)
+    g[3].piece(2)
+    g[2].piece(15)
     g[0].piece(13)
-    g[0].to_core(0)
-    g[1].to_core(0)
-    g[3].piece(3)
-    g[0].piece(14)
-    g[2].piece(11)
-    g[0].piece(15)
-    g[2].piece(15)
-    g[3].piece(2)
+    g[5].piece(3)
     g[0].to_core(1)
-    g[5].piece(3)
     def project(i):
         layer.project(near(i))
         ticks(i, {
-            1: [(g[2].piece, 14), (g[2].piece, 13), (gathered, 0), (g[3].piece, 9), (g[5].piece, 1)],
-            2: [(g[3].piece, 5), (g[3].piece, 11)],
+            1: [(g[2].piece, 13), (g[2].piece, 14), (gathered, 0), (g[3].piece, 9), (g[5].piece, 1)],
+            2: [(g[3].piece, 5)],
         })
 
     each(4, project)
+    g[3].piece(11)
+    g[3].piece(10)
     g[5].piece(2)
-    g[3].piece(10)
     g[3].piece(7)
     def attend(i):
         layer.attend(i)
         ticks(i, {
-            0: [(g[3].piece, 13), (g[4].piece, 1), (g[3].piece, 6), (g[3].to_core, 0), (g[5].piece, 7), (g[4].piece, 2)],
-            1: [(g[5].piece, 6), (g[2].to_core, 1), (g[5].piece, 5), (g[6].piece, 6), (g[4].piece, 3), (start_all, back_in), (g[6].piece, 4), (g[5].piece, 9), (g[5].to_core, 0)],
+            0: [(g[3].piece, 13), (g[4].piece, 1), (g[3].piece, 6), (g[5].piece, 7), (g[3].to_core, 0), (g[4].piece, 2)],
+            1: [(g[5].piece, 5), (g[2].to_core, 1), (g[6].piece, 6), (g[6].piece, 4), (g[4].piece, 3), (g[5].piece, 9), (g[5].piece, 6), (g[5].to_core, 0)],
             2: [(g[5].piece, 11)],
         })
 
     each(4, attend)
     g[6].piece(10)
     g[3].piece(15)
+    start_all(back_in)
     g[4].piece(10)
     layer.norm_first()
     layer.first_turned[...] = layer.first_low[...].T
     g[6].piece(5)
+    g[4].piece(5)
     g[4].piece(6)
     g[3].piece(14)
     g[5].piece(13)
-    g[4].piece(5)
     g[5].piece(10)
     g[3].to_core(1)
     def feed_inner(i):
@@ -1244,15 +1246,15 @@
 
     each(4, feed_inner)
     g[6].piece(9)
+    g[6].piece(13)
     g[6].piece(12)
-    g[6].piece(13)
     g[6].to_core(1)
     g[6].piece(15)
     g[6].to_core(3)
-    g[6].piece(14)
     g[4].piece(15)
     g[6].piece(11)
     g[6].piece(8)
+    g[6].piece(14)
     g[6].to_core(2)
     g[4].piece(13)
     g[4].piece(14)
@@ -1260,7 +1262,7 @@
     def feed_outer(i):
         layer.feed_outer(near(i))
         ticks(i, {
-            1: [(gathered, 2)],
+            1: [(gathered, 2), (passed_on, 2)],
         })
 
     each(4, feed_outer)
@@ -1269,13 +1271,12 @@
     start_all(out_out)
     local[6].start()
     layer.outer_early(order(0))
-    passed_on(2)
     cores[2].to_core(0)
     def outer_back(i):
         layer.outer_back(order(i + 1))
         ticks(i, {
             0: [(cores[2].half, 0, 0), (r[6].start, 0, 0), (r[5].start, 0, 0), (r[4].start, 0, 0)],
-            1: [(passed_on, 1), (cores[2].to_core, 1), (cores[2].half, 0, 1), (r[6].start, 0, 1), (r[5].start, 0, 1), (r[4].start, 0, 1)],
+            1: [(cores[2].to_core, 1), (passed_on, 1), (cores[2].half, 0, 1), (r[6].start, 0, 1), (r[5].start, 0, 1), (r[4].start, 0, 1)],
         })
 
     each(3, outer_back)
@@ -1289,15 +1290,13 @@
         ticks(i, {
             0: [(cores[1].to_core, 0), (cores[2].half, 1, 1), (r[6].start, 1, 1), (r[5].start, 1, 1), (r[4].start, 1, 1), (r[6].add, 2), (r[6].add, 0)],
             1: [(cores[1].half, 0, 0), (r[2].start, 0, 0), (r[3].start, 0, 0)],
-            2: [(cores[1].to_core, 1), (r[6].add, 1), (r[5].add, 4), (cores[1].half, 0, 1), (r[2].start, 0, 1), (r[3].start, 0, 1), (r[2].add, 0), (r[5].add, 1), (r[6].add, 6)],
+            2: [(cores[1].to_core, 1), (r[5].add, 4), (r[6].add, 1), (cores[1].half, 0, 1), (r[2].start, 0, 1), (r[3].start, 0, 1), (r[2].add, 0), (r[5].add, 1), (r[6].add, 6), (r[5].add, 0)],
         })
 
     each(4, inner_back)
-    r[5].add(0)
     r[6].add(3)
     r[5].add(5)
     r[5].add(3)
-    vectors_sent()
     r[6].add(4)
     r[6].add(5)
     layer.second_sums()
@@ -1305,27 +1304,30 @@
     cores[1].half(1, 0)
     r[2].start(1, 0)
     r[3].start(1, 0)
+    layer.norm_first_back()
     cores[1].half(1, 1)
     r[2].start(1, 1)
     r[3].start(1, 1)
-    layer.norm_first_back()
     r[2].add(1)
+    r[5].add(7)
     passed_on(0)
-    r[5].add(7)
     r[5].add(8)
     r[4].add(0)
     r[5].add(9)
+    vectors_sent()
     def attend_back(i):
         layer.attend_back(order(i))
         ticks(i, {
-            2: [(r[4].add, 1), (r[4].add, 2), (r[6].add, 8), (r[2].add, 3), (r[2].add, 6), (r[3].add, 2), (cores[0].half, 0, 1), (r[1].start, 0, 1), (r[0].start, 0, 1), (r[5].add, 10), (r[4].add, 4)],
-            3: [(cores[0].to_core, 1), (r[3].add, 6), (r[3].add, 3), (r[3].add, 7), (r[3].add, 9), (r[1].add, 1), (r[5].add, 11), (r[0].add, 0)],
+            0: [(r[3].add, 0)],
+            1: [(r[5].add, 10)],
+            2: [(r[2].add, 7), (r[4].add, 2), (r[2].add, 3), (r[4].add, 1), (r[4].add, 3), (r[2].add, 6), (r[6].add, 8), (r[3].add, 2), (cores[0].half, 0, 1), (r[1].start, 0, 1), (r[0].start, 0, 1), (r[4].add, 4)],
+            3: [(cores[0].to_core, 1), (r[3].add, 3), (r[3].add, 7), (r[3].add, 9), (r[1].add, 1), (r[5].add, 11), (r[1].add, 0), (r[0].add, 0)],
         })
         layer.joint_back(order(i))
         ticks(i, {
-            0: [(r[3].add, 0), (r[2].add, 4), (cores[0].to_core, 0), (r[3].add, 1), (r[2].add, 5), (r[2].add, 2), (r[5].add, 6)],
-            1: [(cores[0].half, 0, 0), (r[1].start, 0, 0), (r[0].start, 0, 0), (r[2].add, 7), (r[6].add, 7), (r[3].add, 4), (r[3].add, 5)],
-            2: [(r[4].add, 3), (r[3].add, 8)],
+            0: [(cores[0].to_core, 0), (r[2].add, 4), (r[3].add, 1), (r[2].add, 5), (r[6].add, 7), (r[5].add, 6), (r[2].add, 2)],
+            1: [(cores[0].half, 0, 0), (r[1].start, 0, 0), (r[0].start, 0, 0), (r[3].add, 4), (r[3].add, 5)],
+            2: [(r[3].add, 8), (r[3].add, 6)],
         })
 
     each(4, attend_back)
@@ -1333,30 +1335,29 @@
     r[1].start(1, 0)
     r[0].start(1, 0)
     r[2].add(10)
-    r[1].add(0)
     r[1].add(3)
     layer.pack(parts)
+    sums.first()
     r[2].add(9)
     r[6].add(9)
     r[1].add(2)
-    sums.first()
     r[0].add(1)
     r[2].add(8)
     layer.finish()
     r[0].add(2)
     r[4].add(5)
     r[4].add(6)
-    r[6].add(10)
     r[2].add(11)
     sums.core_done()
     start_all(back_out)
     local[7].start()
     r[5].add(12)
-    local[10].start()
+    r[6].add(10)
     cores[0].half(1, 1)
     r[1].start(1, 1)
     r[0].start(1, 1)
     r[0].add(3)
+    local[10].start()
     reduced(2)
     r[3].add(10)
     r[3].add(11)

time: 148 us -> 148 us (level)
  no operation moved by 1% of the time
where the time goes in v7:
time: 148 us
  Pallas kernels  147 us (99%)
    pallas_call x1, Pallas kernels, whole_layer(): pl.pallas_call(partial(layer_kernel, nz), out_shape=(jax.ShapeDtypeStruct...  144 us
    pallas_call x1, Pallas kernels, finish_layer(): pl.pallas_call(partial(finish_kernel, len(shapes)), out_shape=[jax.ShapeD...  2.97 us

profile of v7, /device:TPU:0, one launch (start us, length us, event | category | flops | bytes accessed | tf_op | source)
XLA Modules:
  0.0 148.3 jit_solution(2586116343541481780)
XLA Ops:
  0.7 144.5 %whole_layer.1 = (f32[3,96,768]{2,1,0:T(8,128)}, bf16[4,128,768]{2,1,0:T(8,128)(2,1)}, bf16[4,128,768]{2,1,0:T(8,128)(2,1)}, f32[8,128]{1,0:T(8,128)}) custom-call(bf16[4,128,768]{2,1,0:T(8,128)(2,1)} %refs_0_.1, s32[4]{0:T(128)} %refs_1_.1, bf16[4,128,768]{2,1,0:T(8,128)(2,1)} %refs_2_.1, bf16[96,192]{1,0:T(8,128)(2,1)} %refs_3_.1, ...), custom_call_target="tpu_custom_call" | custom-call | tf_op jit(solution)/shard_map/whole_layer/pallas_call | solution.py:1407
  145.1 3.0 %finish_layer.1 = (bf16[4,128,768]{2,1,0:T(8,128)(2,1)}, f32[4,128,768]{2,1,0:T(8,128)}, f32[96,192]{1,0:T(8,128)}, f32[96,192]{1,0:T(8,128)}, f32[96,192]{1,0:T...) custom-call(f32[3,96,768]{2,1,0:T(8,128)} %get-tuple-element.38.refs, ...), custom_call_target="tpu_custom_call" | custom-call | tf_op jit(solution)/shard_map/finish_layer/pallas_call | solution.py:1488
